TPU v7x, 32 devices: a whole 2x2x4 slice. The times are simulated.
32 devices in a mesh: rep: 4 (over y, core), ep: 4 (over z), tp: 2 (over x).
Axes of the slice: x: 2, y: 2, z: 4, core: 2. Of those that a mesh axis runs over, the one named last changes fastest.
Arguments:
- tokens: bfloat16 [128, 6144], P(('rep', 'ep'), 'tp'), may hold values from -6 to 6
- expert_ids: int32 [128, 2], P(('rep', 'ep')), may hold values from 0 to 3, as said below
- replicas: int32 [128, 2], P(('rep', 'ep')), may hold values from 0 to 3, as said below
- scores: float32 [128, 2], P(('rep', 'ep')), may hold values from -8 to 8
- w_gate: bfloat16 [4, 6144, 1024], P('ep', None, 'tp'), may hold values from -0.078125 to 0.078125
- w_up: bfloat16 [4, 6144, 1024], P('ep', None, 'tp'), may hold values from -0.078125 to 0.078125
- w_down: bfloat16 [4, 1024, 6144], P('ep', 'tp'), may hold values from -0.1875 to 0.1875
Outputs:
- moe_out: bfloat16 [128, 6144], P(('rep', 'ep'), 'tp')
- load_counts: int32 [4, 4], replicated
Inputs may be any that keep to these rules, and one draw needn't show every extreme that they name: `expert_ids`: each row names 2 different experts. In the rows of one device one expert is named by every row. `replicas`: in the rows of one device at most 2 pairs name the same expert with the same replica pick, and some expert and pick reach 2.
All inputs are finite; a program needn't handle non-finite values.
Results may differ from a plain program's by a relative error of at most 0.008.
Values may be sent and summed in bfloat16 or wider, within the bound.
No kernel may reach another device: no remote copies, remote signals or barrier semaphores. Data moves between devices by JAX's collectives and lax.ppermute only.
A program may use at most 64 MiB of HBM per device.

v0:
```python
import jax
import jax.numpy as jnp
from jax import lax
from jax.sharding import PartitionSpec as P

REPL = 4


route_scale = 2.5


def expert_hop(slot_block):
    return lax.all_to_all(slot_block, "ep", split_axis=1, concat_axis=1, tiled=True)


def per_device(tokens, expert_ids, replicas, scores, w_gate, w_up, w_down):
    rep_count = lax.axis_size("rep")
    ep_count = lax.axis_size("ep")
    stride = rep_count // REPL
    tok_rows = expert_ids.shape[0]
    chosen_count = expert_ids.shape[1]
    key_ids = expert_ids.reshape(-1)
    lead_count = 1
    slot_total = ep_count * tok_rows
    onehot = (key_ids[:, None] == jnp.arange(ep_count, dtype=jnp.int32)[None, :]).astype(jnp.int32)
    before = jnp.cumsum(onehot, 0) - onehot
    order_rank = jnp.sum(before * onehot, 1)
    slot_ids = (key_ids * tok_rows + order_rank).reshape(tok_rows, chosen_count)
    matches = slot_ids[:, :, None] == jnp.arange(slot_total, dtype=jnp.int32)[None, None, :]
    select = jnp.sum(matches.astype(jnp.float32), 1).T.astype(jnp.bfloat16)
    sigmoid_scores = jax.nn.sigmoid(scores)
    weights = sigmoid_scores / jnp.sum(sigmoid_scores, 1, keepdims=True) * route_scale
    combine = jnp.sum(jnp.where(matches, weights[:, :, None], 0.0), 1)
    source = lax.all_gather(tokens, "tp", axis=1, tiled=True)
    feature_count = source.shape[1]
    packed = jnp.dot(select, source, preferred_element_type=jnp.float32).astype(jnp.bfloat16)
    packed = packed.reshape(lead_count, ep_count, tok_rows, feature_count)
    arrived = expert_hop(packed)
    slot_rows = arrived.reshape(slot_total, feature_count)
    gate_local = w_gate[0]
    up_local = w_up[0]
    down_local = w_down[0]
    gate_pre = jnp.dot(slot_rows, gate_local, preferred_element_type=jnp.float32)
    up_pre = jnp.dot(slot_rows, up_local, preferred_element_type=jnp.float32)
    hidden = (jax.nn.silu(gate_pre) * up_pre).astype(jnp.bfloat16)
    summed = lax.psum_scatter(
        lax.dot_general(
            down_local, hidden, (((0,), (1,)), ((), ())), preferred_element_type=jnp.float32
        ),
        "tp",
        scatter_dimension=0,
        tiled=True,
    )
    outputs = summed.T.astype(jnp.bfloat16).reshape(lead_count, ep_count, tok_rows, summed.shape[0])
    coming_back = expert_hop(outputs)
    flat_rows = coming_back.reshape(slot_total, summed.shape[0]).astype(jnp.float32)
    moe_out = jnp.dot(combine, flat_rows, precision=lax.Precision.HIGHEST).astype(jnp.bfloat16)
    rep_here = lax.axis_index("rep")
    target = (rep_here + replicas * stride) % rep_count
    group_hit = (
        target.reshape(-1)[:, None, None] == jnp.arange(rep_count, dtype=jnp.int32)[None, :, None]
    )
    expert_hit = (
        expert_ids.reshape(-1)[:, None, None]
        == jnp.arange(ep_count, dtype=jnp.int32)[None, None, :]
    )
    local_counts = jnp.sum((group_hit & expert_hit).astype(jnp.int32), 0)
    load_counts = lax.psum(local_counts, ("rep", "ep"))
    return (moe_out, load_counts)


def solution(mesh):
    placed = (
        P(("rep", "ep"), "tp"),
        P(("rep", "ep"), None),
        P(("rep", "ep"), None),
        P(("rep", "ep"), None),
        P("ep", None, "tp"),
        P("ep", None, "tp"),
        P("ep", "tp", None),
    )
    return jax.shard_map(
        per_device,
        mesh=mesh,
        in_specs=placed,
        out_specs=(P(("rep", "ep"), "tp"), P()),
        check_vma=False,
    )
```

profile of v0, /device:TPU:0, one launch (start us, length us, event | category | flops | bytes accessed | tf_op | source)
XLA Modules:
  0.0 87.5 jit_solution(3239276921868879169)
XLA Ops:
  7.2 0.0 reduce-scatter.2.cloned.1.call-start
  7.2 0.7 divide_reduce_fusion
  7.9 0.7 divide_multiply_fusion
  8.6 0.8 copy.23
  9.4 0.1 eq.62
  9.4 0.1 iota_compare_fusion.1
  9.6 0.2 select_reduce_fusion.1
  9.7 0.1 reduce_sum.48
  9.8 0.1 copy.25
  9.9 6.0 %all_gather.3 = bf16[8,6144]{1,0:T(8,128)(2,1)S(1)} all-gather(bf16[8,3072]{1,0:T(8,128)(2,1)} %param.7), channel_id=1, replica_groups=mesh['rep'=4,'ep'=4,'tp'=2] {'tp'}, dimensions={1}, use_global_device_ids=true | all-gather | bytes 147456 | tf_op jit(solution)/shard_map/all_gather | solution.py:34
  15.9 0.1 convert_reduce_fusion.1
  16.0 0.3 fusion
  16.3 15.7 %all_to_all.10 = bf16[1,4,8,6144]{3,2,0,1:T(8,128)(2,1)S(1)} all-to-all(bf16[1,4,8,6144]{3,2,0,1:T(8,128)(2,1)S(1)} %fusion), channel_id=1, replica_groups=mesh['rep'=4,'ep'=4,'tp'=2] {'ep'}, dimensions={1} | all-to-all | bytes 786432 | tf_op jit(solution)/shard_map/all_to_all | solution.py:13
  31.9 3.9 %fusion.4 = f32[32,512]{1,0:T(8,128)S(1)} fusion(bf16[1,6144,512]{2,1,0:T(8,128)(2,1)} %param.11, bf16[1,4,8,6144]{3,2,0,1:T(8,128)(2,1)S(1)} %all_to_all.10), kind=kOutput, calls=%fused_computation.6 | convolution fusion | flops 201326592 | bytes 6750208 | tf_op jit(solution)/shard_map/dot_general | solution.py:43
  35.9 0.0 copy-start
  35.9 7.9 %convolution_bitcast_fusion = f32[6144,32]{0,1:T(8,128)} fusion(bf16[1,512,6144]{2,1,0:T(8,128)(2,1)} %param.13, bf16[1,6144,512]{2,1,0:T(8,128)(2,1)} %param.12, bf16[1,4,8,6144]{3,2,0,1:T(8,128)(2,1)S(1)} %all_to_all.10, f32[32,512]{1,0:T(8,128)S(1)} %fusion.4), kind=kOutput, calls=%fused_computation | convolution fusion | flops 402751488 | bytes 13828096 | tf_op jit(solution)/shard_map/dot_general | solution.py:47
  43.7 0.0 reduce-scatter.2.cloned.1.call-update
  43.8 0.0 copy-done
  43.8 0.1 copy.28
  43.9 0.1 eq.69
  44.0 0.1 copy.29
  44.1 16.5 %reduce-scatter.2.cloned.1.call-done = f32[3072,32]{0,1:T(8,128)} async-done(((f32[6144,32]{0,1:T(8,128)}), f32[3072,32]{0,1:T(8,128)}) %reduce-scatter.2.cloned.1.call-update) | async-done | bytes 393232 | tf_op jit(solution)/shard_map/reduce_scatter | solution.py:46
  60.5 1.7 %convert_bitcast_fusion = bf16[1,4,8,3072]{3,2,0,1:T(8,128)(2,1)} fusion(f32[3072,32]{0,1:T(8,128)} %reduce-scatter.2.cloned.1.call-done), kind=kLoop, calls=%fused_computation.14 | loop fusion | flops 98304 | bytes 589824 | tf_op jit(solution)/shard_map/reshape | solution.py:54
  62.2 4.6 %all-to-all-start.1 = ((bf16[1,4,8,3072]{3,2,0,1:T(8,128)(2,1)}), bf16[1,4,8,3072]{3,2,0,1:T(8,128)(2,1)S(1)}, u32[]{:S(2)}, u32[]{:S(2)}) async-start(bf16[1,4,8,3072]{3,2,0,1:T(8,128)(2,1)} %convert_bitcast_fusion), calls=%async_computation.2 | async-start | bytes 393216 | tf_op jit(solution)/shard_map/all_to_all | solution.py:13
  66.8 0.2 convert_reduce_fusion
  67.0 12.9 %psum.7 = s32[4,4]{1,0:T(4,128)} all-reduce(s32[4,4]{1,0:T(4,128)S(1)} %convert_reduce_fusion), channel_id=1, replica_groups=mesh['rep'=4,'ep'=4,'tp'=2] {'rep','ep'}, use_global_device_ids=true, to_apply=%region_7.8 | all-reduce | flops 16 | bytes 128 | tf_op jit(solution)/shard_map/psum | solution.py:68
  79.9 0.0 all-to-all-done.1
  79.9 0.8 convolution_convert_fusion.1
  (4 shorter events, 0.1 us)
Async XLA Ops:
  7.2 53.4 %reduce-scatter.2.cloned.1.call-start = ((), (), s32[]{:S(2)}) async-start(), calls=%async_computation.3 | async-start | bytes 1179648 | tf_op jit(solution)/shard_map/reduce_scatter | solution.py:46
  35.9 7.9 %copy-start = (s32[8,2]{0,1:T(2,128)S(1)}, s32[8,2]{0,1:T(2,128)}, u32[]{:S(2)}) copy-start(s32[8,2]{0,1:T(2,128)} %param.9) | copy-start | bytes 196
  62.2 17.6 %all-to-all-start.1 = ((bf16[1,4,8,3072]{3,2,0,1:T(8,128)(2,1)}), bf16[1,4,8,3072]{3,2,0,1:T(8,128)(2,1)S(1)}, u32[]{:S(2)}, u32[]{:S(2)}) async-start(bf16[1,4,8,3072]{3,2,0,1:T(8,128)(2,1)} %convert_bitcast_fusion), calls=%async_computation.2 | async-start | bytes 393216 | tf_op jit(solution)/shard_map/all_to_all | solution.py:13
Sparse Core Ops, SparseCore 0:
  43.9 16.6 reduce-scatter.1
where the time goes:
time: 87.9 us; the launch traced here: 87.5 us
  blocking collectives  34.5 us (39%)
  waiting for transfers between devices  16.5 us (19%)
  between operations  14.1 us (16%)
  matrix products  12.9 us (15%)
  starting transfers between devices  4.64 us (5%)
  other arithmetic  3.63 us (4%)
  local copies, waits for them, and re-layouts  1.27 us (1%)
    reduce_scatter x1, waiting for transfers between devices, per_device(): lax.psum_scatter(lax.dot_general(down_local, hidden, (((0,), (1,)), ((),...  16.5 us
    all_to_all x1, blocking collectives, expert_hop(): lax.all_to_all(slot_block, 'ep', split_axis=1, concat_axis=1, tiled=True)  15.7 us
    psum x1, blocking collectives, per_device(): load_counts = lax.psum(local_counts, ('rep', 'ep'))  12.9 us
    dot_general x1, matrix products, per_device(): lax.dot_general(down_local, hidden, (((0,), (1,)), ((), ())), preferred_e...  7.85 us
    all_gather x1, blocking collectives, per_device(): source = lax.all_gather(tokens, 'tp', axis=1, tiled=True)  5.97 us
    all_to_all x1, starting transfers between devices, expert_hop(): lax.all_to_all(slot_block, 'ep', split_axis=1, concat_axis=1, tiled=True)  4.61 us
    dot_general x1, matrix products, per_device(): jnp.dot(slot_rows, gate_local, preferred_element_type=jnp.float32)  3.94 us
  transfers between devices with their start and end apart: 2, of which 1 were waited for; matrix products, arithmetic and copies ran while one was open for 0% of the time, Pallas kernels for 0%

commit v1 on v0

v1 whole, which is shorter than its diff:
```python
import functools

import jax
import jax.numpy as jnp
from jax import lax
from jax.experimental import pallas as pl
from jax.experimental.pallas import tpu as pltpu
from jax.sharding import PartitionSpec as P

REPL = 4
LANES = 128
SUBLANES = 8
MIB = 1 << 20

route_scale = 2.5


def shift(array, axis, count, step):
    return lax.ppermute(array, axis, [(i, (i + step) % count) for i in range(count)])


def fetch_kernel(pieces, gate_hbm, up_hbm, down_hbm, gate_vmem, up_vmem, down_vmem, sems):
    copies = []
    for source, target in ((gate_hbm, gate_vmem), (up_hbm, up_vmem), (down_hbm, down_vmem)):
        rows = source.shape[0] // pieces
        for piece in range(pieces):
            window = pl.ds(piece * rows, rows)
            copies.append(
                pltpu.make_async_copy(source.at[window], target.at[window], sems.at[len(copies)])
            )
    for copy in copies:
        copy.start()
    for copy in copies:
        copy.wait()


def fetch_weights(gate, up, down):
    pieces = 4
    size = 2 * (gate.size + up.size + down.size)
    return pl.pallas_call(
        functools.partial(fetch_kernel, pieces),
        out_shape=[pltpu.VMEM(w.shape, w.dtype) for w in (gate, up, down)],
        in_specs=[pl.BlockSpec(memory_space=pltpu.HBM)] * 3,
        out_specs=[pl.BlockSpec(memory_space=pltpu.VMEM)] * 3,
        scratch_shapes=[pltpu.SemaphoreType.DMA((3 * pieces,))],
        compiler_params=pltpu.CompilerParams(vmem_limit_bytes=32 * MIB),
        cost_estimate=pl.CostEstimate(flops=10**8, bytes_accessed=size, transcendentals=0),
        name="fetch_weights",
    )(gate, up, down)


def own_kernel(x_ref, gate_ref, up_ref, gate_out, up_out):
    part = x_ref.shape[1]
    base = pl.multiple_of(lax.axis_index("tp") * part, part)
    rows = pl.ds(base, part)
    x = x_ref[...]
    gate_out[...] = jnp.dot(x, gate_ref[rows, :], preferred_element_type=jnp.float32)
    up_out[...] = jnp.dot(x, up_ref[rows, :], preferred_element_type=jnp.float32)


def hidden_kernel(tp_count, *refs):
    others = refs[: tp_count - 1]
    gate_acc, up_acc, gate_ref, up_ref, down_ref = refs[tp_count - 1 : tp_count + 4]
    hidden_out = refs[tp_count + 4]
    partial_outs = refs[tp_count + 5 :]
    me = lax.axis_index("tp")
    gate = gate_acc[...]
    up = up_acc[...]
    for step, other in enumerate(others, 1):
        part = other.shape[1]
        sender = lax.rem(me - step + tp_count, tp_count)
        rows = pl.ds(pl.multiple_of(sender * part, part), part)
        x = other[...]
        gate += jnp.dot(x, gate_ref[rows, :], preferred_element_type=jnp.float32)
        up += jnp.dot(x, up_ref[rows, :], preferred_element_type=jnp.float32)
    hidden = (gate / (1.0 + jnp.exp(-gate)) * up).astype(jnp.bfloat16)
    hidden_out[...] = hidden
    for step, out in enumerate(partial_outs, 1):
        part = out.shape[1]
        target = lax.rem(me + step, tp_count)
        columns = pl.ds(pl.multiple_of(target * part, part), part)
        out[...] = jnp.dot(
            hidden, down_ref[:, columns], preferred_element_type=jnp.float32
        ).astype(jnp.bfloat16)


def down_kernel(hidden_ref, down_ref, out_ref):
    part = out_ref.shape[1]
    columns = pl.ds(pl.multiple_of(lax.axis_index("tp") * part, part), part)
    out_ref[...] = jnp.dot(
        hidden_ref[...], down_ref[:, columns], preferred_element_type=jnp.float32
    )


def vmem_call(kernel, name, outs, args, flops, grant=24):
    return pl.pallas_call(
        kernel,
        out_shape=outs,
        in_specs=[pl.BlockSpec(memory_space=pltpu.VMEM)] * len(args),
        out_specs=[pl.BlockSpec(memory_space=pltpu.VMEM)] * len(outs),
        compiler_params=pltpu.CompilerParams(vmem_limit_bytes=grant * MIB),
        cost_estimate=pl.CostEstimate(flops=flops, bytes_accessed=MIB, transcendentals=0),
        name=name,
    )(*args)


def per_device(tokens, expert_ids, replicas, scores, w_gate, w_up, w_down):
    rep_count = lax.axis_size("rep")
    ep_count = lax.axis_size("ep")
    tp_count = lax.axis_size("tp")
    tok_rows, part = tokens.shape
    features = part * tp_count
    ffe = w_gate.shape[2]
    rows = ep_count * tok_rows
    bf16, f32 = jnp.bfloat16, jnp.float32
    arr = jax.ShapeDtypeStruct

    blocks = [tokens] + [shift(tokens, "ep", ep_count, s) for s in range(1, ep_count)]
    gate_w, up_w, down_w = fetch_weights(w_gate[0], w_up[0], w_down[0])
    own = jnp.concatenate(blocks, 0)
    others = [shift(own, "tp", tp_count, s) for s in range(1, tp_count)]

    dot_flops = 2 * rows * part * ffe
    gate_acc, up_acc = vmem_call(
        own_kernel, "own_features", [arr((rows, ffe), f32)] * 2, (own, gate_w, up_w), 2 * dot_flops
    )
    hidden, *partials = vmem_call(
        functools.partial(hidden_kernel, tp_count),
        "hidden",
        [arr((rows, ffe), bf16)] + [arr((rows, part), bf16)] * (tp_count - 1),
        (*others, gate_acc, up_acc, gate_w, up_w, down_w),
        3 * (tp_count - 1) * dot_flops,
    )
    arrived = [shift(p, "tp", tp_count, s) for s, p in enumerate(partials, 1)]
    (mine,) = vmem_call(
        down_kernel, "own_down", [arr((rows, part), f32)], (hidden, down_w), dot_flops
    )
    for piece in arrived:
        mine = mine + piece.astype(f32)
    expert_out = mine.astype(bf16).reshape(ep_count, tok_rows, part)

    target = (lax.axis_index("rep") + replicas * (rep_count // REPL)) % rep_count
    cells = (target * ep_count + expert_ids).reshape(-1)
    cell_count = rep_count * ep_count
    counts = jnp.sum(
        (cells[:, None] == jnp.arange(cell_count, dtype=jnp.int32)[None, :]).astype(jnp.int32), 0
    )
    span = 1
    while span < rep_count:
        swap = [(i, i ^ span) for i in range(rep_count)]
        counts = counts + lax.ppermute(counts, "rep", swap)
        span *= 2
    width = -(-cell_count // (tok_rows * LANES)) * LANES
    carried = jnp.pad(counts, (0, tok_rows * width - cell_count)).astype(bf16)
    carried = carried.reshape(tok_rows, width)

    message = jnp.concatenate([expert_out[0], carried], 1)
    back = [message] + [
        shift(jnp.concatenate([expert_out[s], carried], 1), "ep", ep_count, -s)
        for s in range(1, ep_count)
    ]
    sigmoid_scores = jax.nn.sigmoid(scores)
    weights = sigmoid_scores / jnp.sum(sigmoid_scores, 1, keepdims=True) * route_scale
    me = lax.axis_index("ep")
    total = 0.0
    count_total = 0.0
    for s, piece in enumerate(back):
        expert = (me + s) % ep_count
        coefficient = jnp.sum(jnp.where(expert_ids == expert, weights, 0.0), 1, keepdims=True)
        total = total + coefficient * piece[:, :part].astype(f32)
        count_total = count_total + piece[:, part:].astype(f32)
    load_counts = count_total.reshape(-1)[:cell_count].astype(jnp.int32)
    return total.astype(bf16), load_counts.reshape(rep_count, ep_count)


def solution(mesh):
    placed = (
        P(("rep", "ep"), "tp"),
        P(("rep", "ep"), None),
        P(("rep", "ep"), None),
        P(("rep", "ep"), None),
        P("ep", None, "tp"),
        P("ep", None, "tp"),
        P("ep", "tp", None),
    )
    return jax.shard_map(
        per_device,
        mesh=mesh,
        in_specs=placed,
        out_specs=(P(("rep", "ep"), "tp"), P()),
        check_vma=False,
    )
```

time: 87.9 us -> 56.6 us (0.64)
  blocking collectives: 34.5 us -> 0 us
  local copies, waits for them, and re-layouts: 1.27 us -> 16.3 us
  between operations: 14.1 us -> 0.78 us
  matrix products: 12.9 us -> 0 us
  Pallas kernels: 0 us -> 10.1 us
  starting transfers between devices: 4.64 us -> 14.6 us
  waiting for transfers between devices: 16.5 us -> 12.3 us
  other arithmetic: 3.63 us -> 2.22 us
    reduce_scatter x1 -> x0, waiting for transfers between devices: 16.5 us -> none  [per_device(): lax.psum_scatter(lax.dot_general(down_local, hidden, (((0,), (1,)), ((),...]
    all_to_all x1 -> x0, blocking collectives: 15.7 us -> none  [expert_hop(): lax.all_to_all(slot_block, 'ep', split_axis=1, concat_axis=1, tiled=True)]
    unnamed x3 -> x19, local copies, waits for them, and re-layouts: 0.77 us -> 15.9 us
    ppermute x0 -> x10, starting transfers between devices: none -> 14.6 us  [the longest x8 13 us: shift(): lax.ppermute(array, axis, [(i, (i + step) % count) for i in range(count)])]
    dot_general x4 -> x0, matrix products: 12.9 us -> none  [the longest x1 7.85 us: per_device(): lax.dot_general(down_local, hidden, (((0,), (1,)), ((), ())), preferred_e...]
    psum x1 -> x0, blocking collectives: 12.9 us -> none  [per_device(): load_counts = lax.psum(local_counts, ('rep', 'ep'))]
    ppermute x0 -> x10, waiting for transfers between devices: none -> 12.3 us  [the longest x8 12.3 us: shift(): lax.ppermute(array, axis, [(i, (i + step) % count) for i in range(count)])]
    pallas_call x0 -> x4, Pallas kernels: none -> 10.1 us  [the longest x1 6.53 us: fetch_weights(): pl.pallas_call(functools.partial(fetch_kernel, pieces), out_shape=[pltpu....]
  transfers between devices with their start and end apart: 2 -> 10, of which waited for: 1 -> 6; matrix products, arithmetic and copies ran while one was open for 0% -> 3% of each run, Pallas kernels for 0% -> 18%
where the time goes in v1:
time: 56.6 us; the launch traced here: 56.3 us
  local copies, waits for them, and re-layouts  16.3 us (29%)
  starting transfers between devices  14.6 us (26%)
  waiting for transfers between devices  12.3 us (22%)
  Pallas kernels  10.1 us (18%)
  other arithmetic  2.22 us (4%)
  between operations  0.78 us (1%)
    unnamed x19, local copies, waits for them, and re-layouts  15.9 us
    ppermute x8, starting transfers between devices, shift(): lax.ppermute(array, axis, [(i, (i + step) % count) for i in range(count)])  13 us
    ppermute x8, waiting for transfers between devices, shift(): lax.ppermute(array, axis, [(i, (i + step) % count) for i in range(count)])  12.3 us
    pallas_call x1, Pallas kernels, fetch_weights(): pl.pallas_call(functools.partial(fetch_kernel, pieces), out_shape=[pltpu....  6.53 us
    pallas_call x3, Pallas kernels, vmem_call(): pl.pallas_call(kernel, out_shape=outs, in_specs=[pl.BlockSpec(memory_spac...  3.59 us
    ppermute x2, starting transfers between devices, per_device(): counts = counts + lax.ppermute(counts, 'rep', swap)  1.65 us
  transfers between devices with their start and end apart: 10, of which 6 were waited for; matrix products, arithmetic and copies ran while one was open for 3% of the time, Pallas kernels for 18%

profile of v1, /device:TPU:0, one launch (start us, length us, event | category | flops | bytes accessed | tf_op | source)
XLA Modules:
  0.0 56.3 jit_solution(5206072052702396568)
XLA Ops:
  0.6 3.1 %collective-permute-start = (bf16[8,3072]{1,0:T(8,128)(2,1)}, bf16[8,3072]{1,0:T(8,128)(2,1)S(1)}, u32[]{:S(2)}, u32[]{:S(2)}) collective-permute-start(bf16[8,3072]{1,0:T(8,128)(2,1)} %param.7), channel_id=1, source_target_pairs={{0,2},{2,4},{4,6},{6,0},{1,3},{3,5},{5,7},{7,1},{8,10},{10,12},{12... | collective-permute-start | bytes 147464 | tf_op jit(solution)/shard_map/ppermute | solution.py:19
  3.7 2.6 %collective-permute-start.1 = (bf16[8,3072]{1,0:T(8,128)(2,1)}, bf16[8,3072]{1,0:T(8,128)(2,1)S(1)}, u32[]{:S(2)}, u32[]{:S(2)}) collective-permute-start(bf16[8,3072]{1,0:T(8,128)(2,1)} %param.7), channel_id=1, source_target_pairs={{0,4},{2,6},{4,0},{6,2},{1,5},{3,7},{5,1},{7,3},{8,12},{10,14},{12... | collective-permute-start | bytes 147464 | tf_op jit(solution)/shard_map/ppermute | solution.py:19
  6.3 1.3 %collective-permute-start.2 = (bf16[8,3072]{1,0:T(8,128)(2,1)}, bf16[8,3072]{1,0:T(8,128)(2,1)S(1)}, u32[]{:S(2)}, u32[]{:S(2)}) collective-permute-start(bf16[8,3072]{1,0:T(8,128)(2,1)} %param.7), channel_id=1, source_target_pairs={{0,6},{2,0},{4,2},{6,4},{1,7},{3,1},{5,3},{7,5},{8,14},{10,8},{12,... | collective-permute-start | bytes 147464 | tf_op jit(solution)/shard_map/ppermute | solution.py:19
  7.7 0.8 %constant_dynamic-update-slice_fusion.3 = bf16[32,3072]{1,0:T(8,128)(2,1)S(1)} fusion(bf16[8,3072]{1,0:T(8,128)(2,1)} %param.7), kind=kLoop, calls=%fused_computation.8 | loop fusion | bytes 98304
  8.5 0.7 %fusion.3 = s32[8,2]{0,1:T(2,128)S(1)} fusion(s32[8,2]{0,1:T(2,128)} %param.8, s32[8,2]{0,1:T(2,128)} %param.9, s32[]{:T(128)S(6)} %axis_index.28), kind=kLoop, calls=%fused_computation.24 | loop fusion | flops 224 | bytes 196 | tf_op jit(solution)/shard_map/add | solution.py:143
  9.2 0.1 copy.11
  9.3 0.1 eq.50
  9.4 0.7 %collective-permute-done.1 = bf16[8,3072]{1,0:T(8,128)(2,1)S(1)} collective-permute-done((bf16[8,3072]{1,0:T(8,128)(2,1)}, bf16[8,3072]{1,0:T(8,128)(2,1)S(1)}, u32[]{:S(2)}, u32[]{:S(2)}) %collective-permute-start.1) | collective-permute-done | bytes 49184 | tf_op jit(solution)/shard_map/ppermute | solution.py:19
  10.1 0.5 collective-permute-done.2
  10.7 1.6 %collective-permute-start.3 = (bf16[32,3072]{1,0:T(8,128)(2,1)S(1)}, bf16[32,3072]{1,0:T(8,128)(2,1)S(1)}, u32[]{:S(2)}, u32[]{:S(2)}) collective-permute-start(bf16[32,3072]{1,0:T(8,128)(2,1)S(1)} %constant_dynamic-update-slice_fusion.x_ref), channel_id=1, source_target_pairs={{0,1},{1,0},{2,3},{3,2},{4,5},{5,4},{6,7},{7,6},{8,9},{9,8},{10,11... | collective-permute-start | bytes 589832 | tf_op jit(solution)/shard_map/ppermute | solution.py:19
  12.3 0.1 convert_reduce_fusion
  12.5 6.5 %fetch_weights.1 = (bf16[6144,512]{1,0:T(8,128)(2,1)S(1)}, bf16[6144,512]{1,0:T(8,128)(2,1)S(1)}, bf16[512,6144]{1,0:T(8,128)(2,1)S(1)}) custom-call(bf16[6144,512]{1,0:T(8,128)(2,1)} %bitcast.7, bf16[6144,512]{1,0:T(8,128)(2,1)} %bitcast.8, bf16[512,6144]{1,0:T(8,128)(2,1)} %bitcast.9), custom_call_target="tpu_custom_call" | custom-call | flops 100000000 | bytes 18874368 | tf_op jit(solution)/shard_map/fetch_weights/pallas_call | solution.py:40
  19.0 2.7 %copy-done = bf16[512,6144]{1,0:T(8,128)(2,1)} copy-done((bf16[512,6144]{1,0:T(8,128)(2,1)}, bf16[512,6144]{1,0:T(8,128)(2,1)S(1)}, u32[]{:S(2)}) %copy-start) | copy-done | bytes 6291480
  21.7 2.6 %copy-done.2 = bf16[6144,512]{1,0:T(8,128)(2,1)} copy-done((bf16[6144,512]{1,0:T(8,128)(2,1)}, bf16[6144,512]{1,0:T(8,128)(2,1)S(1)}, u32[]{:S(2)}) %copy-start.2) | copy-done | bytes 6291480
  24.3 2.6 %copy-done.4 = bf16[6144,512]{1,0:T(8,128)(2,1)} copy-done((bf16[6144,512]{1,0:T(8,128)(2,1)}, bf16[6144,512]{1,0:T(8,128)(2,1)S(1)}, u32[]{:S(2)}) %copy-start.4) | copy-done | bytes 6291480
  27.0 1.6 %collective-permute-start.6 = (s32[16]{0:T(128)S(1)}, s32[16]{0:T(128)S(1)}, u32[]{:S(2)}, u32[]{:S(2)}) collective-permute-start(s32[16]{0:T(128)S(1)} %add.78), channel_id=1, source_target_pairs={{0,16},{8,24},{16,0},{24,8},{1,17},{9,25},{17,1},{25,9},{2,18},{10... | collective-permute-start | bytes 200 | tf_op jit(solution)/shard_map/ppermute | solution.py:151
  28.6 2.8 %copy-done.3 = bf16[6144,512]{1,0:T(8,128)(2,1)S(1)} copy-done((bf16[6144,512]{1,0:T(8,128)(2,1)S(1)}, bf16[6144,512]{1,0:T(8,128)(2,1)}, u32[]{:S(2)}) %copy-start.3) | copy-done | bytes 6291480
  31.3 2.8 %copy-done.5 = bf16[6144,512]{1,0:T(8,128)(2,1)S(1)} copy-done((bf16[6144,512]{1,0:T(8,128)(2,1)S(1)}, bf16[6144,512]{1,0:T(8,128)(2,1)}, u32[]{:S(2)}) %copy-start.5) | copy-done | bytes 6291480
  34.1 1.2 %own_features.1 = (f32[32,512]{1,0:T(8,128)S(1)}, f32[32,512]{1,0:T(8,128)S(1)}) custom-call(bf16[32,3072]{1,0:T(8,128)(2,1)S(1)} %constant_dynamic-update-slice_fusion.x_ref, bf16[6144,512]{1,0:T(8,128)(2,1)S(1)} %copy-done.3, bf16[6144,512]{1,0:T(8,128)(2,1)S(1)} %copy-done.5), custom_call_target="tpu_custom_call" | custom-call | flops 201326592 | bytes 1048576 | tf_op jit(solution)/shard_map/own_features/pallas_call | solution.py:96
  35.3 1.6 %copy-done.1 = bf16[512,6144]{1,0:T(8,128)(2,1)S(1)} copy-done((bf16[512,6144]{1,0:T(8,128)(2,1)S(1)}, bf16[512,6144]{1,0:T(8,128)(2,1)}, u32[]{:S(2)}) %copy-start.1) | copy-done | bytes 6291480
  36.9 1.8 %hidden.1 = (bf16[32,512]{1,0:T(8,128)(2,1)S(1)}, bf16[32,3072]{1,0:T(8,128)(2,1)S(1)}) custom-call(bf16[32,3072]{1,0:T(8,128)(2,1)S(1)} %collective-permute-done.3.refs_0_, f32[32,512]{1,0:T(8,128)S(1)} %get-tuple-element.11.refs_1_, f32[32,512]{1,0:T(8,128)S(1)} %get-tuple-element.12.refs_2_, bf16[6144,512]{1,0:T(8,128)(2,1)S(1)} %copy-done.3, ...), custom_call_target="tpu_custom_call" | custom-call | flops 301989888 | bytes 1048576 | tf_op jit(solution)/shard_map/hidden/pallas_call | solution.py:96
  38.7 0.6 %collective-permute-start.4 = (bf16[32,3072]{1,0:T(8,128)(2,1)S(1)}, bf16[32,3072]{1,0:T(8,128)(2,1)S(1)}, u32[]{:S(2)}, u32[]{:S(2)}) collective-permute-start(bf16[32,3072]{1,0:T(8,128)(2,1)S(1)} %get-tuple-element.15), channel_id=1, source_target_pairs={{0,1},{1,0},{2,3},{3,2},{4,5},{5,4},{6,7},{7,6},{8,9},{9,8},{10,11... | collective-permute-start | bytes 589832 | tf_op jit(solution)/shard_map/ppermute | solution.py:19
  39.3 0.6 %own_down.1 = f32[32,3072]{1,0:T(8,128)S(1)} custom-call(bf16[32,512]{1,0:T(8,128)(2,1)S(1)} %get-tuple-element.14.hidden_ref, bf16[512,6144]{1,0:T(8,128)(2,1)S(1)} %copy-done.1), custom_call_target="tpu_custom_call" | custom-call | flops 100663296 | bytes 1048576 | tf_op jit(solution)/shard_map/own_down/pallas_call | solution.py:96
  40.0 5.8 %collective-permute-done.4 = bf16[32,3072]{1,0:T(8,128)(2,1)S(1)} collective-permute-done((bf16[32,3072]{1,0:T(8,128)(2,1)S(1)}, bf16[32,3072]{1,0:T(8,128)(2,1)S(1)}, u32[]{:S(2)}, u32[]{:S(2)}) %collective-permute-start.4) | collective-permute-done | bytes 196640 | tf_op jit(solution)/shard_map/ppermute | solution.py:19
  45.8 3.1 %collective-permute-start.7 = (bf16[8,3200]{1,0:T(8,128)(2,1)S(1)}, bf16[8,3200]{1,0:T(8,128)(2,1)S(1)}, u32[]{:S(2)}, u32[]{:S(2)}) collective-permute-start(bf16[8,3200]{1,0:T(8,128)(2,1)S(1)} %get-tuple-element.23), channel_id=1, source_target_pairs={{0,6},{2,0},{4,2},{6,4},{1,7},{3,1},{5,3},{7,5},{8,14},{10,8},{12,... | collective-permute-start | bytes 153608 | tf_op jit(solution)/shard_map/ppermute | solution.py:19
  48.9 0.6 %collective-permute-start.9 = (bf16[8,3200]{1,0:T(8,128)(2,1)S(1)}, bf16[8,3200]{1,0:T(8,128)(2,1)S(1)}, u32[]{:S(2)}, u32[]{:S(2)}) collective-permute-start(bf16[8,3200]{1,0:T(8,128)(2,1)S(1)} %get-tuple-element.24), channel_id=1, source_target_pairs={{0,2},{2,4},{4,6},{6,0},{1,3},{3,5},{5,7},{7,1},{8,10},{10,12},{12... | collective-permute-start | bytes 153608 | tf_op jit(solution)/shard_map/ppermute | solution.py:19
  49.6 1.1 %collective-permute-done.7 = bf16[8,3200]{1,0:T(8,128)(2,1)S(1)} collective-permute-done((bf16[8,3200]{1,0:T(8,128)(2,1)S(1)}, bf16[8,3200]{1,0:T(8,128)(2,1)S(1)}, u32[]{:S(2)}, u32[]{:S(2)}) %collective-permute-start.7) | collective-permute-done | bytes 51232 | tf_op jit(solution)/shard_map/ppermute | solution.py:19
  50.7 3.2 %collective-permute-done.8 = bf16[8,3200]{1,0:T(8,128)(2,1)S(1)} collective-permute-done((bf16[8,3200]{1,0:T(8,128)(2,1)S(1)}, bf16[8,3200]{1,0:T(8,128)(2,1)S(1)}, u32[]{:S(2)}, u32[]{:S(2)}) %collective-permute-start.8) | collective-permute-done | bytes 51232 | tf_op jit(solution)/shard_map/ppermute | solution.py:19
  53.9 0.9 %collective-permute-done.9 = bf16[8,3200]{1,0:T(8,128)(2,1)S(1)} collective-permute-done((bf16[8,3200]{1,0:T(8,128)(2,1)S(1)}, bf16[8,3200]{1,0:T(8,128)(2,1)S(1)}, u32[]{:S(2)}, u32[]{:S(2)}) %collective-permute-start.9) | collective-permute-done | bytes 51232 | tf_op jit(solution)/shard_map/ppermute | solution.py:19
  54.8 0.1 slice.50
  55.0 0.6 %slice_convert_fusion = s32[4,4]{1,0:T(4,128)} fusion(f32[256,4]{1,0:T(8,128)S(1)} %slice.50), kind=kLoop, calls=%fused_computation.14 | loop fusion | flops 16 | bytes 128 | tf_op jit(solution)/shard_map/convert_element_type | solution.py:172
  55.5 0.7 %add_convert_fusion.1 = bf16[8,3072]{1,0:T(8,128)(2,1)} fusion(bf16[8,3200]{1,0:T(8,128)(2,1)S(1)} %collective-permute-done.9, bf16[8,3200]{1,0:T(8,128)(2,1)S(1)} %collective-permute-done.8, bf16[8,3200]{1,0:T(8,128)(2,1)S(1)} %collective-permute-done.7, bf16[32,3072]{1,0:T(8,128)(2,1)S(1)} %add_convert_fusion, f32[8]{0:T(128)S(1)} %get-tuple-element.17, ...), kind=kLoop, calls=%fused_computation.1 | loop fusion | flops 294912 | bytes 245888 | tf_op jit(solution)/shard_map/convert_element_type | solution.py:173
  (28 shorter events, 0.3 us)
Async XLA Ops:
  0.6 8.8 %collective-permute-start = (bf16[8,3072]{1,0:T(8,128)(2,1)}, bf16[8,3072]{1,0:T(8,128)(2,1)S(1)}, u32[]{:S(2)}, u32[]{:S(2)}) collective-permute-start(bf16[8,3072]{1,0:T(8,128)(2,1)} %param.7), channel_id=1, source_target_pairs={{0,2},{2,4},{4,6},{6,0},{1,3},{3,5},{5,7},{7,1},{8,10},{10,12},{12... | collective-permute-start | bytes 147464 | tf_op jit(solution)/shard_map/ppermute | solution.py:19
  3.7 6.4 %collective-permute-start.1 = (bf16[8,3072]{1,0:T(8,128)(2,1)}, bf16[8,3072]{1,0:T(8,128)(2,1)S(1)}, u32[]{:S(2)}, u32[]{:S(2)}) collective-permute-start(bf16[8,3072]{1,0:T(8,128)(2,1)} %param.7), channel_id=1, source_target_pairs={{0,4},{2,6},{4,0},{6,2},{1,5},{3,7},{5,1},{7,3},{8,12},{10,14},{12... | collective-permute-start | bytes 147464 | tf_op jit(solution)/shard_map/ppermute | solution.py:19
  6.3 4.3 %collective-permute-start.2 = (bf16[8,3072]{1,0:T(8,128)(2,1)}, bf16[8,3072]{1,0:T(8,128)(2,1)S(1)}, u32[]{:S(2)}, u32[]{:S(2)}) collective-permute-start(bf16[8,3072]{1,0:T(8,128)(2,1)} %param.7), channel_id=1, source_target_pairs={{0,6},{2,0},{4,2},{6,4},{1,7},{3,1},{5,3},{7,5},{8,14},{10,8},{12,... | collective-permute-start | bytes 147464 | tf_op jit(solution)/shard_map/ppermute | solution.py:19
  10.7 24.6 %collective-permute-start.3 = (bf16[32,3072]{1,0:T(8,128)(2,1)S(1)}, bf16[32,3072]{1,0:T(8,128)(2,1)S(1)}, u32[]{:S(2)}, u32[]{:S(2)}) collective-permute-start(bf16[32,3072]{1,0:T(8,128)(2,1)S(1)} %constant_dynamic-update-slice_fusion.x_ref), channel_id=1, source_target_pairs={{0,1},{1,0},{2,3},{3,2},{4,5},{5,4},{6,7},{7,6},{8,9},{9,8},{10,11... | collective-permute-start | bytes 589832 | tf_op jit(solution)/shard_map/ppermute | solution.py:19
  12.3 14.6 %collective-permute-start.5 = (s32[16]{0:T(128)S(1)}, s32[16]{0:T(128)S(1)}, u32[]{:S(2)}, u32[]{:S(2)}) collective-permute-start(s32[16]{0:T(128)S(1)} %convert_reduce_fusion), channel_id=1, source_target_pairs={{0,8},{8,0},{16,24},{24,16},{1,9},{9,1},{17,25},{25,17},{2,10},{10... | collective-permute-start | bytes 200 | tf_op jit(solution)/shard_map/ppermute | solution.py:151
  12.5 14.5 %copy-start.7 = (f32[8,2]{0,1:T(2,128)S(1)}, f32[8,2]{0,1:T(2,128)}, u32[]{:S(2)}) copy-start(f32[8,2]{0,1:T(2,128)} %param.10) | copy-start | bytes 196
  19.0 2.7 %copy-start = (bf16[512,6144]{1,0:T(8,128)(2,1)}, bf16[512,6144]{1,0:T(8,128)(2,1)S(1)}, u32[]{:S(2)}) copy-start(bf16[512,6144]{1,0:T(8,128)(2,1)S(1)} %get-tuple-element.13.refs_5_.down_ref) | copy-start | bytes 18874372
  21.7 2.6 %copy-start.2 = (bf16[6144,512]{1,0:T(8,128)(2,1)}, bf16[6144,512]{1,0:T(8,128)(2,1)S(1)}, u32[]{:S(2)}) copy-start(bf16[6144,512]{1,0:T(8,128)(2,1)S(1)} %get-tuple-element.9.gate_ref.refs_3_) | copy-start | bytes 18874372
  24.3 2.6 %copy-start.4 = (bf16[6144,512]{1,0:T(8,128)(2,1)}, bf16[6144,512]{1,0:T(8,128)(2,1)S(1)}, u32[]{:S(2)}) copy-start(bf16[6144,512]{1,0:T(8,128)(2,1)S(1)} %get-tuple-element.10.up_ref.refs_4_) | copy-start | bytes 18874372
  27.0 12.3 %collective-permute-start.6 = (s32[16]{0:T(128)S(1)}, s32[16]{0:T(128)S(1)}, u32[]{:S(2)}, u32[]{:S(2)}) collective-permute-start(s32[16]{0:T(128)S(1)} %add.78), channel_id=1, source_target_pairs={{0,16},{8,24},{16,0},{24,8},{1,17},{9,25},{17,1},{25,9},{2,18},{10... | collective-permute-start | bytes 200 | tf_op jit(solution)/shard_map/ppermute | solution.py:151
  28.6 2.8 %copy-start.3 = (bf16[6144,512]{1,0:T(8,128)(2,1)S(1)}, bf16[6144,512]{1,0:T(8,128)(2,1)}, u32[]{:S(2)}) copy-start(bf16[6144,512]{1,0:T(8,128)(2,1)} %copy-done.2) | copy-start | bytes 18874372
  31.3 2.8 %copy-start.5 = (bf16[6144,512]{1,0:T(8,128)(2,1)S(1)}, bf16[6144,512]{1,0:T(8,128)(2,1)}, u32[]{:S(2)}) copy-start(bf16[6144,512]{1,0:T(8,128)(2,1)} %copy-done.4) | copy-start | bytes 18874372
  34.1 2.8 %copy-start.1 = (bf16[512,6144]{1,0:T(8,128)(2,1)S(1)}, bf16[512,6144]{1,0:T(8,128)(2,1)}, u32[]{:S(2)}) copy-start(bf16[512,6144]{1,0:T(8,128)(2,1)} %copy-done) | copy-start | bytes 18874372
  38.7 10.8 %copy-start.6 = (s32[8,2]{0,1:T(2,128)S(1)}, s32[8,2]{0,1:T(2,128)}, u32[]{:S(2)}) copy-start(s32[8,2]{0,1:T(2,128)} %param.8) | copy-start | bytes 196
  38.7 7.0 %collective-permute-start.4 = (bf16[32,3072]{1,0:T(8,128)(2,1)S(1)}, bf16[32,3072]{1,0:T(8,128)(2,1)S(1)}, u32[]{:S(2)}, u32[]{:S(2)}) collective-permute-start(bf16[32,3072]{1,0:T(8,128)(2,1)S(1)} %get-tuple-element.15), channel_id=1, source_target_pairs={{0,1},{1,0},{2,3},{3,2},{4,5},{5,4},{6,7},{7,6},{8,9},{9,8},{10,11... | collective-permute-start | bytes 589832 | tf_op jit(solution)/shard_map/ppermute | solution.py:19
  45.8 4.8 %collective-permute-start.7 = (bf16[8,3200]{1,0:T(8,128)(2,1)S(1)}, bf16[8,3200]{1,0:T(8,128)(2,1)S(1)}, u32[]{:S(2)}, u32[]{:S(2)}) collective-permute-start(bf16[8,3200]{1,0:T(8,128)(2,1)S(1)} %get-tuple-element.23), channel_id=1, source_target_pairs={{0,6},{2,0},{4,2},{6,4},{1,7},{3,1},{5,3},{7,5},{8,14},{10,8},{12,... | collective-permute-start | bytes 153608 | tf_op jit(solution)/shard_map/ppermute | solution.py:19
  48.9 5.0 %collective-permute-start.8 = (bf16[8,3200]{1,0:T(8,128)(2,1)S(1)}, bf16[8,3200]{1,0:T(8,128)(2,1)S(1)}, u32[]{:S(2)}, u32[]{:S(2)}) collective-permute-start(bf16[8,3200]{1,0:T(8,128)(2,1)S(1)} %get-tuple-element.25), channel_id=1, source_target_pairs={{0,4},{2,6},{4,0},{6,2},{1,5},{3,7},{5,1},{7,3},{8,12},{10,14},{12... | collective-permute-start | bytes 153608 | tf_op jit(solution)/shard_map/ppermute | solution.py:19
  48.9 5.9 %collective-permute-start.9 = (bf16[8,3200]{1,0:T(8,128)(2,1)S(1)}, bf16[8,3200]{1,0:T(8,128)(2,1)S(1)}, u32[]{:S(2)}, u32[]{:S(2)}) collective-permute-start(bf16[8,3200]{1,0:T(8,128)(2,1)S(1)} %get-tuple-element.24), channel_id=1, source_target_pairs={{0,2},{2,4},{4,6},{6,0},{1,3},{3,5},{5,7},{7,1},{8,10},{10,12},{12... | collective-permute-start | bytes 153608 | tf_op jit(solution)/shard_map/ppermute | solution.py:19

commit v2 on v1

v2 whole, which is shorter than its diff:
```python
import functools

import jax
import jax.numpy as jnp
from jax import lax
from jax.experimental import pallas as pl
from jax.experimental.pallas import tpu as pltpu
from jax.sharding import PartitionSpec as P

REPL = 4
LANES = 128
PIECES = 2
MIB = 1 << 20

route_scale = 2.5


def shift(array, axis, count, step):
    return lax.ppermute(array, axis, [(i, (i + step) % count) for i in range(count)])


def swap(array, axis, count, span):
    return lax.ppermute(array, axis, [(i, i ^ span) for i in range(count)])


def window(index, size):
    return pl.ds(pl.multiple_of(index * size, size), size)


def copies_into(pairs, sems, pieces):
    copies = []
    for source, target in pairs:
        rows = target.shape[0] // pieces
        for piece in range(pieces):
            span = pl.ds(piece * rows, rows)
            copies.append(
                pltpu.make_async_copy(source.at[span], target.at[span], sems.at[len(copies)])
            )
    return copies


def first_kernel(ep_count, rep_count, ids_ref, picks_ref, gate_hbm, up_hbm, *refs):
    gate_out, up_out, counts_ref, sems = refs
    rows = window(lax.axis_index("tp"), gate_out.shape[0])
    copies = copies_into([(gate_hbm.at[rows], gate_out), (up_hbm.at[rows], up_out)], sems, PIECES)
    for copy in copies:
        copy.start()
    target = lax.axis_index("rep") + picks_ref[...] * (rep_count // REPL)
    cells = lax.rem(target, rep_count) * ep_count + ids_ref[...]
    rows, lanes = counts_ref.shape
    position = lax.broadcasted_iota(jnp.int32, (rows, lanes), 0) * lanes
    position = position + lax.broadcasted_iota(jnp.int32, (rows, lanes), 1)
    total = jnp.zeros((rows, lanes), jnp.int32)
    for k in range(cells.shape[0]):
        for t in range(cells.shape[1]):
            total += (position == cells[k : k + 1, t : t + 1]).astype(jnp.int32)
    counts_ref[...] = total
    for copy in copies:
        copy.wait()


def stack_kernel(*refs):
    pieces, out_ref = refs[:-2], refs[-1]
    for s, piece in enumerate(pieces):
        out_ref[pl.ds(s * piece.shape[0], piece.shape[0]), :] = piece[...]


def own_kernel(tp_count, *refs):
    x_ref, gate_ref, up_ref, gate_hbm, up_hbm, down_hbm = refs[:6]
    gate_acc, up_acc, gate_rest, up_rest, down_out, sems = refs[6:]
    part = x_ref.shape[1]
    me = lax.axis_index("tp")
    pairs = []
    for step in range(1, tp_count):
        rows = window(lax.rem(me - step + tp_count, tp_count), part)
        held = pl.ds((step - 1) * part, part)
        pairs.append((gate_hbm.at[rows], gate_rest.at[held]))
        pairs.append((up_hbm.at[rows], up_rest.at[held]))
    pairs.append((down_hbm, down_out))
    copies = copies_into(pairs, sems, PIECES)
    for copy in copies:
        copy.start()
    x = x_ref[...]
    gate_acc[...] = jnp.dot(x, gate_ref[...], preferred_element_type=jnp.float32)
    up_acc[...] = jnp.dot(x, up_ref[...], preferred_element_type=jnp.float32)
    for copy in copies:
        copy.wait()


def hidden_kernel(tp_count, *refs):
    others = refs[: tp_count - 1]
    gate_acc, up_acc, gate_ref, up_ref, down_ref = refs[tp_count - 1 : tp_count + 4]
    hidden_out = refs[tp_count + 4]
    partial_outs = refs[tp_count + 5 :]
    me = lax.axis_index("tp")
    gate = gate_acc[...]
    up = up_acc[...]
    for step, other in enumerate(others):
        rows = pl.ds(step * other.shape[1], other.shape[1])
        x = other[...]
        gate += jnp.dot(x, gate_ref[rows, :], preferred_element_type=jnp.float32)
        up += jnp.dot(x, up_ref[rows, :], preferred_element_type=jnp.float32)
    hidden = (gate / (1.0 + jnp.exp(-gate)) * up).astype(jnp.bfloat16)
    hidden_out[...] = hidden
    for step, out in enumerate(partial_outs, 1):
        columns = window(lax.rem(me + step, tp_count), out.shape[1])
        out[...] = jnp.dot(
            hidden, down_ref[:, columns], preferred_element_type=jnp.float32
        ).astype(jnp.bfloat16)


def down_kernel(hidden_ref, down_ref, counts_ref, swapped_ref, out_ref, sum_ref):
    sum_ref[...] = counts_ref[...] + swapped_ref[...]
    columns = window(lax.axis_index("tp"), out_ref.shape[1])
    out_ref[...] = jnp.dot(
        hidden_ref[...], down_ref[:, columns], preferred_element_type=jnp.float32
    )


def pack_kernel(arrived_count, *refs):
    mine_ref = refs[0]
    arrived = refs[1 : 1 + arrived_count]
    counts = refs[1 + arrived_count : 3 + arrived_count]
    outs = refs[3 + arrived_count :]
    tok_rows, part = outs[0].shape[0], mine_ref.shape[1]
    carried = (counts[0][...] + counts[1][...]).astype(jnp.float32).astype(jnp.bfloat16)
    for s, out in enumerate(outs):
        rows = pl.ds(s * tok_rows, tok_rows)
        total = mine_ref[rows, :]
        for piece in arrived:
            total += piece[rows, :].astype(jnp.float32)
        out[:, :part] = total.astype(jnp.bfloat16)
        out[:, part:] = carried


def combine_kernel(ep_count, ids_ref, scores_ref, *refs):
    pieces, (out_ref, counts_ref) = refs[:-2], refs[-2:]
    tok_rows, part = out_ref.shape
    me = lax.axis_index("ep")
    gains = jax.nn.sigmoid(scores_ref[...])
    weights = gains / jnp.sum(gains, 0, keepdims=True) * route_scale
    ids = ids_ref[...]
    total = jnp.zeros((tok_rows, part), jnp.float32)
    counts = jnp.zeros(counts_ref.shape, jnp.float32)
    diagonal = lax.broadcasted_iota(jnp.int32, (tok_rows, tok_rows), 0) == (
        lax.broadcasted_iota(jnp.int32, (tok_rows, tok_rows), 1)
    )
    for s, piece in enumerate(pieces):
        expert = lax.rem(me + s, ep_count)
        row = jnp.sum(jnp.where(ids == expert, weights, 0.0), 0, keepdims=True)
        column = jnp.sum(jnp.where(diagonal, row, 0.0), 1, keepdims=True)
        total += column * piece[:, :part].astype(jnp.float32)
        counts += piece[:, part:].astype(jnp.float32)
    out_ref[...] = total.astype(jnp.bfloat16)
    counts_ref[...] = counts.astype(jnp.int32)


def vmem_call(kernel, name, outs, args, flops, remote=0, copies=0):
    specs = [pl.BlockSpec(memory_space=pltpu.VMEM)] * (len(args) - remote)
    return pl.pallas_call(
        kernel,
        out_shape=[pltpu.VMEM(shape, dtype) for shape, dtype in outs],
        in_specs=specs + [pl.BlockSpec(memory_space=pltpu.HBM)] * remote,
        out_specs=[pl.BlockSpec(memory_space=pltpu.VMEM)] * len(outs),
        scratch_shapes=[pltpu.SemaphoreType.DMA((copies,))] if copies else [],
        compiler_params=pltpu.CompilerParams(vmem_limit_bytes=24 * MIB),
        cost_estimate=pl.CostEstimate(flops=flops, bytes_accessed=MIB, transcendentals=0),
        name=name,
    )(*args)


def per_device(tokens, expert_ids, replicas, scores, w_gate, w_up, w_down):
    rep_count = lax.axis_size("rep")
    ep_count = lax.axis_size("ep")
    tp_count = lax.axis_size("tp")
    tok_rows, part = tokens.shape
    ffe = w_gate.shape[2]
    rows = ep_count * tok_rows
    bf16, f32, i32 = jnp.bfloat16, jnp.float32, jnp.int32
    gate_w, up_w, down_w = (
        pltpu.with_memory_space_constraint(w[0], pltpu.HBM) for w in (w_gate, w_up, w_down)
    )
    ids, picks, gains = expert_ids.T, replicas.T, scores.T

    blocks = [tokens] + [shift(tokens, "ep", ep_count, s) for s in range(1, ep_count)]

    cell_count = rep_count * ep_count
    width = -(-cell_count // (tok_rows * LANES)) * LANES
    table = ((tok_rows, width), i32)
    gate_own, up_own, counts = vmem_call(
        functools.partial(first_kernel, ep_count, rep_count),
        "first_weights",
        [((part, ffe), bf16)] * 2 + [table],
        (ids, picks, gate_w, up_w),
        10**8,
        remote=2,
        copies=2 * PIECES,
    )
    (own,) = vmem_call(stack_kernel, "stack", [((rows, part), bf16)], (*blocks, counts), 1000)
    others = [shift(own, "tp", tp_count, s) for s in range(1, tp_count)]
    spans = [1 << bit for bit in range(rep_count.bit_length() - 1)]
    for span in spans[:-1]:
        swapped = swap(counts, "rep", rep_count, span)
        if span != spans[-2]:
            counts = counts + swapped
    dot_flops = 2 * rows * part * ffe
    rest = ((tp_count - 1) * part, ffe)
    gate_acc, up_acc, gate_rest, up_rest, down = vmem_call(
        functools.partial(own_kernel, tp_count),
        "own_features",
        [((rows, ffe), f32)] * 2 + [(rest, bf16)] * 2 + [(down_w.shape, bf16)],
        (own, gate_own, up_own, gate_w, up_w, down_w),
        2 * dot_flops,
        remote=3,
        copies=(2 * tp_count - 1) * PIECES,
    )
    hidden, *partials = vmem_call(
        functools.partial(hidden_kernel, tp_count),
        "hidden",
        [((rows, ffe), bf16)] + [((rows, part), bf16)] * (tp_count - 1),
        (*others, gate_acc, up_acc, gate_rest, up_rest, down),
        3 * (tp_count - 1) * dot_flops,
    )
    arrived = [shift(p, "tp", tp_count, s) for s, p in enumerate(partials, 1)]
    mine, counts = vmem_call(
        down_kernel,
        "own_down",
        [((rows, part), f32), table],
        (hidden, down, counts, swapped),
        dot_flops,
    )
    swapped = swap(counts, "rep", rep_count, spans[-1])

    outgoing = vmem_call(
        functools.partial(pack_kernel, tp_count - 1),
        "pack",
        [((tok_rows, part + width), bf16)] * ep_count,
        (mine, *arrived, counts, swapped),
        rows * part,
    )
    back = [outgoing[0]] + [
        shift(outgoing[s], "ep", ep_count, -s) for s in range(1, ep_count)
    ]
    moe_out, totals = pl.pallas_call(
        functools.partial(combine_kernel, ep_count),
        out_shape=[
            jax.ShapeDtypeStruct((tok_rows, part), bf16),
            jax.ShapeDtypeStruct((tok_rows, width), i32),
        ],
        compiler_params=pltpu.CompilerParams(vmem_limit_bytes=8 * MIB),
        name="combine",
    )(ids, gains, *back)
    load_counts = totals.reshape(-1)[:cell_count].reshape(rep_count, ep_count)
    return moe_out, load_counts


def solution(mesh):
    placed = (
        P(("rep", "ep"), "tp"),
        P(("rep", "ep"), None),
        P(("rep", "ep"), None),
        P(("rep", "ep"), None),
        P("ep", None, "tp"),
        P("ep", None, "tp"),
        P("ep", "tp", None),
    )
    return jax.shard_map(
        per_device,
        mesh=mesh,
        in_specs=placed,
        out_specs=(P(("rep", "ep"), "tp"), P()),
        check_vma=False,
    )
```

time: 56.6 us -> 37 us (0.65)
  local copies, waits for them, and re-layouts: 16.3 us -> 2.08 us
  waiting for transfers between devices: 12.3 us -> 8.87 us
  other arithmetic: 2.22 us -> 0 us
  Pallas kernels: 10.1 us -> 11.9 us
  starting transfers between devices: 14.6 us -> 13.2 us
    unnamed x19 -> x10, local copies, waits for them, and re-layouts: 15.9 us -> 1.37 us
    ppermute x8, waiting for transfers between devices: 12.3 us -> 5.62 us  [shift(): lax.ppermute(array, axis, [(i, (i + step) % count) for i in range(count)])]
    ppermute x2, waiting for transfers between devices: 0.01 us -> 3.25 us  [swap(): return lax.ppermute(array, axis, [(i, i ^ span) for i in range(count)])]
    pallas_call x4 -> x7, Pallas kernels: 10.1 us -> 11.9 us  [the longest x6 11.1 us: vmem_call(): pl.pallas_call(kernel, out_shape=[pltpu.VMEM(shape, dtype) for shape, dty...]
    convert_element_type x3 -> x0, other arithmetic: 1.34 us -> none  [the longest x1 0.73 us: per_device(): return (total.astype(bf16), load_counts.reshape(rep_count, ep_count))]
    ppermute x8, starting transfers between devices: 13 us -> 11.7 us  [shift(): lax.ppermute(array, axis, [(i, (i + step) % count) for i in range(count)])]
    add x3 -> x0, other arithmetic: 0.72 us -> none  [the longest x1 0.71 us: per_device(): cells = (target * ep_count + expert_ids).reshape(-1)]
  transfers between devices with their start and end apart: 10 -> 10, of which waited for: 6 -> 5; matrix products, arithmetic and copies ran while one was open for 3% -> 0% of each run, Pallas kernels for 18% -> 25%
where the time goes in v2:
time: 37 us; the launch traced here: 36.8 us
  starting transfers between devices  13.2 us (36%)
  Pallas kernels  11.9 us (32%)
  waiting for transfers between devices  8.87 us (24%)
  local copies, waits for them, and re-layouts  2.08 us (6%)
  between operations  0.73 us (2%)
    ppermute x8, starting transfers between devices, shift(): lax.ppermute(array, axis, [(i, (i + step) % count) for i in range(count)])  11.7 us
    pallas_call x6, Pallas kernels, vmem_call(): pl.pallas_call(kernel, out_shape=[pltpu.VMEM(shape, dtype) for shape, dty...  11.1 us
    ppermute x8, waiting for transfers between devices, shift(): lax.ppermute(array, axis, [(i, (i + step) % count) for i in range(count)])  5.62 us
    ppermute x2, waiting for transfers between devices, swap(): return lax.ppermute(array, axis, [(i, i ^ span) for i in range(count)])  3.25 us
    ppermute x2, starting transfers between devices, swap(): return lax.ppermute(array, axis, [(i, i ^ span) for i in range(count)])  1.54 us
    unnamed x10, local copies, waits for them, and re-layouts  1.37 us
    pallas_call x1, Pallas kernels, per_device(): pl.pallas_call(functools.partial(combine_kernel, ep_count), out_shape=[ja...  0.77 us
  transfers between devices with their start and end apart: 10, of which 5 were waited for; matrix products, arithmetic and copies ran while one was open for 0% of the time, Pallas kernels for 25%

profile of v2, /device:TPU:0, one launch (start us, length us, event | category | flops | bytes accessed | tf_op | source)
XLA Modules:
  0.0 36.8 jit_solution(12207234829645679353)
XLA Ops:
  0.6 3.1 %collective-permute-start = (bf16[8,3072]{1,0:T(8,128)(2,1)}, bf16[8,3072]{1,0:T(8,128)(2,1)S(1)}, u32[]{:S(2)}, u32[]{:S(2)}) collective-permute-start(bf16[8,3072]{1,0:T(8,128)(2,1)} %refs_0_.1), channel_id=1, source_target_pairs={{0,2},{2,4},{4,6},{6,0},{1,3},{3,5},{5,7},{7,1},{8,10},{10,12},{12... | collective-permute-start | bytes 147464 | tf_op jit(solution)/shard_map/ppermute | solution.py:19
  3.7 2.6 %collective-permute-start.1 = (bf16[8,3072]{1,0:T(8,128)(2,1)}, bf16[8,3072]{1,0:T(8,128)(2,1)S(1)}, u32[]{:S(2)}, u32[]{:S(2)}) collective-permute-start(bf16[8,3072]{1,0:T(8,128)(2,1)} %refs_0_.1), channel_id=1, source_target_pairs={{0,4},{2,6},{4,0},{6,2},{1,5},{3,7},{5,1},{7,3},{8,12},{10,14},{12... | collective-permute-start | bytes 147464 | tf_op jit(solution)/shard_map/ppermute | solution.py:19
  6.3 1.3 %collective-permute-start.2 = (bf16[8,3072]{1,0:T(8,128)(2,1)}, bf16[8,3072]{1,0:T(8,128)(2,1)S(1)}, u32[]{:S(2)}, u32[]{:S(2)}) collective-permute-start(bf16[8,3072]{1,0:T(8,128)(2,1)} %refs_0_.1), channel_id=1, source_target_pairs={{0,6},{2,0},{4,2},{6,4},{1,7},{3,1},{5,3},{7,5},{8,14},{10,8},{12,... | collective-permute-start | bytes 147464 | tf_op jit(solution)/shard_map/ppermute | solution.py:19
  7.7 0.7 %copy-done.1 = s32[8,2]{0,1:T(2,128)S(1)} copy-done((s32[8,2]{0,1:T(2,128)S(1)}, s32[8,2]{0,1:T(2,128)}, u32[]{:S(2)}) %copy-start.1) | copy-done | bytes 88
  8.4 0.7 %copy-done.4 = s32[8,2]{0,1:T(2,128)S(1)} copy-done((s32[8,2]{0,1:T(2,128)S(1)}, s32[8,2]{0,1:T(2,128)}, u32[]{:S(2)}) %copy-start.4) | copy-done | bytes 88
  9.0 2.9 %first_weights.1 = (bf16[3072,512]{1,0:T(8,128)(2,1)S(1)}, bf16[3072,512]{1,0:T(8,128)(2,1)S(1)}, s32[8,128]{1,0:T(8,128)S(1)}) custom-call(s32[2,8]{1,0:T(2,128)S(1)} %bitcast.6, s32[2,8]{1,0:T(2,128)S(1)} %bitcast.9, bf16[6144,512]{1,0:T(8,128)(2,1)} %bitcast.10, bf16[6144,512]{1,0:T(8,128)(2,1)} %bitcast.12), custom_call_target="tpu_custom_call" | custom-call | flops 100000000 | bytes 1048576 | tf_op jit(solution)/shard_map/first_weights/pallas_call | solution.py:160
  11.9 0.0 collective-permute-done.refs_1_
  11.9 0.0 collective-permute-done.1.refs_2_
  11.9 0.0 collective-permute-done.2.refs_3_
  12.0 1.6 %collective-permute-start.3 = (bf16[32,3072]{1,0:T(8,128)(2,1)S(1)}, bf16[32,3072]{1,0:T(8,128)(2,1)S(1)}, u32[]{:S(2)}, u32[]{:S(2)}) collective-permute-start(bf16[32,3072]{1,0:T(8,128)(2,1)S(1)} %stack.1.refs_0_), channel_id=1, source_target_pairs={{0,1},{1,0},{2,3},{3,2},{4,5},{5,4},{6,7},{7,6},{8,9},{9,8},{10,11... | collective-permute-start | bytes 589832 | tf_op jit(solution)/shard_map/ppermute | solution.py:19
  13.5 5.8 %own_features.1 = (f32[32,512]{1,0:T(8,128)S(1)}, f32[32,512]{1,0:T(8,128)S(1)}, bf16[3072,512]{1,0:T(8,128)(2,1)S(1)}, bf16[3072,512]{1,0:T(8,128)(2,1)S(1)}, bf16[512,6144]{1,0:T(8,128)(2,1)S(1)}) custom-call(bf16[32,3072]{1,0:T(8,128)(2,1)S(1)} %stack.1.refs_0_, bf16[3072,512]{1,0:T(8,128)(2,1)S(1)} %get-tuple-element.21.refs_1_, ...), custom_call_target="tpu_custom_call" | custom-call | flops 201326592 | bytes 1048576 | tf_op jit(solution)/shard_map/own_features/pallas_call | solution.py:160
  19.3 0.0 collective-permute-done.3.refs_0_
  19.3 1.8 %hidden.1 = (bf16[32,512]{1,0:T(8,128)(2,1)S(1)}, bf16[32,3072]{1,0:T(8,128)(2,1)S(1)}) custom-call(bf16[32,3072]{1,0:T(8,128)(2,1)S(1)} %collective-permute-done.3.refs_0_, f32[32,512]{1,0:T(8,128)S(1)} %get-tuple-element.23.refs_1_, f32[32,512]{1,0:T(8,128)S(1)} %get-tuple-element.24.refs_2_, bf16[3072,512]{1,0:T(8,128)(2,1)S(1)} %get-tuple-element.25.refs_3_, ...), custom_call_target="tpu_custom_call" | custom-call | flops 301989888 | bytes 1048576 | tf_op jit(solution)/shard_map/hidden/pallas_call | solution.py:160
  21.1 0.0 copy-start.2
  21.1 0.0 copy-start.3
  21.1 0.6 %collective-permute-start.5 = (bf16[32,3072]{1,0:T(8,128)(2,1)S(1)}, bf16[32,3072]{1,0:T(8,128)(2,1)S(1)}, u32[]{:S(2)}, u32[]{:S(2)}) collective-permute-start(bf16[32,3072]{1,0:T(8,128)(2,1)S(1)} %get-tuple-element.30), channel_id=1, source_target_pairs={{0,1},{1,0},{2,3},{3,2},{4,5},{5,4},{6,7},{7,6},{8,9},{9,8},{10,11... | collective-permute-start | bytes 589832 | tf_op jit(solution)/shard_map/ppermute | solution.py:19
  21.7 0.0 collective-permute-start.4
  21.7 1.2 %collective-permute-done.4.swapped_ref = s32[8,128]{1,0:T(8,128)S(1)} collective-permute-done((s32[8,128]{1,0:T(8,128)S(1)}, s32[8,128]{1,0:T(8,128)S(1)}, u32[]{:S(2)}, u32[]{:S(2)}) %collective-permute-start.4) | collective-permute-done | bytes 4128 | tf_op jit(solution)/shard_map/ppermute | solution.py:23
  22.9 0.6 %own_down.1 = (f32[32,3072]{1,0:T(8,128)S(1)}, s32[8,128]{1,0:T(8,128)S(1)}) custom-call(bf16[32,512]{1,0:T(8,128)(2,1)S(1)} %get-tuple-element.28.hidden_ref, bf16[512,6144]{1,0:T(8,128)(2,1)S(1)} %get-tuple-element.27.refs_5_.down_ref, s32[8,128]{1,0:T(8,128)S(1)} %get-tuple-element.20.refs_4_.counts_ref, s32[8,128]{1,0:T(8,128)S(1)} %collective-permute-done.4.swapped_ref), custom_call_target="tpu_custom_call" | custom-call | flops 100663296 | bytes 1048576 | tf_op jit(solution)/shard_map/own_down/pallas_call | solution.py:160
  23.6 1.5 %collective-permute-start.6 = (s32[8,128]{1,0:T(8,128)S(1)}, s32[8,128]{1,0:T(8,128)S(1)}, u32[]{:S(2)}, u32[]{:S(2)}) collective-permute-start(s32[8,128]{1,0:T(8,128)S(1)} %get-tuple-element.31.refs_2_), channel_id=1, source_target_pairs={{0,16},{8,24},{16,0},{24,8},{1,17},{9,25},{17,1},{25,9},{2,18},{10... | collective-permute-start | bytes 12296 | tf_op jit(solution)/shard_map/ppermute | solution.py:23
  25.1 2.1 %collective-permute-done.6.refs_3_ = s32[8,128]{1,0:T(8,128)S(1)} collective-permute-done((s32[8,128]{1,0:T(8,128)S(1)}, s32[8,128]{1,0:T(8,128)S(1)}, u32[]{:S(2)}, u32[]{:S(2)}) %collective-permute-start.6) | collective-permute-done | bytes 4128 | tf_op jit(solution)/shard_map/ppermute | solution.py:23
  27.2 0.0 collective-permute-done.5.refs_1_
  27.2 1.9 %collective-permute-start.7 = (bf16[8,3200]{1,0:T(8,128)(2,1)S(1)}, bf16[8,3200]{1,0:T(8,128)(2,1)S(1)}, u32[]{:S(2)}, u32[]{:S(2)}) collective-permute-start(bf16[8,3200]{1,0:T(8,128)(2,1)S(1)} %get-tuple-element.33), channel_id=1, source_target_pairs={{0,6},{2,0},{4,2},{6,4},{1,7},{3,1},{5,3},{7,5},{8,14},{10,8},{12,... | collective-permute-start | bytes 153608 | tf_op jit(solution)/shard_map/ppermute | solution.py:19
  29.1 0.3 collective-permute-start.8
  29.4 0.3 collective-permute-start.9
  29.7 1.7 %collective-permute-done.7.refs_1_ = bf16[8,3200]{1,0:T(8,128)(2,1)S(1)} collective-permute-done((bf16[8,3200]{1,0:T(8,128)(2,1)S(1)}, bf16[8,3200]{1,0:T(8,128)(2,1)S(1)}, u32[]{:S(2)}, u32[]{:S(2)}) %collective-permute-start.7) | collective-permute-done | bytes 51232 | tf_op jit(solution)/shard_map/ppermute | solution.py:19
  31.4 2.9 %collective-permute-done.8.refs_2_ = bf16[8,3200]{1,0:T(8,128)(2,1)S(1)} collective-permute-done((bf16[8,3200]{1,0:T(8,128)(2,1)S(1)}, bf16[8,3200]{1,0:T(8,128)(2,1)S(1)}, u32[]{:S(2)}, u32[]{:S(2)}) %collective-permute-start.8) | collective-permute-done | bytes 51232 | tf_op jit(solution)/shard_map/ppermute | solution.py:19
  34.3 1.0 %collective-permute-done.9.refs_3_ = bf16[8,3200]{1,0:T(8,128)(2,1)S(1)} collective-permute-done((bf16[8,3200]{1,0:T(8,128)(2,1)S(1)}, bf16[8,3200]{1,0:T(8,128)(2,1)S(1)}, u32[]{:S(2)}, u32[]{:S(2)}) %collective-permute-start.9) | collective-permute-done | bytes 51232 | tf_op jit(solution)/shard_map/ppermute | solution.py:19
  35.3 0.0 copy-done.3
  35.3 0.8 %combine.1 = (bf16[8,3072]{1,0:T(8,128)(2,1)}, s32[8,128]{1,0:T(8,128)S(1)}) custom-call(s32[2,8]{1,0:T(2,128)S(1)} %bitcast.7, f32[2,8]{1,0:T(2,128)S(1)} %bitcast.8, bf16[8,3200]{1,0:T(8,128)(2,1)S(1)} %get-tuple-element.32.refs_0_, bf16[8,3200]{1,0:T(8,128)(2,1)S(1)} %collective-permute-done.7.refs_1_, ...), custom_call_target="tpu_custom_call" | custom-call | tf_op jit(solution)/shard_map/combine/pallas_call | solution.py:244
  36.1 0.1 slice.6
  36.2 0.6 %slice.8 = s32[4,4]{1,0:T(4,128)} slice(s32[256,4]{1,0:T(8,128)S(1)} %slice.6), slice={[0:4], [0:4]} | slice | bytes 128 | tf_op jit(solution)/shard_map/slice | solution.py:253
  (7 shorter events, 0.1 us)
Async XLA Ops:
  0.6 11.3 %collective-permute-start = (bf16[8,3072]{1,0:T(8,128)(2,1)}, bf16[8,3072]{1,0:T(8,128)(2,1)S(1)}, u32[]{:S(2)}, u32[]{:S(2)}) collective-permute-start(bf16[8,3072]{1,0:T(8,128)(2,1)} %refs_0_.1), channel_id=1, source_target_pairs={{0,2},{2,4},{4,6},{6,0},{1,3},{3,5},{5,7},{7,1},{8,10},{10,12},{12... | collective-permute-start | bytes 147464 | tf_op jit(solution)/shard_map/ppermute | solution.py:19
  3.7 8.2 %collective-permute-start.1 = (bf16[8,3072]{1,0:T(8,128)(2,1)}, bf16[8,3072]{1,0:T(8,128)(2,1)S(1)}, u32[]{:S(2)}, u32[]{:S(2)}) collective-permute-start(bf16[8,3072]{1,0:T(8,128)(2,1)} %refs_0_.1), channel_id=1, source_target_pairs={{0,4},{2,6},{4,0},{6,2},{1,5},{3,7},{5,1},{7,3},{8,12},{10,14},{12... | collective-permute-start | bytes 147464 | tf_op jit(solution)/shard_map/ppermute | solution.py:19
  6.3 5.6 %collective-permute-start.2 = (bf16[8,3072]{1,0:T(8,128)(2,1)}, bf16[8,3072]{1,0:T(8,128)(2,1)S(1)}, u32[]{:S(2)}, u32[]{:S(2)}) collective-permute-start(bf16[8,3072]{1,0:T(8,128)(2,1)} %refs_0_.1), channel_id=1, source_target_pairs={{0,6},{2,0},{4,2},{6,4},{1,7},{3,1},{5,3},{7,5},{8,14},{10,8},{12,... | collective-permute-start | bytes 147464 | tf_op jit(solution)/shard_map/ppermute | solution.py:19
  7.7 0.7 %copy-start.1 = (s32[8,2]{0,1:T(2,128)S(1)}, s32[8,2]{0,1:T(2,128)}, u32[]{:S(2)}) copy-start(s32[8,2]{0,1:T(2,128)} %param.8) | copy-start | bytes 196
  8.4 0.7 %copy-start.4 = (s32[8,2]{0,1:T(2,128)S(1)}, s32[8,2]{0,1:T(2,128)}, u32[]{:S(2)}) copy-start(s32[8,2]{0,1:T(2,128)} %param.9) | copy-start | bytes 196
  9.0 2.9 %copy-start = (bf16[8,3072]{1,0:T(8,128)(2,1)S(1)}, bf16[8,3072]{1,0:T(8,128)(2,1)}, u32[]{:S(2)}) copy-start(bf16[8,3072]{1,0:T(8,128)(2,1)} %refs_0_.1) | copy-start | bytes 147460
  12.0 7.3 %collective-permute-start.3 = (bf16[32,3072]{1,0:T(8,128)(2,1)S(1)}, bf16[32,3072]{1,0:T(8,128)(2,1)S(1)}, u32[]{:S(2)}, u32[]{:S(2)}) collective-permute-start(bf16[32,3072]{1,0:T(8,128)(2,1)S(1)} %stack.1.refs_0_), channel_id=1, source_target_pairs={{0,1},{1,0},{2,3},{3,2},{4,5},{5,4},{6,7},{7,6},{8,9},{9,8},{10,11... | collective-permute-start | bytes 589832 | tf_op jit(solution)/shard_map/ppermute | solution.py:19
  21.1 14.2 %copy-start.2 = (s32[8,2]{0,1:T(2,128)S(1)}, s32[8,2]{0,1:T(2,128)}, u32[]{:S(2)}) copy-start(s32[8,2]{0,1:T(2,128)} %param.8) | copy-start | bytes 196
  21.1 14.2 %copy-start.3 = (f32[8,2]{0,1:T(2,128)S(1)}, f32[8,2]{0,1:T(2,128)}, u32[]{:S(2)}) copy-start(f32[8,2]{0,1:T(2,128)} %param.10) | copy-start | bytes 196
  21.1 6.0 %collective-permute-start.5 = (bf16[32,3072]{1,0:T(8,128)(2,1)S(1)}, bf16[32,3072]{1,0:T(8,128)(2,1)S(1)}, u32[]{:S(2)}, u32[]{:S(2)}) collective-permute-start(bf16[32,3072]{1,0:T(8,128)(2,1)S(1)} %get-tuple-element.30), channel_id=1, source_target_pairs={{0,1},{1,0},{2,3},{3,2},{4,5},{5,4},{6,7},{7,6},{8,9},{9,8},{10,11... | collective-permute-start | bytes 589832 | tf_op jit(solution)/shard_map/ppermute | solution.py:19
  21.7 1.2 %collective-permute-start.4 = (s32[8,128]{1,0:T(8,128)S(1)}, s32[8,128]{1,0:T(8,128)S(1)}, u32[]{:S(2)}, u32[]{:S(2)}) collective-permute-start(s32[8,128]{1,0:T(8,128)S(1)} %get-tuple-element.20.refs_4_.counts_ref), channel_id=1, source_target_pairs={{0,8},{8,0},{16,24},{24,16},{1,9},{9,1},{17,25},{25,17},{2,10},{10... | collective-permute-start | bytes 12296 | tf_op jit(solution)/shard_map/ppermute | solution.py:23
  23.6 3.6 %collective-permute-start.6 = (s32[8,128]{1,0:T(8,128)S(1)}, s32[8,128]{1,0:T(8,128)S(1)}, u32[]{:S(2)}, u32[]{:S(2)}) collective-permute-start(s32[8,128]{1,0:T(8,128)S(1)} %get-tuple-element.31.refs_2_), channel_id=1, source_target_pairs={{0,16},{8,24},{16,0},{24,8},{1,17},{9,25},{17,1},{25,9},{2,18},{10... | collective-permute-start | bytes 12296 | tf_op jit(solution)/shard_map/ppermute | solution.py:23
  27.2 4.2 %collective-permute-start.7 = (bf16[8,3200]{1,0:T(8,128)(2,1)S(1)}, bf16[8,3200]{1,0:T(8,128)(2,1)S(1)}, u32[]{:S(2)}, u32[]{:S(2)}) collective-permute-start(bf16[8,3200]{1,0:T(8,128)(2,1)S(1)} %get-tuple-element.33), channel_id=1, source_target_pairs={{0,6},{2,0},{4,2},{6,4},{1,7},{3,1},{5,3},{7,5},{8,14},{10,8},{12,... | collective-permute-start | bytes 153608 | tf_op jit(solution)/shard_map/ppermute | solution.py:19
  29.1 5.2 %collective-permute-start.8 = (bf16[8,3200]{1,0:T(8,128)(2,1)S(1)}, bf16[8,3200]{1,0:T(8,128)(2,1)S(1)}, u32[]{:S(2)}, u32[]{:S(2)}) collective-permute-start(bf16[8,3200]{1,0:T(8,128)(2,1)S(1)} %get-tuple-element.34), channel_id=1, source_target_pairs={{0,4},{2,6},{4,0},{6,2},{1,5},{3,7},{5,1},{7,3},{8,12},{10,14},{12... | collective-permute-start | bytes 153608 | tf_op jit(solution)/shard_map/ppermute | solution.py:19
  29.4 5.9 %collective-permute-start.9 = (bf16[8,3200]{1,0:T(8,128)(2,1)S(1)}, bf16[8,3200]{1,0:T(8,128)(2,1)S(1)}, u32[]{:S(2)}, u32[]{:S(2)}) collective-permute-start(bf16[8,3200]{1,0:T(8,128)(2,1)S(1)} %get-tuple-element.35), channel_id=1, source_target_pairs={{0,2},{2,4},{4,6},{6,0},{1,3},{3,5},{5,7},{7,1},{8,10},{10,12},{12... | collective-permute-start | bytes 153608 | tf_op jit(solution)/shard_map/ppermute | solution.py:19

commit v3 on v2

v3 whole, which is shorter than its diff:
```python
import functools

import jax
import jax.numpy as jnp
from jax import lax
from jax.experimental import pallas as pl
from jax.experimental.pallas import tpu as pltpu
from jax.sharding import PartitionSpec as P

REPL = 4
LANES = 128
MIB = 1 << 20

route_scale = 2.5


def shift(array, axis, count, step):
    return lax.ppermute(array, axis, [(i, (i + step) % count) for i in range(count)])


def swap(array, axis, count, span):
    return lax.ppermute(array, axis, [(i, i ^ span) for i in range(count)])


def window(index, size):
    return pl.ds(pl.multiple_of(index * size, size), size)


def intake_kernel(ep_count, rep_count, tokens_hbm, ids_hbm, picks_hbm, *refs):
    tokens_out, counts_ref, ids_ref, picks_ref, sems = refs
    pairs = [(ids_hbm, ids_ref), (picks_hbm, picks_ref), (tokens_hbm, tokens_out)]
    copies = [
        pltpu.make_async_copy(source, held, sems.at[i]) for i, (source, held) in enumerate(pairs)
    ]
    for copy in copies:
        copy.start()
    for copy in copies:
        copy.wait()
    group = lax.rem(lax.axis_index("rep") + picks_ref[...] * (rep_count // REPL), rep_count)
    ids = ids_ref[...]
    rows, lanes = counts_ref.shape
    lane = (group // rows) * LANES + ids
    row = lax.rem(group, rows)
    cells = row * lanes + lane
    position = lax.broadcasted_iota(jnp.int32, (rows, lanes), 0) * lanes
    position = position + lax.broadcasted_iota(jnp.int32, (rows, lanes), 1)
    total = jnp.zeros((rows, lanes), jnp.int32)
    for k in range(cells.shape[0]):
        for t in range(cells.shape[1]):
            total += (position == cells[k : k + 1, t : t + 1]).astype(jnp.int32)
    counts_ref[...] = total


def stack_kernel(*refs):
    pieces, out_ref = refs[:-1], refs[-1]
    for s, piece in enumerate(pieces):
        out_ref[pl.ds(s * piece.shape[0], piece.shape[0]), :] = piece[...]


def own_kernel(x_ref, gate_ref, up_ref, gate_acc, up_acc):
    rows = window(lax.axis_index("tp"), x_ref.shape[1])
    x = x_ref[...]
    gate_acc[...] = jnp.dot(x, gate_ref[rows, :], preferred_element_type=jnp.float32)
    up_acc[...] = jnp.dot(x, up_ref[rows, :], preferred_element_type=jnp.float32)


def hidden_kernel(tp_count, *refs):
    others = refs[: tp_count - 1]
    gate_acc, up_acc, gate_ref, up_ref, down_ref = refs[tp_count - 1 : tp_count + 4]
    hidden_out = refs[tp_count + 4]
    partial_outs = refs[tp_count + 5 :]
    me = lax.axis_index("tp")
    gate = gate_acc[...]
    up = up_acc[...]
    for step, other in enumerate(others, 1):
        rows = window(lax.rem(me - step + tp_count, tp_count), other.shape[1])
        x = other[...]
        gate += jnp.dot(x, gate_ref[rows, :], preferred_element_type=jnp.float32)
        up += jnp.dot(x, up_ref[rows, :], preferred_element_type=jnp.float32)
    hidden = (gate / (1.0 + jnp.exp(-gate)) * up).astype(jnp.bfloat16)
    hidden_out[...] = hidden
    for step, out in enumerate(partial_outs, 1):
        columns = window(lax.rem(me + step, tp_count), out.shape[1])
        out[...] = jnp.dot(
            hidden, down_ref[:, columns], preferred_element_type=jnp.float32
        ).astype(jnp.bfloat16)


def down_kernel(hidden_ref, down_ref, counts_ref, swapped_ref, out_ref, sum_ref):
    sum_ref[...] = counts_ref[...] + swapped_ref[...]
    columns = window(lax.axis_index("tp"), out_ref.shape[1])
    out_ref[...] = jnp.dot(
        hidden_ref[...], down_ref[:, columns], preferred_element_type=jnp.float32
    )


def pack_kernel(arrived_count, *refs):
    mine_ref = refs[0]
    arrived = refs[1 : 1 + arrived_count]
    counts = refs[1 + arrived_count : 3 + arrived_count]
    outs = refs[3 + arrived_count :]
    tok_rows, part = outs[0].shape[0], mine_ref.shape[1]
    carried = (counts[0][...] + counts[1][...]).astype(jnp.float32).astype(jnp.bfloat16)
    for s, out in enumerate(outs):
        rows = pl.ds(s * tok_rows, tok_rows)
        total = mine_ref[rows, :]
        for piece in arrived:
            total += piece[rows, :].astype(jnp.float32)
        out[:, :part] = total.astype(jnp.bfloat16)
        out[:, part:] = carried


def combine_kernel(ep_count, ids_ref, scores_ref, *refs):
    pieces, (out_ref, counts_ref) = refs[:-2], refs[-2:]
    tok_rows, part = out_ref.shape
    me = lax.axis_index("ep")
    gains = jax.nn.sigmoid(scores_ref[...])
    weights = gains / jnp.sum(gains, 0, keepdims=True) * route_scale
    ids = ids_ref[...]
    total = jnp.zeros((tok_rows, part), jnp.float32)
    counts = jnp.zeros((tok_rows, pieces[0].shape[1] - part), jnp.float32)
    diagonal = lax.broadcasted_iota(jnp.int32, (tok_rows, tok_rows), 0) == (
        lax.broadcasted_iota(jnp.int32, (tok_rows, tok_rows), 1)
    )
    for s, piece in enumerate(pieces):
        expert = lax.rem(me + s, ep_count)
        row = jnp.sum(jnp.where(ids == expert, weights, 0.0), 0, keepdims=True)
        column = jnp.sum(jnp.where(diagonal, row, 0.0), 1, keepdims=True)
        total += column * piece[:, :part].astype(jnp.float32)
        counts += piece[:, part:].astype(jnp.float32)
    out_ref[...] = total.astype(jnp.bfloat16)
    for group in range(0, counts_ref.shape[0], tok_rows):
        size = min(tok_rows, counts_ref.shape[0] - group)
        start = group // tok_rows * LANES
        counts_ref[pl.ds(group, size), :] = counts[:size, start : start + ep_count].astype(jnp.int32)


def vmem_call(kernel, name, outs, args, flops, remote=0, scratch=()):
    specs = [pl.BlockSpec(memory_space=pltpu.VMEM)] * (len(args) - remote)
    return pl.pallas_call(
        kernel,
        out_shape=[pltpu.VMEM(shape, dtype) for shape, dtype in outs],
        in_specs=specs + [pl.BlockSpec(memory_space=pltpu.HBM)] * remote,
        out_specs=[pl.BlockSpec(memory_space=pltpu.VMEM)] * len(outs),
        scratch_shapes=list(scratch),
        compiler_params=pltpu.CompilerParams(vmem_limit_bytes=24 * MIB),
        cost_estimate=pl.CostEstimate(flops=flops, bytes_accessed=MIB, transcendentals=0),
        name=name,
    )(*args)


def per_device(tokens, expert_ids, replicas, scores, w_gate, w_up, w_down):
    rep_count = lax.axis_size("rep")
    ep_count = lax.axis_size("ep")
    tp_count = lax.axis_size("tp")
    tok_rows, part = tokens.shape
    ffe = w_gate.shape[2]
    rows = ep_count * tok_rows
    bf16, f32, i32 = jnp.bfloat16, jnp.float32, jnp.int32
    gate_w, up_w, down_w = w_gate[0], w_up[0], w_down[0]
    ids, picks, gains = expert_ids.T, replicas.T, scores.T

    width = -(-rep_count // tok_rows) * LANES
    table = ((tok_rows, width), i32)
    tokens, counts = vmem_call(
        functools.partial(intake_kernel, ep_count, rep_count),
        "intake",
        [((tok_rows, part), bf16), table],
        tuple(pltpu.with_memory_space_constraint(a, pltpu.HBM) for a in (tokens, ids, picks)),
        10**11,
        remote=3,
        scratch=[pltpu.VMEM(ids.shape, i32)] * 2 + [pltpu.SemaphoreType.DMA((3,))],
    )

    blocks = [tokens] + [shift(tokens, "ep", ep_count, s) for s in range(1, ep_count)]
    (own,) = vmem_call(stack_kernel, "stack", [((rows, part), bf16)], tuple(blocks), 1000)
    others = [shift(own, "tp", tp_count, s) for s in range(1, tp_count)]
    spans = [1 << bit for bit in range(rep_count.bit_length() - 1)]
    for span in spans[:-1]:
        swapped = swap(counts, "rep", rep_count, span)
        if span != spans[-2]:
            counts = counts + swapped
    dot_flops = 2 * rows * part * ffe
    gate_acc, up_acc = vmem_call(
        own_kernel,
        "own_features",
        [((rows, ffe), f32)] * 2,
        (own, gate_w, up_w),
        2 * dot_flops,
    )
    hidden, *partials = vmem_call(
        functools.partial(hidden_kernel, tp_count),
        "hidden",
        [((rows, ffe), bf16)] + [((rows, part), bf16)] * (tp_count - 1),
        (*others, gate_acc, up_acc, gate_w, up_w, down_w),
        3 * (tp_count - 1) * dot_flops,
    )
    arrived = [shift(p, "tp", tp_count, s) for s, p in enumerate(partials, 1)]
    mine, counts = vmem_call(
        down_kernel,
        "own_down",
        [((rows, part), f32), table],
        (hidden, down_w, counts, swapped),
        dot_flops,
    )
    swapped = swap(counts, "rep", rep_count, spans[-1])

    outgoing = vmem_call(
        functools.partial(pack_kernel, tp_count - 1),
        "pack",
        [((tok_rows, part + width), bf16)] * ep_count,
        (mine, *arrived, counts, swapped),
        rows * part,
    )
    back = [outgoing[0]] + [
        shift(outgoing[s], "ep", ep_count, -s) for s in range(1, ep_count)
    ]
    return pl.pallas_call(
        functools.partial(combine_kernel, ep_count),
        out_shape=[
            jax.ShapeDtypeStruct((tok_rows, part), bf16),
            jax.ShapeDtypeStruct((rep_count, ep_count), i32),
        ],
        compiler_params=pltpu.CompilerParams(vmem_limit_bytes=8 * MIB),
        name="combine",
    )(ids, gains, *back)


def solution(mesh):
    placed = (
        P(("rep", "ep"), "tp"),
        P(("rep", "ep"), None),
        P(("rep", "ep"), None),
        P(("rep", "ep"), None),
        P("ep", None, "tp"),
        P("ep", None, "tp"),
        P("ep", "tp", None),
    )
    return jax.shard_map(
        per_device,
        mesh=mesh,
        in_specs=placed,
        out_specs=(P(("rep", "ep"), "tp"), P()),
        check_vma=False,
    )
```

time: 37 us -> 35.9 us (0.970)
  Pallas kernels: 11.9 us -> 5.56 us
  waiting for transfers between devices: 8.87 us -> 15.1 us
  local copies, waits for them, and re-layouts: 2.08 us -> 0.02 us
  starting transfers between devices: 13.2 us -> 14.4 us
    pallas_call x6, Pallas kernels: 11.1 us -> 4.8 us  [vmem_call(): pl.pallas_call(kernel, out_shape=[pltpu.VMEM(shape, dtype) for shape, dty...]
    ppermute x8, waiting for transfers between devices: 5.62 us -> 11.8 us  [shift(): lax.ppermute(array, axis, [(i, (i + step) % count) for i in range(count)])]
    unnamed x10, local copies, waits for them, and re-layouts: 1.37 us -> 0.02 us
    ppermute x8, starting transfers between devices: 11.7 us -> 12.9 us  [shift(): lax.ppermute(array, axis, [(i, (i + step) % count) for i in range(count)])]
    slice x2 -> x0, local copies, waits for them, and re-layouts: 0.71 us -> none  [per_device(): load_counts = totals.reshape(-1)[:cell_count].reshape(rep_count, ep_count)]
  transfers between devices with their start and end apart: 10 -> 10, of which waited for: 5 -> 9; matrix products, arithmetic and copies ran while one was open for 0% -> 0% of each run, Pallas kernels for 25% -> 5%
where the time goes in v3:
time: 35.9 us; the launch traced here: 35.8 us
  waiting for transfers between devices  15.1 us (42%)
  starting transfers between devices  14.4 us (40%)
  Pallas kernels  5.56 us (15%)
  between operations  0.69 us (2%)
    ppermute x8, starting transfers between devices, shift(): lax.ppermute(array, axis, [(i, (i + step) % count) for i in range(count)])  12.9 us
    ppermute x8, waiting for transfers between devices, shift(): lax.ppermute(array, axis, [(i, (i + step) % count) for i in range(count)])  11.8 us
    pallas_call x6, Pallas kernels, vmem_call(): pl.pallas_call(kernel, out_shape=[pltpu.VMEM(shape, dtype) for shape, dty...  4.8 us
    ppermute x2, waiting for transfers between devices, swap(): return lax.ppermute(array, axis, [(i, i ^ span) for i in range(count)])  3.25 us
    ppermute x2, starting transfers between devices, swap(): return lax.ppermute(array, axis, [(i, i ^ span) for i in range(count)])  1.54 us
    pallas_call x1, Pallas kernels, per_device(): pl.pallas_call(functools.partial(combine_kernel, ep_count), out_shape=[ja...  0.77 us
  transfers between devices with their start and end apart: 10, of which 9 were waited for; matrix products, arithmetic and copies ran while one was open for 0% of the time, Pallas kernels for 5%

profile of v3, /device:TPU:0, one launch (start us, length us, event | category | flops | bytes accessed | tf_op | source)
XLA Modules:
  0.0 35.8 jit_solution(4433662987059225565)
XLA Ops:
  0.6 0.0 copy-start
  0.6 0.0 copy-start.1
  0.7 1.1 %intake.1 = (bf16[8,3072]{1,0:T(8,128)(2,1)S(1)}, s32[8,128]{1,0:T(8,128)S(1)}) custom-call(bf16[8,3072]{1,0:T(8,128)(2,1)} %tokens_hbm.1, s32[2,8]{1,0:T(2,128)} %bitcast.12, s32[2,8]{1,0:T(2,128)} %bitcast.15), custom_call_target="tpu_custom_call" | custom-call | flops 99999997952 | bytes 1048576 | tf_op jit(solution)/shard_map/intake/pallas_call | solution.py:140
  1.8 5.1 %collective-permute-start.2 = (bf16[8,3072]{1,0:T(8,128)(2,1)S(1)}, bf16[8,3072]{1,0:T(8,128)(2,1)S(1)}, u32[]{:S(2)}, u32[]{:S(2)}) collective-permute-start(bf16[8,3072]{1,0:T(8,128)(2,1)S(1)} %get-tuple-element.14.refs_0_), channel_id=1, source_target_pairs={{0,6},{2,0},{4,2},{6,4},{1,7},{3,1},{5,3},{7,5},{8,14},{10,8},{12,... | collective-permute-start | bytes 147464 | tf_op jit(solution)/shard_map/ppermute | solution.py:18
  6.9 0.0 collective-permute-start.1
  6.9 1.0 %collective-permute-start = (bf16[8,3072]{1,0:T(8,128)(2,1)S(1)}, bf16[8,3072]{1,0:T(8,128)(2,1)S(1)}, u32[]{:S(2)}, u32[]{:S(2)}) collective-permute-start(bf16[8,3072]{1,0:T(8,128)(2,1)S(1)} %get-tuple-element.14.refs_0_), channel_id=1, source_target_pairs={{0,2},{2,4},{4,6},{6,0},{1,3},{3,5},{5,7},{7,1},{8,10},{10,12},{12... | collective-permute-start | bytes 147464 | tf_op jit(solution)/shard_map/ppermute | solution.py:18
  8.0 1.0 %collective-permute-done.2.refs_3_ = bf16[8,3072]{1,0:T(8,128)(2,1)S(1)} collective-permute-done((bf16[8,3072]{1,0:T(8,128)(2,1)S(1)}, bf16[8,3072]{1,0:T(8,128)(2,1)S(1)}, u32[]{:S(2)}, u32[]{:S(2)}) %collective-permute-start.2) | collective-permute-done | bytes 49184 | tf_op jit(solution)/shard_map/ppermute | solution.py:18
  9.0 2.9 %collective-permute-done.1.refs_2_ = bf16[8,3072]{1,0:T(8,128)(2,1)S(1)} collective-permute-done((bf16[8,3072]{1,0:T(8,128)(2,1)S(1)}, bf16[8,3072]{1,0:T(8,128)(2,1)S(1)}, u32[]{:S(2)}, u32[]{:S(2)}) %collective-permute-start.1) | collective-permute-done | bytes 49184 | tf_op jit(solution)/shard_map/ppermute | solution.py:18
  11.9 0.9 %collective-permute-done.refs_1_ = bf16[8,3072]{1,0:T(8,128)(2,1)S(1)} collective-permute-done((bf16[8,3072]{1,0:T(8,128)(2,1)S(1)}, bf16[8,3072]{1,0:T(8,128)(2,1)S(1)}, u32[]{:S(2)}, u32[]{:S(2)}) %collective-permute-start) | collective-permute-done | bytes 49184 | tf_op jit(solution)/shard_map/ppermute | solution.py:18
  12.8 1.6 %collective-permute-start.3 = (bf16[32,3072]{1,0:T(8,128)(2,1)S(1)}, bf16[32,3072]{1,0:T(8,128)(2,1)S(1)}, u32[]{:S(2)}, u32[]{:S(2)}) collective-permute-start(bf16[32,3072]{1,0:T(8,128)(2,1)S(1)} %stack.1.x_ref), channel_id=1, source_target_pairs={{0,1},{1,0},{2,3},{3,2},{4,5},{5,4},{6,7},{7,6},{8,9},{9,8},{10,11... | collective-permute-start | bytes 589832 | tf_op jit(solution)/shard_map/ppermute | solution.py:18
  14.4 0.0 copy-done
  14.4 0.0 copy-done.1
  14.4 1.2 %own_features.1 = (f32[32,512]{1,0:T(8,128)S(1)}, f32[32,512]{1,0:T(8,128)S(1)}) custom-call(bf16[32,3072]{1,0:T(8,128)(2,1)S(1)} %stack.1.x_ref, bf16[6144,512]{1,0:T(8,128)(2,1)S(1)} %bitcast.6, bf16[6144,512]{1,0:T(8,128)(2,1)S(1)} %bitcast.8), custom_call_target="tpu_custom_call" | custom-call | flops 201326592 | bytes 1048576 | tf_op jit(solution)/shard_map/own_features/pallas_call | solution.py:140
  15.6 3.0 %collective-permute-done.3.refs_0_ = bf16[32,3072]{1,0:T(8,128)(2,1)S(1)} collective-permute-done((bf16[32,3072]{1,0:T(8,128)(2,1)S(1)}, bf16[32,3072]{1,0:T(8,128)(2,1)S(1)}, u32[]{:S(2)}, u32[]{:S(2)}) %collective-permute-start.3) | collective-permute-done | bytes 196640 | tf_op jit(solution)/shard_map/ppermute | solution.py:18
  18.6 0.0 copy-done.2
  18.6 1.8 %hidden.1 = (bf16[32,512]{1,0:T(8,128)(2,1)S(1)}, bf16[32,3072]{1,0:T(8,128)(2,1)S(1)}) custom-call(bf16[32,3072]{1,0:T(8,128)(2,1)S(1)} %collective-permute-done.3.refs_0_, f32[32,512]{1,0:T(8,128)S(1)} %get-tuple-element.15.refs_1_, f32[32,512]{1,0:T(8,128)S(1)} %get-tuple-element.16.refs_2_, bf16[6144,512]{1,0:T(8,128)(2,1)S(1)} %bitcast.7, ...), custom_call_target="tpu_custom_call" | custom-call | flops 301989888 | bytes 1048576 | tf_op jit(solution)/shard_map/hidden/pallas_call | solution.py:140
  20.4 0.0 copy-start.3
  20.4 0.0 copy-start.4
  20.4 1.6 %collective-permute-start.5 = (bf16[32,3072]{1,0:T(8,128)(2,1)S(1)}, bf16[32,3072]{1,0:T(8,128)(2,1)S(1)}, u32[]{:S(2)}, u32[]{:S(2)}) collective-permute-start(bf16[32,3072]{1,0:T(8,128)(2,1)S(1)} %get-tuple-element.20), channel_id=1, source_target_pairs={{0,1},{1,0},{2,3},{3,2},{4,5},{5,4},{6,7},{7,6},{8,9},{9,8},{10,11... | collective-permute-start | bytes 589832 | tf_op jit(solution)/shard_map/ppermute | solution.py:18
  21.9 0.0 collective-permute-start.4
  22.0 1.2 %collective-permute-done.4.swapped_ref = s32[8,128]{1,0:T(8,128)S(1)} collective-permute-done((s32[8,128]{1,0:T(8,128)S(1)}, s32[8,128]{1,0:T(8,128)S(1)}, u32[]{:S(2)}, u32[]{:S(2)}) %collective-permute-start.4) | collective-permute-done | bytes 4128 | tf_op jit(solution)/shard_map/ppermute | solution.py:22
  23.1 0.6 %own_down.1 = (f32[32,3072]{1,0:T(8,128)S(1)}, s32[8,128]{1,0:T(8,128)S(1)}) custom-call(bf16[32,512]{1,0:T(8,128)(2,1)S(1)} %get-tuple-element.17.hidden_ref, bf16[512,6144]{1,0:T(8,128)(2,1)S(1)} %bitcast.11, s32[8,128]{1,0:T(8,128)S(1)} %get-tuple-element.18.counts_ref, s32[8,128]{1,0:T(8,128)S(1)} %collective-permute-done.4.swapped_ref), custom_call_target="tpu_custom_call" | custom-call | flops 100663296 | bytes 1048576 | tf_op jit(solution)/shard_map/own_down/pallas_call | solution.py:140
  23.8 1.5 %collective-permute-start.6 = (s32[8,128]{1,0:T(8,128)S(1)}, s32[8,128]{1,0:T(8,128)S(1)}, u32[]{:S(2)}, u32[]{:S(2)}) collective-permute-start(s32[8,128]{1,0:T(8,128)S(1)} %get-tuple-element.21.refs_2_), channel_id=1, source_target_pairs={{0,16},{8,24},{16,0},{24,8},{1,17},{9,25},{17,1},{25,9},{2,18},{10... | collective-permute-start | bytes 12296 | tf_op jit(solution)/shard_map/ppermute | solution.py:22
  25.3 2.1 %collective-permute-done.6.refs_3_ = s32[8,128]{1,0:T(8,128)S(1)} collective-permute-done((s32[8,128]{1,0:T(8,128)S(1)}, s32[8,128]{1,0:T(8,128)S(1)}, u32[]{:S(2)}, u32[]{:S(2)}) %collective-permute-start.6) | collective-permute-done | bytes 4128 | tf_op jit(solution)/shard_map/ppermute | solution.py:22
  27.4 0.0 collective-permute-done.5.refs_1_
  27.4 1.3 %collective-permute-start.7 = (bf16[8,3200]{1,0:T(8,128)(2,1)S(1)}, bf16[8,3200]{1,0:T(8,128)(2,1)S(1)}, u32[]{:S(2)}, u32[]{:S(2)}) collective-permute-start(bf16[8,3200]{1,0:T(8,128)(2,1)S(1)} %get-tuple-element.23), channel_id=1, source_target_pairs={{0,6},{2,0},{4,2},{6,4},{1,7},{3,1},{5,3},{7,5},{8,14},{10,8},{12,... | collective-permute-start | bytes 153608 | tf_op jit(solution)/shard_map/ppermute | solution.py:18
  28.7 0.4 %collective-permute-start.8 = (bf16[8,3200]{1,0:T(8,128)(2,1)S(1)}, bf16[8,3200]{1,0:T(8,128)(2,1)S(1)}, u32[]{:S(2)}, u32[]{:S(2)}) collective-permute-start(bf16[8,3200]{1,0:T(8,128)(2,1)S(1)} %get-tuple-element.24), channel_id=1, source_target_pairs={{0,4},{2,6},{4,0},{6,2},{1,5},{3,7},{5,1},{7,3},{8,12},{10,14},{12... | collective-permute-start | bytes 153608 | tf_op jit(solution)/shard_map/ppermute | solution.py:18
  29.1 1.9 %collective-permute-start.9 = (bf16[8,3200]{1,0:T(8,128)(2,1)S(1)}, bf16[8,3200]{1,0:T(8,128)(2,1)S(1)}, u32[]{:S(2)}, u32[]{:S(2)}) collective-permute-start(bf16[8,3200]{1,0:T(8,128)(2,1)S(1)} %get-tuple-element.25), channel_id=1, source_target_pairs={{0,2},{2,4},{4,6},{6,0},{1,3},{3,5},{5,7},{7,1},{8,10},{10,12},{12... | collective-permute-start | bytes 153608 | tf_op jit(solution)/shard_map/ppermute | solution.py:18
  31.1 0.6 %collective-permute-done.7.refs_1_ = bf16[8,3200]{1,0:T(8,128)(2,1)S(1)} collective-permute-done((bf16[8,3200]{1,0:T(8,128)(2,1)S(1)}, bf16[8,3200]{1,0:T(8,128)(2,1)S(1)}, u32[]{:S(2)}, u32[]{:S(2)}) %collective-permute-start.7) | collective-permute-done | bytes 51232 | tf_op jit(solution)/shard_map/ppermute | solution.py:18
  31.7 2.6 %collective-permute-done.8.refs_2_ = bf16[8,3200]{1,0:T(8,128)(2,1)S(1)} collective-permute-done((bf16[8,3200]{1,0:T(8,128)(2,1)S(1)}, bf16[8,3200]{1,0:T(8,128)(2,1)S(1)}, u32[]{:S(2)}, u32[]{:S(2)}) %collective-permute-start.8) | collective-permute-done | bytes 51232 | tf_op jit(solution)/shard_map/ppermute | solution.py:18
  34.3 0.7 %collective-permute-done.9.refs_3_ = bf16[8,3200]{1,0:T(8,128)(2,1)S(1)} collective-permute-done((bf16[8,3200]{1,0:T(8,128)(2,1)S(1)}, bf16[8,3200]{1,0:T(8,128)(2,1)S(1)}, u32[]{:S(2)}, u32[]{:S(2)}) %collective-permute-start.9) | collective-permute-done | bytes 51232 | tf_op jit(solution)/shard_map/ppermute | solution.py:18
  35.0 0.8 %combine.1 = (bf16[8,3072]{1,0:T(8,128)(2,1)}, s32[4,4]{1,0:T(4,128)}) custom-call(s32[2,8]{1,0:T(2,128)S(1)} %bitcast.13, f32[2,8]{1,0:T(2,128)S(1)} %bitcast.14, bf16[8,3200]{1,0:T(8,128)(2,1)S(1)} %get-tuple-element.22.refs_0_, bf16[8,3200]{1,0:T(8,128)(2,1)S(1)} %collective-permute-done.7.refs_1_, bf16[8,3200]{1,0:T(8,128)(2,1)S(1)} %collective-permute-done.8.refs_2_, ...), custom_call_target="tpu_custom_call" | custom-call | tf_op jit(solution)/shard_map/combine/pallas_call | solution.py:218
  (5 shorter events, 0.1 us)
Async XLA Ops:
  0.6 13.8 %copy-start = (bf16[1,6144,512]{2,1,0:T(8,128)(2,1)S(1)}, bf16[1,6144,512]{2,1,0:T(8,128)(2,1)}, u32[]{:S(2)}) copy-start(bf16[1,6144,512]{2,1,0:T(8,128)(2,1)} %param.11) | copy-start | bytes 18874372
  0.6 13.8 %copy-start.1 = (bf16[1,6144,512]{2,1,0:T(8,128)(2,1)S(1)}, bf16[1,6144,512]{2,1,0:T(8,128)(2,1)}, u32[]{:S(2)}) copy-start(bf16[1,6144,512]{2,1,0:T(8,128)(2,1)} %param.12) | copy-start | bytes 18874372
  1.8 7.2 %collective-permute-start.2 = (bf16[8,3072]{1,0:T(8,128)(2,1)S(1)}, bf16[8,3072]{1,0:T(8,128)(2,1)S(1)}, u32[]{:S(2)}, u32[]{:S(2)}) collective-permute-start(bf16[8,3072]{1,0:T(8,128)(2,1)S(1)} %get-tuple-element.14.refs_0_), channel_id=1, source_target_pairs={{0,6},{2,0},{4,2},{6,4},{1,7},{3,1},{5,3},{7,5},{8,14},{10,8},{12,... | collective-permute-start | bytes 147464 | tf_op jit(solution)/shard_map/ppermute | solution.py:18
  6.9 5.0 %collective-permute-start.1 = (bf16[8,3072]{1,0:T(8,128)(2,1)S(1)}, bf16[8,3072]{1,0:T(8,128)(2,1)S(1)}, u32[]{:S(2)}, u32[]{:S(2)}) collective-permute-start(bf16[8,3072]{1,0:T(8,128)(2,1)S(1)} %get-tuple-element.14.refs_0_), channel_id=1, source_target_pairs={{0,4},{2,6},{4,0},{6,2},{1,5},{3,7},{5,1},{7,3},{8,12},{10,14},{12... | collective-permute-start | bytes 147464 | tf_op jit(solution)/shard_map/ppermute | solution.py:18
  6.9 5.9 %collective-permute-start = (bf16[8,3072]{1,0:T(8,128)(2,1)S(1)}, bf16[8,3072]{1,0:T(8,128)(2,1)S(1)}, u32[]{:S(2)}, u32[]{:S(2)}) collective-permute-start(bf16[8,3072]{1,0:T(8,128)(2,1)S(1)} %get-tuple-element.14.refs_0_), channel_id=1, source_target_pairs={{0,2},{2,4},{4,6},{6,0},{1,3},{3,5},{5,7},{7,1},{8,10},{10,12},{12... | collective-permute-start | bytes 147464 | tf_op jit(solution)/shard_map/ppermute | solution.py:18
  12.8 5.7 %collective-permute-start.3 = (bf16[32,3072]{1,0:T(8,128)(2,1)S(1)}, bf16[32,3072]{1,0:T(8,128)(2,1)S(1)}, u32[]{:S(2)}, u32[]{:S(2)}) collective-permute-start(bf16[32,3072]{1,0:T(8,128)(2,1)S(1)} %stack.1.x_ref), channel_id=1, source_target_pairs={{0,1},{1,0},{2,3},{3,2},{4,5},{5,4},{6,7},{7,6},{8,9},{9,8},{10,11... | collective-permute-start | bytes 589832 | tf_op jit(solution)/shard_map/ppermute | solution.py:18
  14.4 4.2 %copy-start.2 = (bf16[1,512,6144]{2,1,0:T(8,128)(2,1)S(1)}, bf16[1,512,6144]{2,1,0:T(8,128)(2,1)}, u32[]{:S(2)}) copy-start(bf16[1,512,6144]{2,1,0:T(8,128)(2,1)} %param.13) | copy-start | bytes 18874372
  20.4 14.7 %copy-start.3 = (s32[8,2]{0,1:T(2,128)S(1)}, s32[8,2]{0,1:T(2,128)}, u32[]{:S(2)}) copy-start(s32[8,2]{0,1:T(2,128)} %param.8) | copy-start | bytes 196
  20.4 14.7 %copy-start.4 = (f32[8,2]{0,1:T(2,128)S(1)}, f32[8,2]{0,1:T(2,128)}, u32[]{:S(2)}) copy-start(f32[8,2]{0,1:T(2,128)} %param.10) | copy-start | bytes 196
  20.4 7.0 %collective-permute-start.5 = (bf16[32,3072]{1,0:T(8,128)(2,1)S(1)}, bf16[32,3072]{1,0:T(8,128)(2,1)S(1)}, u32[]{:S(2)}, u32[]{:S(2)}) collective-permute-start(bf16[32,3072]{1,0:T(8,128)(2,1)S(1)} %get-tuple-element.20), channel_id=1, source_target_pairs={{0,1},{1,0},{2,3},{3,2},{4,5},{5,4},{6,7},{7,6},{8,9},{9,8},{10,11... | collective-permute-start | bytes 589832 | tf_op jit(solution)/shard_map/ppermute | solution.py:18
  21.9 1.2 %collective-permute-start.4 = (s32[8,128]{1,0:T(8,128)S(1)}, s32[8,128]{1,0:T(8,128)S(1)}, u32[]{:S(2)}, u32[]{:S(2)}) collective-permute-start(s32[8,128]{1,0:T(8,128)S(1)} %get-tuple-element.18.counts_ref), channel_id=1, source_target_pairs={{0,8},{8,0},{16,24},{24,16},{1,9},{9,1},{17,25},{25,17},{2,10},{10... | collective-permute-start | bytes 12296 | tf_op jit(solution)/shard_map/ppermute | solution.py:22
  23.8 3.6 %collective-permute-start.6 = (s32[8,128]{1,0:T(8,128)S(1)}, s32[8,128]{1,0:T(8,128)S(1)}, u32[]{:S(2)}, u32[]{:S(2)}) collective-permute-start(s32[8,128]{1,0:T(8,128)S(1)} %get-tuple-element.21.refs_2_), channel_id=1, source_target_pairs={{0,16},{8,24},{16,0},{24,8},{1,17},{9,25},{17,1},{25,9},{2,18},{10... | collective-permute-start | bytes 12296 | tf_op jit(solution)/shard_map/ppermute | solution.py:22
  27.4 4.3 %collective-permute-start.7 = (bf16[8,3200]{1,0:T(8,128)(2,1)S(1)}, bf16[8,3200]{1,0:T(8,128)(2,1)S(1)}, u32[]{:S(2)}, u32[]{:S(2)}) collective-permute-start(bf16[8,3200]{1,0:T(8,128)(2,1)S(1)} %get-tuple-element.23), channel_id=1, source_target_pairs={{0,6},{2,0},{4,2},{6,4},{1,7},{3,1},{5,3},{7,5},{8,14},{10,8},{12,... | collective-permute-start | bytes 153608 | tf_op jit(solution)/shard_map/ppermute | solution.py:18
  28.7 5.6 %collective-permute-start.8 = (bf16[8,3200]{1,0:T(8,128)(2,1)S(1)}, bf16[8,3200]{1,0:T(8,128)(2,1)S(1)}, u32[]{:S(2)}, u32[]{:S(2)}) collective-permute-start(bf16[8,3200]{1,0:T(8,128)(2,1)S(1)} %get-tuple-element.24), channel_id=1, source_target_pairs={{0,4},{2,6},{4,0},{6,2},{1,5},{3,7},{5,1},{7,3},{8,12},{10,14},{12... | collective-permute-start | bytes 153608 | tf_op jit(solution)/shard_map/ppermute | solution.py:18
  29.1 5.9 %collective-permute-start.9 = (bf16[8,3200]{1,0:T(8,128)(2,1)S(1)}, bf16[8,3200]{1,0:T(8,128)(2,1)S(1)}, u32[]{:S(2)}, u32[]{:S(2)}) collective-permute-start(bf16[8,3200]{1,0:T(8,128)(2,1)S(1)} %get-tuple-element.25), channel_id=1, source_target_pairs={{0,2},{2,4},{4,6},{6,0},{1,3},{3,5},{5,7},{7,1},{8,10},{10,12},{12... | collective-permute-start | bytes 153608 | tf_op jit(solution)/shard_map/ppermute | solution.py:18

commit v4 on v3

v4 whole, which is shorter than its diff:
```python
import functools

import jax
import jax.numpy as jnp
from jax import lax
from jax.experimental import pallas as pl
from jax.experimental.pallas import tpu as pltpu
from jax.sharding import PartitionSpec as P

REPL = 4
LANES = 128
MIB = 1 << 20

route_scale = 2.5


def shift(array, axis, count, step):
    return lax.ppermute(array, axis, [(i, (i + step) % count) for i in range(count)])


def swap(array, axis, count, span):
    return lax.ppermute(array, axis, [(i, i ^ span) for i in range(count)])


def window(index, size):
    return pl.ds(pl.multiple_of(index * size, size), size)


def dot(a, b):
    return jnp.dot(a, b, preferred_element_type=jnp.float32)


def ready_kernel(out_ref):
    out_ref[...] = jnp.zeros(out_ref.shape, out_ref.dtype)


def intake_kernel(rep_count, tokens_ref, ids_ref, picks_ref, ready_ref, out_ref):
    part = tokens_ref.shape[1]
    group = lax.rem(lax.axis_index("rep") + picks_ref[...] * (rep_count // REPL), rep_count)
    ids = ids_ref[...]
    rows, lanes = out_ref.shape[0], out_ref.shape[1] - part
    cells = lax.rem(group, rows) * lanes + (group // rows) * LANES + ids
    position = lax.broadcasted_iota(jnp.int32, (rows, lanes), 0) * lanes
    position = position + lax.broadcasted_iota(jnp.int32, (rows, lanes), 1)
    total = jnp.zeros((rows, lanes), jnp.float32)
    for k in range(cells.shape[0]):
        for t in range(cells.shape[1]):
            total += (position == cells[k : k + 1, t : t + 1]).astype(jnp.float32)
    out_ref[:, :part] = tokens_ref[...]
    out_ref[:, part:] = total.astype(out_ref.dtype)


def stack_kernel(*refs):
    pieces, out_ref = refs[:-1], refs[-1]
    tok_rows, part = pieces[0].shape[0], out_ref.shape[1]
    for s, piece in enumerate(pieces):
        out_ref[pl.ds(s * tok_rows, tok_rows), :] = piece[:, :part]


def sum_kernel(*refs):
    pieces, out_ref = refs[:-1], refs[-1]
    part = pieces[0].shape[1] - out_ref.shape[1]
    out_ref[...] = sum(piece[:, part:].astype(jnp.float32) for piece in pieces).astype(jnp.int32)


def joined(refs):
    return jnp.concatenate([ref[...] for ref in refs], 0)


def own_kernel(*refs):
    pieces, (gate_ref, up_ref, down_ref, gate_acc, up_acc) = refs[:-5], refs[-5:]
    rows = window(lax.axis_index("tp"), pieces[0].shape[1])
    x = joined(pieces)
    gate_acc[...] = dot(x, gate_ref[rows, :])
    up_acc[...] = dot(x, up_ref[rows, :])


def hidden_kernel(tp_count, group_count, places, *refs):
    total = (tp_count - 1) * group_count
    others, refs = refs[:total], refs[total:]
    (gate_acc, up_acc, gate_ref, up_ref, down_ref, hidden_out), outs = refs[:6], refs[6:]
    me = lax.axis_index("tp")
    part = others[0].shape[1]
    gate = gate_acc[...]
    up = up_acc[...]
    for step in range(1, tp_count):
        rows = window(lax.rem(me - step + tp_count, tp_count), part)
        x = joined(others[(step - 1) * group_count : step * group_count])
        gate += dot(x, gate_ref[rows, :])
        up += dot(x, up_ref[rows, :])
    hidden = (gate / (1.0 + jnp.exp(-gate)) * up).astype(jnp.bfloat16)
    hidden_out[...] = hidden
    for step in range(1, tp_count):
        columns = window(lax.rem(me + step, tp_count), part)
        partial = dot(hidden, down_ref[:, columns]).astype(jnp.bfloat16)
        for place, out in zip(places, outs[(step - 1) * len(places) :]):
            size = out.shape[0] // len(place)
            for i, p in enumerate(place):
                out[pl.ds(i * size, size), :] = partial[p * size : (p + 1) * size]


def down_kernel(hidden_ref, down_ref, out_ref):
    columns = window(lax.axis_index("tp"), out_ref.shape[1])
    out_ref[...] = dot(hidden_ref[...], down_ref[:, columns])


def pack_kernel(place, arrived_count, mine_ref, *refs):
    arrived, outs = refs[:arrived_count], refs[arrived_count:]
    size = outs[0].shape[0]
    for i, (p, out) in enumerate(zip(place, outs)):
        total = mine_ref[pl.ds(p * size, size), :]
        for piece in arrived:
            total += piece[pl.ds(i * size, size), :].astype(jnp.float32)
        out[...] = total.astype(jnp.bfloat16)


def combine_kernel(ids_ref, scores_ref, sum_ref, swapped_ref, *refs):
    pieces, (out_ref, counts_ref) = refs[:-2], refs[-2:]
    ep_count = len(pieces)
    tok_rows, part = out_ref.shape
    me = lax.axis_index("ep")
    gains = jax.nn.sigmoid(scores_ref[...])
    weights = gains / jnp.sum(gains, 0, keepdims=True) * route_scale
    ids = ids_ref[...]
    total = jnp.zeros((tok_rows, part), jnp.float32)
    diagonal = lax.broadcasted_iota(jnp.int32, (tok_rows, tok_rows), 0) == (
        lax.broadcasted_iota(jnp.int32, (tok_rows, tok_rows), 1)
    )
    for s, piece in enumerate(pieces):
        row = jnp.sum(jnp.where(ids == (me ^ s), weights, 0.0), 0, keepdims=True)
        column = jnp.sum(jnp.where(diagonal, row, 0.0), 1, keepdims=True)
        total += column * piece[...].astype(jnp.float32)
    out_ref[...] = total.astype(jnp.bfloat16)
    counts = sum_ref[...] + swapped_ref[...]
    for group in range(0, counts_ref.shape[0], tok_rows):
        size = min(tok_rows, counts_ref.shape[0] - group)
        start = group // tok_rows * LANES
        counts_ref[pl.ds(group, size), :] = counts[:size, start : start + ep_count]


def vmem_call(kernel, outs, args, flops):
    return pl.pallas_call(
        kernel,
        out_shape=[pltpu.VMEM(shape, dtype) for shape, dtype in outs],
        in_specs=[pl.BlockSpec(memory_space=pltpu.VMEM)] * len(args),
        out_specs=[pl.BlockSpec(memory_space=pltpu.VMEM)] * len(outs),
        compiler_params=pltpu.CompilerParams(vmem_limit_bytes=24 * MIB),
        cost_estimate=pl.CostEstimate(flops=flops, bytes_accessed=MIB, transcendentals=0),
    )(*args)


def per_device(tokens, expert_ids, replicas, scores, w_gate, w_up, w_down):
    rep_count = lax.axis_size("rep")
    ep_count = lax.axis_size("ep")
    tp_count = lax.axis_size("tp")
    tok_rows, part = tokens.shape
    ffe = w_gate.shape[2]
    rows = ep_count * tok_rows
    groups, out_groups = row_groups(ep_count)
    order = [s for group in groups for s in group]
    places = [[order.index(s) for s in group] for group in out_groups]
    bf16, f32, i32 = jnp.bfloat16, jnp.float32, jnp.int32
    gate_w, up_w, down_w = w_gate[0], w_up[0], w_down[0]

    ids, picks, gains = expert_ids.T, replicas.T, scores.T

    (ready,) = vmem_call(ready_kernel, [((8, LANES), f32)], (), 10**11)

    width = -(-rep_count // tok_rows) * LANES
    (message,) = vmem_call(
        functools.partial(intake_kernel, rep_count),
        [((tok_rows, part + width), bf16)],
        (tokens, ids, picks, ready),
        1000,
    )

    blocks = [message]
    blocks += [swap(message, "ep", ep_count, s) for s in range(1, ep_count)]
    steps = range(1, tp_count)
    owned, others = [], []
    for group in groups:
        shape = (len(group) * tok_rows, part)
        held = tuple(blocks[s] for s in group)
        owned += vmem_call(stack_kernel, [(shape, bf16)], held, 1000)
        others.append([shift(owned[-1], "tp", tp_count, s) for s in steps])
    (counts,) = vmem_call(sum_kernel, [((tok_rows, width), i32)], tuple(blocks), 1000)
    swapped = jnp.zeros_like(counts)
    for bit in range(rep_count.bit_length() - 1):
        counts = counts + swapped
        swapped = swap(counts, "rep", rep_count, 1 << bit)
    dot_flops = 2 * rows * part * ffe
    gate_acc, up_acc = vmem_call(
        own_kernel, [((rows, ffe), f32)] * 2, (*owned, gate_w, up_w, down_w), 2 * dot_flops
    )
    hidden, *partials = vmem_call(
        functools.partial(hidden_kernel, tp_count, len(groups), places),
        [((rows, ffe), bf16)]
        + [((len(p) * tok_rows, part), bf16) for p in places] * len(steps),
        (*[group[s - 1] for s in steps for group in others], gate_acc, up_acc, gate_w, up_w, down_w),
        3 * len(steps) * dot_flops,
    )
    arrived = []
    for number in range(len(places)):
        pieces = partials[number :: len(places)]
        arrived.append([shift(p, "tp", tp_count, s) for s, p in zip(steps, pieces)])
    (mine,) = vmem_call(down_kernel, [((rows, part), f32)], (hidden, down_w), dot_flops)

    back = [None] * ep_count
    for number, group in enumerate(out_groups):
        outgoing = vmem_call(
            functools.partial(pack_kernel, places[number], len(steps)),
            [((tok_rows, part), bf16)] * len(group),
            (mine, *arrived[number]),
            1000,
        )
        for s, piece in zip(group, outgoing):
            back[s] = swap(piece, "ep", ep_count, s) if s else piece
    return pl.pallas_call(
        combine_kernel,
        out_shape=[
            jax.ShapeDtypeStruct((tok_rows, part), bf16),
            jax.ShapeDtypeStruct((rep_count, ep_count), i32),
        ],
        compiler_params=pltpu.CompilerParams(vmem_limit_bytes=8 * MIB),
        name="combine",
    )(ids, gains, counts, swapped, *back)


def row_groups(ep_count):
    half = ep_count // 2
    far = list(range(ep_count - 1, half, -1))
    near = list(range(1, half))
    return [[0, half], far + near], [[half], far, near + [0]]


def solution(mesh):
    placed = (
        P(("rep", "ep"), "tp"),
        P(("rep", "ep"), None),
        P(("rep", "ep"), None),
        P(("rep", "ep"), None),
        P("ep", None, "tp"),
        P("ep", None, "tp"),
        P("ep", "tp", None),
    )

    return jax.shard_map(
        per_device,
        mesh=mesh,
        in_specs=placed,
        out_specs=(P(("rep", "ep"), "tp"), P()),
        check_vma=False,
    )
```

time: 35.9 us -> 34 us (0.947)
  waiting for transfers between devices: 15.1 us -> 9.28 us
  starting transfers between devices: 14.4 us -> 18.5 us
  Pallas kernels: 5.56 us -> 4.57 us
  local copies, waits for them, and re-layouts: 0.02 us -> 0.79 us
    ppermute x2 -> x8, starting transfers between devices: 1.54 us -> 11.6 us  [swap(): return lax.ppermute(array, axis, [(i, i ^ span) for i in range(count)])]
    ppermute x8 -> x5, waiting for transfers between devices: 11.8 us -> 3.38 us  [shift(): lax.ppermute(array, axis, [(i, (i + step) % count) for i in range(count)])]
    ppermute x8 -> x5, starting transfers between devices: 12.9 us -> 6.9 us  [shift(): lax.ppermute(array, axis, [(i, (i + step) % count) for i in range(count)])]
    ppermute x2 -> x8, waiting for transfers between devices: 3.25 us -> 5.9 us  [swap(): return lax.ppermute(array, axis, [(i, i ^ span) for i in range(count)])]
    pallas_call x6 -> x11, Pallas kernels: 4.8 us -> 3.81 us  [vmem_call(): pl.pallas_call(kernel, out_shape=[pltpu.VMEM(shape, dtype) for shape, dty...]
    unnamed x10 -> x14, local copies, waits for them, and re-layouts: 0.02 us -> 0.79 us
  transfers between devices with their start and end apart: 10 -> 13, of which waited for: 9 -> 6; matrix products, arithmetic and copies ran while one was open for 0% -> 0% of each run, Pallas kernels for 5% -> 6%
where the time goes in v4:
time: 34 us; the launch traced here: 33.9 us
  starting transfers between devices  18.5 us (54%)
  waiting for transfers between devices  9.28 us (27%)
  Pallas kernels  4.57 us (13%)
  local copies, waits for them, and re-layouts  0.79 us (2%)
  between operations  0.77 us (2%)
    ppermute x8, starting transfers between devices, swap(): return lax.ppermute(array, axis, [(i, i ^ span) for i in range(count)])  11.6 us
    ppermute x5, starting transfers between devices, shift(): lax.ppermute(array, axis, [(i, (i + step) % count) for i in range(count)])  6.9 us
    ppermute x8, waiting for transfers between devices, swap(): return lax.ppermute(array, axis, [(i, i ^ span) for i in range(count)])  5.9 us
    pallas_call x11, Pallas kernels, vmem_call(): pl.pallas_call(kernel, out_shape=[pltpu.VMEM(shape, dtype) for shape, dty...  3.81 us
    ppermute x5, waiting for transfers between devices, shift(): lax.ppermute(array, axis, [(i, (i + step) % count) for i in range(count)])  3.38 us
    unnamed x14, local copies, waits for them, and re-layouts  0.79 us
    pallas_call x1, Pallas kernels, per_device(): pl.pallas_call(combine_kernel, out_shape=[jax.ShapeDtypeStruct((tok_rows,...  0.77 us
  transfers between devices with their start and end apart: 13, of which 6 were waited for; matrix products, arithmetic and copies ran while one was open for 0% of the time, Pallas kernels for 6%

profile of v4, /device:TPU:0, one launch (start us, length us, event | category | flops | bytes accessed | tf_op | source)
XLA Modules:
  0.0 33.9 jit_solution(9235905868369746029)
XLA Ops:
  0.7 0.6 %copy-done.6 = s32[8,2]{0,1:T(2,128)S(1)} copy-done((s32[8,2]{0,1:T(2,128)S(1)}, s32[8,2]{0,1:T(2,128)}, u32[]{:S(2)}) %copy-start.6) | copy-done | bytes 88
  1.3 0.0 copy-done.4
  1.3 0.1 copy-done.3
  1.5 0.1 shard_map.87.refs_0_
  1.6 4.1 %collective-permute-start.1 = (bf16[8,3200]{1,0:T(8,128)(2,1)S(1)}, bf16[8,3200]{1,0:T(8,128)(2,1)S(1)}, u32[]{:S(2)}, u32[]{:S(2)}) collective-permute-start(bf16[8,3200]{1,0:T(8,128)(2,1)S(1)} %shard_map.87.refs_0_), channel_id=1, source_target_pairs={{0,4},{2,6},{4,0},{6,2},{1,5},{3,7},{5,1},{7,3},{8,12},{10,14},{12... | collective-permute-start | bytes 153608 | tf_op jit(solution)/shard_map/ppermute | solution.py:22
  5.7 1.3 %collective-permute-start.2 = (bf16[8,3200]{1,0:T(8,128)(2,1)S(1)}, bf16[8,3200]{1,0:T(8,128)(2,1)S(1)}, u32[]{:S(2)}, u32[]{:S(2)}) collective-permute-start(bf16[8,3200]{1,0:T(8,128)(2,1)S(1)} %shard_map.87.refs_0_), channel_id=1, source_target_pairs={{0,6},{2,4},{4,2},{6,0},{1,7},{3,5},{5,3},{7,1},{8,14},{10,12},{12... | collective-permute-start | bytes 153608 | tf_op jit(solution)/shard_map/ppermute | solution.py:22
  7.1 0.2 collective-permute-start
  7.3 1.1 %collective-permute-done.1.refs_2_.refs_1_ = bf16[8,3200]{1,0:T(8,128)(2,1)S(1)} collective-permute-done((bf16[8,3200]{1,0:T(8,128)(2,1)S(1)}, bf16[8,3200]{1,0:T(8,128)(2,1)S(1)}, u32[]{:S(2)}, u32[]{:S(2)}) %collective-permute-start.1) | collective-permute-done | bytes 51232 | tf_op jit(solution)/shard_map/ppermute | solution.py:22
  8.4 1.8 %collective-permute-start.5 = (bf16[16,3072]{1,0:T(8,128)(2,1)S(1)}, bf16[16,3072]{1,0:T(8,128)(2,1)S(1)}, u32[]{:S(2)}, u32[]{:S(2)}) collective-permute-start(bf16[16,3072]{1,0:T(8,128)(2,1)S(1)} %shard_map.89.refs_0_), channel_id=1, source_target_pairs={{0,1},{1,0},{2,3},{3,2},{4,5},{5,4},{6,7},{7,6},{8,9},{9,8},{10,11... | collective-permute-start | bytes 294920 | tf_op jit(solution)/shard_map/ppermute | solution.py:18
  10.2 1.6 %collective-permute-done.2.refs_3_.refs_0_ = bf16[8,3200]{1,0:T(8,128)(2,1)S(1)} collective-permute-done((bf16[8,3200]{1,0:T(8,128)(2,1)S(1)}, bf16[8,3200]{1,0:T(8,128)(2,1)S(1)}, u32[]{:S(2)}, u32[]{:S(2)}) %collective-permute-start.2) | collective-permute-done | bytes 51232 | tf_op jit(solution)/shard_map/ppermute | solution.py:22
  11.8 0.0 collective-permute-done.refs_1_
  11.8 1.6 %collective-permute-start.6 = (bf16[16,3072]{1,0:T(8,128)(2,1)S(1)}, bf16[16,3072]{1,0:T(8,128)(2,1)S(1)}, u32[]{:S(2)}, u32[]{:S(2)}) collective-permute-start(bf16[16,3072]{1,0:T(8,128)(2,1)S(1)} %shard_map.90.refs_1_), channel_id=1, source_target_pairs={{0,1},{1,0},{2,3},{3,2},{4,5},{5,4},{6,7},{7,6},{8,9},{9,8},{10,11... | collective-permute-start | bytes 294920 | tf_op jit(solution)/shard_map/ppermute | solution.py:18
  13.3 1.2 %shard_map.91 = (f32[32,512]{1,0:T(8,128)S(1)}, f32[32,512]{1,0:T(8,128)S(1)}) custom-call(bf16[16,3072]{1,0:T(8,128)(2,1)S(1)} %shard_map.89.refs_0_, bf16[16,3072]{1,0:T(8,128)(2,1)S(1)} %shard_map.90.refs_1_, bf16[6144,512]{1,0:T(8,128)(2,1)S(1)} %bitcast.9, bf16[6144,512]{1,0:T(8,128)(2,1)S(1)} %bitcast.11, bf16[512,6144]{1,0:T(8,128)(2,1)S(1)} %bitcast.6), custom_call_target="tpu_custom_call" | custom-call | flops 201326592 | bytes 1048576 | tf_op jit(solution)/shard_map/pallas_call | solution.py:142
  14.5 0.0 collective-permute-done.5.refs_0_
  14.5 1.9 %collective-permute-done.6.refs_1_ = bf16[16,3072]{1,0:T(8,128)(2,1)S(1)} collective-permute-done((bf16[16,3072]{1,0:T(8,128)(2,1)S(1)}, bf16[16,3072]{1,0:T(8,128)(2,1)S(1)}, u32[]{:S(2)}, u32[]{:S(2)}) %collective-permute-start.6) | collective-permute-done | bytes 98336 | tf_op jit(solution)/shard_map/ppermute | solution.py:18
  16.4 1.8 %shard_map.92 = (bf16[32,512]{1,0:T(8,128)(2,1)S(1)}, bf16[8,3072]{1,0:T(8,128)(2,1)S(1)}, bf16[8,3072]{1,0:T(8,128)(2,1)S(1)}, bf16[16,3072]{1,0:T(8,128)(2,1)S(1)}) custom-call(bf16[16,3072]{1,0:T(8,128)(2,1)S(1)} %collective-permute-done.5.refs_0_, bf16[16,3072]{1,0:T(8,128)(2,1)S(1)} %collective-permute-done.6.refs_1_, ...), custom_call_target="tpu_custom_call" | custom-call | flops 301989888 | bytes 1048576 | tf_op jit(solution)/shard_map/pallas_call | solution.py:142
  18.2 0.0 copy-start.5
  18.2 1.6 %collective-permute-start.7 = (bf16[16,3072]{1,0:T(8,128)(2,1)S(1)}, bf16[16,3072]{1,0:T(8,128)(2,1)S(1)}, u32[]{:S(2)}, u32[]{:S(2)}) collective-permute-start(bf16[16,3072]{1,0:T(8,128)(2,1)S(1)} %get-tuple-element.13), channel_id=1, source_target_pairs={{0,1},{1,0},{2,3},{3,2},{4,5},{5,4},{6,7},{7,6},{8,9},{9,8},{10,11... | collective-permute-start | bytes 294920 | tf_op jit(solution)/shard_map/ppermute | solution.py:18
  19.8 0.5 %collective-permute-start.9 = (bf16[8,3072]{1,0:T(8,128)(2,1)S(1)}, bf16[8,3072]{1,0:T(8,128)(2,1)S(1)}, u32[]{:S(2)}, u32[]{:S(2)}) collective-permute-start(bf16[8,3072]{1,0:T(8,128)(2,1)S(1)} %get-tuple-element.16), channel_id=1, source_target_pairs={{0,1},{1,0},{2,3},{3,2},{4,5},{5,4},{6,7},{7,6},{8,9},{9,8},{10,11... | collective-permute-start | bytes 147464 | tf_op jit(solution)/shard_map/ppermute | solution.py:18
  20.3 1.5 %collective-permute-start.11 = (bf16[8,3072]{1,0:T(8,128)(2,1)S(1)}, bf16[8,3072]{1,0:T(8,128)(2,1)S(1)}, u32[]{:S(2)}, u32[]{:S(2)}) collective-permute-start(bf16[8,3072]{1,0:T(8,128)(2,1)S(1)} %get-tuple-element.17), channel_id=1, source_target_pairs={{0,1},{1,0},{2,3},{3,2},{4,5},{5,4},{6,7},{7,6},{8,9},{9,8},{10,11... | collective-permute-start | bytes 147464 | tf_op jit(solution)/shard_map/ppermute | solution.py:18
  21.8 0.6 %shard_map.93.mine_ref = f32[32,3072]{1,0:T(8,128)S(1)} custom-call(bf16[32,512]{1,0:T(8,128)(2,1)S(1)} %get-tuple-element.12.hidden_ref, bf16[512,6144]{1,0:T(8,128)(2,1)S(1)} %bitcast.8), custom_call_target="tpu_custom_call" | custom-call | flops 100663296 | bytes 1048576 | tf_op jit(solution)/shard_map/pallas_call | solution.py:142
  22.5 1.4 %collective-permute-done.9.refs_0_ = bf16[8,3072]{1,0:T(8,128)(2,1)S(1)} collective-permute-done((bf16[8,3072]{1,0:T(8,128)(2,1)S(1)}, bf16[8,3072]{1,0:T(8,128)(2,1)S(1)}, u32[]{:S(2)}, u32[]{:S(2)}) %collective-permute-start.9) | collective-permute-done | bytes 49184 | tf_op jit(solution)/shard_map/ppermute | solution.py:18
  23.9 1.8 %collective-permute-start.10 = (bf16[8,3072]{1,0:T(8,128)(2,1)S(1)}, bf16[8,3072]{1,0:T(8,128)(2,1)S(1)}, u32[]{:S(2)}, u32[]{:S(2)}) collective-permute-start(bf16[8,3072]{1,0:T(8,128)(2,1)S(1)} %shard_map.95), channel_id=1, source_target_pairs={{0,4},{2,6},{4,0},{6,2},{1,5},{3,7},{5,1},{7,3},{8,12},{10,14},{12... | collective-permute-start | bytes 147464 | tf_op jit(solution)/shard_map/ppermute | solution.py:22
  25.7 0.0 collective-permute-done.11.refs_0_
  25.7 2.4 %collective-permute-start.12 = (bf16[8,3072]{1,0:T(8,128)(2,1)S(1)}, bf16[8,3072]{1,0:T(8,128)(2,1)S(1)}, u32[]{:S(2)}, u32[]{:S(2)}) collective-permute-start(bf16[8,3072]{1,0:T(8,128)(2,1)S(1)} %shard_map.96), channel_id=1, source_target_pairs={{0,6},{2,4},{4,2},{6,0},{1,7},{3,5},{5,3},{7,1},{8,14},{10,12},{12... | collective-permute-start | bytes 147464 | tf_op jit(solution)/shard_map/ppermute | solution.py:22
  28.2 0.1 collective-permute-start.8
  28.3 0.1 collective-permute-start.3
  28.3 1.2 %collective-permute-done.3 = s32[8,128]{1,0:T(8,128)S(1)} collective-permute-done((s32[8,128]{1,0:T(8,128)S(1)}, s32[8,128]{1,0:T(8,128)S(1)}, u32[]{:S(2)}, u32[]{:S(2)}) %collective-permute-start.3) | collective-permute-done | bytes 4128 | tf_op jit(solution)/shard_map/ppermute | solution.py:22
  29.5 1.5 %collective-permute-start.4 = (s32[8,128]{1,0:T(8,128)S(1)}, s32[8,128]{1,0:T(8,128)S(1)}, u32[]{:S(2)}, u32[]{:S(2)}) collective-permute-start(s32[8,128]{1,0:T(8,128)S(1)} %add.3.sum_ref), channel_id=1, source_target_pairs={{0,16},{8,24},{16,0},{24,8},{1,17},{9,25},{17,1},{25,9},{2,18},{10... | collective-permute-start | bytes 12296 | tf_op jit(solution)/shard_map/ppermute | solution.py:22
  31.0 2.1 %collective-permute-done.4.swapped_ref = s32[8,128]{1,0:T(8,128)S(1)} collective-permute-done((s32[8,128]{1,0:T(8,128)S(1)}, s32[8,128]{1,0:T(8,128)S(1)}, u32[]{:S(2)}, u32[]{:S(2)}) %collective-permute-start.4) | collective-permute-done | bytes 4128 | tf_op jit(solution)/shard_map/ppermute | solution.py:22
  33.1 0.0 collective-permute-done.10.refs_2_
  33.1 0.8 %combine.1 = (bf16[8,3072]{1,0:T(8,128)(2,1)}, s32[4,4]{1,0:T(4,128)}) custom-call(s32[2,8]{1,0:T(2,128)S(1)} %bitcast.14, f32[2,8]{1,0:T(2,128)S(1)} %bitcast.15, s32[8,128]{1,0:T(8,128)S(1)} %add.3.sum_ref, s32[8,128]{1,0:T(8,128)S(1)} %collective-permute-done.4.swapped_ref, bf16[8,3072]{1,0:T(8,128)(2,1)S(1)} %get-tuple-element.14.refs_0_, ...), custom_call_target="tpu_custom_call" | custom-call | tf_op jit(solution)/shard_map/combine/pallas_call | solution.py:218
  (21 shorter events, 0.1 us)
Async XLA Ops:
  0.6 0.7 %copy-start.6 = (s32[8,2]{0,1:T(2,128)S(1)}, s32[8,2]{0,1:T(2,128)}, u32[]{:S(2)}) copy-start(s32[8,2]{0,1:T(2,128)} %param.9) | copy-start | bytes 196
  0.6 0.7 %copy-start.4 = (s32[8,2]{0,1:T(2,128)S(1)}, s32[8,2]{0,1:T(2,128)}, u32[]{:S(2)}) copy-start(s32[8,2]{0,1:T(2,128)} %param.8) | copy-start | bytes 196
  0.7 0.8 %copy-start.3 = (bf16[8,3072]{1,0:T(8,128)(2,1)S(1)}, bf16[8,3072]{1,0:T(8,128)(2,1)}, u32[]{:S(2)}) copy-start(bf16[8,3072]{1,0:T(8,128)(2,1)} %tokens_ref.1) | copy-start | bytes 147460
  0.7 12.7 %copy-start = (bf16[1,512,6144]{2,1,0:T(8,128)(2,1)S(1)}, bf16[1,512,6144]{2,1,0:T(8,128)(2,1)}, u32[]{:S(2)}) copy-start(bf16[1,512,6144]{2,1,0:T(8,128)(2,1)} %param.13) | copy-start | bytes 18874372
  0.7 12.7 %copy-start.2 = (bf16[1,6144,512]{2,1,0:T(8,128)(2,1)S(1)}, bf16[1,6144,512]{2,1,0:T(8,128)(2,1)}, u32[]{:S(2)}) copy-start(bf16[1,6144,512]{2,1,0:T(8,128)(2,1)} %param.12) | copy-start | bytes 18874372
  0.7 12.6 %copy-start.1 = (bf16[1,6144,512]{2,1,0:T(8,128)(2,1)S(1)}, bf16[1,6144,512]{2,1,0:T(8,128)(2,1)}, u32[]{:S(2)}) copy-start(bf16[1,6144,512]{2,1,0:T(8,128)(2,1)} %param.11) | copy-start | bytes 18874372
  1.6 6.8 %collective-permute-start.1 = (bf16[8,3200]{1,0:T(8,128)(2,1)S(1)}, bf16[8,3200]{1,0:T(8,128)(2,1)S(1)}, u32[]{:S(2)}, u32[]{:S(2)}) collective-permute-start(bf16[8,3200]{1,0:T(8,128)(2,1)S(1)} %shard_map.87.refs_0_), channel_id=1, source_target_pairs={{0,4},{2,6},{4,0},{6,2},{1,5},{3,7},{5,1},{7,3},{8,12},{10,14},{12... | collective-permute-start | bytes 153608 | tf_op jit(solution)/shard_map/ppermute | solution.py:22
  5.7 6.0 %collective-permute-start.2 = (bf16[8,3200]{1,0:T(8,128)(2,1)S(1)}, bf16[8,3200]{1,0:T(8,128)(2,1)S(1)}, u32[]{:S(2)}, u32[]{:S(2)}) collective-permute-start(bf16[8,3200]{1,0:T(8,128)(2,1)S(1)} %shard_map.87.refs_0_), channel_id=1, source_target_pairs={{0,6},{2,4},{4,2},{6,0},{1,7},{3,5},{5,3},{7,1},{8,14},{10,12},{12... | collective-permute-start | bytes 153608 | tf_op jit(solution)/shard_map/ppermute | solution.py:22
  7.1 4.7 %collective-permute-start = (bf16[8,3200]{1,0:T(8,128)(2,1)S(1)}, bf16[8,3200]{1,0:T(8,128)(2,1)S(1)}, u32[]{:S(2)}, u32[]{:S(2)}) collective-permute-start(bf16[8,3200]{1,0:T(8,128)(2,1)S(1)} %shard_map.87.refs_0_), channel_id=1, source_target_pairs={{0,2},{2,0},{4,6},{6,4},{1,3},{3,1},{5,7},{7,5},{8,10},{10,8},{12,... | collective-permute-start | bytes 153608 | tf_op jit(solution)/shard_map/ppermute | solution.py:22
  8.4 6.1 %collective-permute-start.5 = (bf16[16,3072]{1,0:T(8,128)(2,1)S(1)}, bf16[16,3072]{1,0:T(8,128)(2,1)S(1)}, u32[]{:S(2)}, u32[]{:S(2)}) collective-permute-start(bf16[16,3072]{1,0:T(8,128)(2,1)S(1)} %shard_map.89.refs_0_), channel_id=1, source_target_pairs={{0,1},{1,0},{2,3},{3,2},{4,5},{5,4},{6,7},{7,6},{8,9},{9,8},{10,11... | collective-permute-start | bytes 294920 | tf_op jit(solution)/shard_map/ppermute | solution.py:18
  11.8 4.7 %collective-permute-start.6 = (bf16[16,3072]{1,0:T(8,128)(2,1)S(1)}, bf16[16,3072]{1,0:T(8,128)(2,1)S(1)}, u32[]{:S(2)}, u32[]{:S(2)}) collective-permute-start(bf16[16,3072]{1,0:T(8,128)(2,1)S(1)} %shard_map.90.refs_1_), channel_id=1, source_target_pairs={{0,1},{1,0},{2,3},{3,2},{4,5},{5,4},{6,7},{7,6},{8,9},{9,8},{10,11... | collective-permute-start | bytes 294920 | tf_op jit(solution)/shard_map/ppermute | solution.py:18
  18.2 14.9 %copy-start.5 = (f32[8,2]{0,1:T(2,128)S(1)}, f32[8,2]{0,1:T(2,128)}, u32[]{:S(2)}) copy-start(f32[8,2]{0,1:T(2,128)} %param.10) | copy-start | bytes 196
  18.2 9.9 %collective-permute-start.7 = (bf16[16,3072]{1,0:T(8,128)(2,1)S(1)}, bf16[16,3072]{1,0:T(8,128)(2,1)S(1)}, u32[]{:S(2)}, u32[]{:S(2)}) collective-permute-start(bf16[16,3072]{1,0:T(8,128)(2,1)S(1)} %get-tuple-element.13), channel_id=1, source_target_pairs={{0,1},{1,0},{2,3},{3,2},{4,5},{5,4},{6,7},{7,6},{8,9},{9,8},{10,11... | collective-permute-start | bytes 294920 | tf_op jit(solution)/shard_map/ppermute | solution.py:18
  19.8 4.1 %collective-permute-start.9 = (bf16[8,3072]{1,0:T(8,128)(2,1)S(1)}, bf16[8,3072]{1,0:T(8,128)(2,1)S(1)}, u32[]{:S(2)}, u32[]{:S(2)}) collective-permute-start(bf16[8,3072]{1,0:T(8,128)(2,1)S(1)} %get-tuple-element.16), channel_id=1, source_target_pairs={{0,1},{1,0},{2,3},{3,2},{4,5},{5,4},{6,7},{7,6},{8,9},{9,8},{10,11... | collective-permute-start | bytes 147464 | tf_op jit(solution)/shard_map/ppermute | solution.py:18
  20.3 5.3 %collective-permute-start.11 = (bf16[8,3072]{1,0:T(8,128)(2,1)S(1)}, bf16[8,3072]{1,0:T(8,128)(2,1)S(1)}, u32[]{:S(2)}, u32[]{:S(2)}) collective-permute-start(bf16[8,3072]{1,0:T(8,128)(2,1)S(1)} %get-tuple-element.17), channel_id=1, source_target_pairs={{0,1},{1,0},{2,3},{3,2},{4,5},{5,4},{6,7},{7,6},{8,9},{9,8},{10,11... | collective-permute-start | bytes 147464 | tf_op jit(solution)/shard_map/ppermute | solution.py:18
  23.9 9.2 %collective-permute-start.10 = (bf16[8,3072]{1,0:T(8,128)(2,1)S(1)}, bf16[8,3072]{1,0:T(8,128)(2,1)S(1)}, u32[]{:S(2)}, u32[]{:S(2)}) collective-permute-start(bf16[8,3072]{1,0:T(8,128)(2,1)S(1)} %shard_map.95), channel_id=1, source_target_pairs={{0,4},{2,6},{4,0},{6,2},{1,5},{3,7},{5,1},{7,3},{8,12},{10,14},{12... | collective-permute-start | bytes 147464 | tf_op jit(solution)/shard_map/ppermute | solution.py:22
  25.7 7.4 %collective-permute-start.12 = (bf16[8,3072]{1,0:T(8,128)(2,1)S(1)}, bf16[8,3072]{1,0:T(8,128)(2,1)S(1)}, u32[]{:S(2)}, u32[]{:S(2)}) collective-permute-start(bf16[8,3072]{1,0:T(8,128)(2,1)S(1)} %shard_map.96), channel_id=1, source_target_pairs={{0,6},{2,4},{4,2},{6,0},{1,7},{3,5},{5,3},{7,1},{8,14},{10,12},{12... | collective-permute-start | bytes 147464 | tf_op jit(solution)/shard_map/ppermute | solution.py:22
  28.2 4.9 %collective-permute-start.8 = (bf16[8,3072]{1,0:T(8,128)(2,1)S(1)}, bf16[8,3072]{1,0:T(8,128)(2,1)S(1)}, u32[]{:S(2)}, u32[]{:S(2)}) collective-permute-start(bf16[8,3072]{1,0:T(8,128)(2,1)S(1)} %get-tuple-element.15), channel_id=1, source_target_pairs={{0,2},{2,0},{4,6},{6,4},{1,3},{3,1},{5,7},{7,5},{8,10},{10,8},{12,... | collective-permute-start | bytes 147464 | tf_op jit(solution)/shard_map/ppermute | solution.py:22
  28.3 1.2 %collective-permute-start.3 = (s32[8,128]{1,0:T(8,128)S(1)}, s32[8,128]{1,0:T(8,128)S(1)}, u32[]{:S(2)}, u32[]{:S(2)}) collective-permute-start(s32[8,128]{1,0:T(8,128)S(1)} %shard_map.88), channel_id=1, source_target_pairs={{0,8},{8,0},{16,24},{24,16},{1,9},{9,1},{17,25},{25,17},{2,10},{10... | collective-permute-start | bytes 12296 | tf_op jit(solution)/shard_map/ppermute | solution.py:22
  29.5 3.6 %collective-permute-start.4 = (s32[8,128]{1,0:T(8,128)S(1)}, s32[8,128]{1,0:T(8,128)S(1)}, u32[]{:S(2)}, u32[]{:S(2)}) collective-permute-start(s32[8,128]{1,0:T(8,128)S(1)} %add.3.sum_ref), channel_id=1, source_target_pairs={{0,16},{8,24},{16,0},{24,8},{1,17},{9,25},{17,1},{25,9},{2,18},{10... | collective-permute-start | bytes 12296 | tf_op jit(solution)/shard_map/ppermute | solution.py:22

commit v5 on v4

--- a/solution.py
+++ b/solution.py
@@ -20,6 +20,15 @@
 
 def swap(array, axis, count, span):
     return lax.ppermute(array, axis, [(i, i ^ span) for i in range(count)])
+
+
+def diagonal(array, ep_count, tp_count, span, step):
+    pairs = [
+        (e * tp_count + t, (e ^ span) * tp_count + (t + step) % tp_count)
+        for e in range(ep_count)
+        for t in range(tp_count)
+    ]
+    return lax.ppermute(array, ("ep", "tp"), pairs)
 
 
 def window(index, size):
@@ -51,10 +60,11 @@
 
 
 def stack_kernel(*refs):
-    pieces, out_ref = refs[:-1], refs[-1]
-    tok_rows, part = pieces[0].shape[0], out_ref.shape[1]
+    pieces, outs = refs[:-2], refs[-2:]
+    tok_rows, size = pieces[0].shape[0], outs[0].shape[1]
     for s, piece in enumerate(pieces):
-        out_ref[pl.ds(s * tok_rows, tok_rows), :] = piece[:, :part]
+        for h, out in enumerate(outs):
+            out[pl.ds(s * tok_rows, tok_rows), :] = piece[:, h * size : (h + 1) * size]
 
 
 def sum_kernel(*refs):
@@ -63,31 +73,54 @@
     out_ref[...] = sum(piece[:, part:].astype(jnp.float32) for piece in pieces).astype(jnp.int32)
 
 
-def joined(refs):
-    return jnp.concatenate([ref[...] for ref in refs], 0)
+def slab(split_ref, whole_refs, h):
+    size = split_ref.shape[1]
+    pieces = [split_ref[...]] + [ref[:, h * size : (h + 1) * size] for ref in whole_refs]
+    return jnp.concatenate(pieces, 0)
 
 
 def own_kernel(*refs):
-    pieces, (gate_ref, up_ref, down_ref, gate_acc, up_acc) = refs[:-5], refs[-5:]
-    rows = window(lax.axis_index("tp"), pieces[0].shape[1])
-    x = joined(pieces)
-    gate_acc[...] = dot(x, gate_ref[rows, :])
-    up_acc[...] = dot(x, up_ref[rows, :])
-
-
-def hidden_kernel(tp_count, group_count, places, *refs):
-    total = (tp_count - 1) * group_count
-    others, refs = refs[:total], refs[total:]
+    splits, pieces = refs[:2], refs[2:-5]
+    gate_ref, up_ref, _, gate_acc, up_acc = refs[-5:]
+    size = splits[0].shape[1]
+    gate, up = 0.0, 0.0
+    for h, split in enumerate(splits):
+        rows = window(lax.axis_index("tp") * 2 + h, size)
+        x = slab(split, pieces, h)
+        gate += dot(x, gate_ref[rows, :])
+        up += dot(x, up_ref[rows, :])
+    gate_acc[...] = gate
+    up_acc[...] = up
+
+
+def other_features(tp_count, h, others, gate_ref, up_ref):
+    me = lax.axis_index("tp")
+    each = len(others) // (tp_count - 1)
+    gate, up = 0.0, 0.0
+    for step in range(1, tp_count):
+        split, *whole = others[(step - 1) * each : step * each]
+        rows = window(lax.rem(me - step + tp_count, tp_count) * 2 + h, split.shape[1])
+        x = slab(split, whole, h)
+        gate += dot(x, gate_ref[rows, :])
+        up += dot(x, up_ref[rows, :])
+    return gate, up
+
+
+def early_kernel(tp_count, *refs):
+    others, (gate_ref, up_ref, gate_acc, up_acc, gate_out, up_out) = refs[:-6], refs[-6:]
+    gate, up = other_features(tp_count, 0, others, gate_ref, up_ref)
+    gate_out[...] = gate_acc[...] + gate
+    up_out[...] = up_acc[...] + up
+
+
+def hidden_kernel(tp_count, count, places, *refs):
+    others, refs = refs[:count], refs[count:]
     (gate_acc, up_acc, gate_ref, up_ref, down_ref, hidden_out), outs = refs[:6], refs[6:]
     me = lax.axis_index("tp")
-    part = others[0].shape[1]
-    gate = gate_acc[...]
-    up = up_acc[...]
-    for step in range(1, tp_count):
-        rows = window(lax.rem(me - step + tp_count, tp_count), part)
-        x = joined(others[(step - 1) * group_count : step * group_count])
-        gate += dot(x, gate_ref[rows, :])
-        up += dot(x, up_ref[rows, :])
+    part = gate_ref.shape[0] // tp_count
+    gate, up = other_features(tp_count, 1, others, gate_ref, up_ref)
+    gate += gate_acc[...]
+    up += up_acc[...]
     hidden = (gate / (1.0 + jnp.exp(-gate)) * up).astype(jnp.bfloat16)
     hidden_out[...] = hidden
     for step in range(1, tp_count):
@@ -156,8 +189,8 @@
     tok_rows, part = tokens.shape
     ffe = w_gate.shape[2]
     rows = ep_count * tok_rows
-    groups, out_groups = row_groups(ep_count)
-    order = [s for group in groups for s in group]
+    group, direct, out_groups = row_groups(ep_count)
+    order = group + direct
     places = [[order.index(s) for s in group] for group in out_groups]
     bf16, f32, i32 = jnp.bfloat16, jnp.float32, jnp.int32
     gate_w, up_w, down_w = w_gate[0], w_up[0], w_down[0]
@@ -177,12 +210,18 @@
     blocks = [message]
     blocks += [swap(message, "ep", ep_count, s) for s in range(1, ep_count)]
     steps = range(1, tp_count)
-    owned, others = [], []
-    for group in groups:
-        shape = (len(group) * tok_rows, part)
-        held = tuple(blocks[s] for s in group)
-        owned += vmem_call(stack_kernel, [(shape, bf16)], held, 1000)
-        others.append([shift(owned[-1], "tp", tp_count, s) for s in steps])
+    shape = (len(group) * tok_rows, part // 2)
+    halves = vmem_call(stack_kernel, [(shape, bf16)] * 2, tuple(blocks[s] for s in group), 1000)
+    exchanged = []
+    for held in halves:
+        exchanged.append([shift(held, "tp", tp_count, d) for d in steps])
+    across = []
+    for s in direct:
+        across.append([diagonal(tokens, ep_count, tp_count, s, d) for d in steps])
+    others = [
+        [ref for d in steps for ref in (exchanged[h][d - 1], *[a[d - 1] for a in across])]
+        for h in range(2)
+    ]
     (counts,) = vmem_call(sum_kernel, [((tok_rows, width), i32)], tuple(blocks), 1000)
     swapped = jnp.zeros_like(counts)
     for bit in range(rep_count.bit_length() - 1):
@@ -190,13 +229,22 @@
         swapped = swap(counts, "rep", rep_count, 1 << bit)
     dot_flops = 2 * rows * part * ffe
     gate_acc, up_acc = vmem_call(
-        own_kernel, [((rows, ffe), f32)] * 2, (*owned, gate_w, up_w, down_w), 2 * dot_flops
+        own_kernel,
+        [((rows, ffe), f32)] * 2,
+        (*halves, *[blocks[s] for s in direct], gate_w, up_w, down_w),
+        2 * dot_flops,
+    )
+    gate_acc, up_acc = vmem_call(
+        functools.partial(early_kernel, tp_count),
+        [((rows, ffe), f32)] * 2,
+        (*others[0], gate_w, up_w, gate_acc, up_acc),
+        dot_flops,
     )
     hidden, *partials = vmem_call(
-        functools.partial(hidden_kernel, tp_count, len(groups), places),
+        functools.partial(hidden_kernel, tp_count, len(others[1]), places),
         [((rows, ffe), bf16)]
         + [((len(p) * tok_rows, part), bf16) for p in places] * len(steps),
-        (*[group[s - 1] for s in steps for group in others], gate_acc, up_acc, gate_w, up_w, down_w),
+        (*others[1], gate_acc, up_acc, gate_w, up_w, down_w),
         3 * len(steps) * dot_flops,
     )
     arrived = []
@@ -230,7 +278,7 @@
     half = ep_count // 2
     far = list(range(ep_count - 1, half, -1))
     near = list(range(1, half))
-    return [[0, half], far + near], [[half], far, near + [0]]
+    return [0, half] + near, far, [[half], far, near + [0]]
 
 
 def solution(mesh):

time: 34 us -> 38.1 us (1.12)
  starting transfers between devices: 18.5 us -> 20.9 us
  waiting for transfers between devices: 9.28 us -> 10.9 us
    ppermute x0 -> x1, waiting for transfers between devices: none -> 2.57 us  [diagonal(): return lax.ppermute(array, ('ep', 'tp'), pairs)]
    ppermute x0 -> x1, starting transfers between devices: none -> 2.4 us  [diagonal(): return lax.ppermute(array, ('ep', 'tp'), pairs)]
    ppermute x5, waiting for transfers between devices: 3.38 us -> 1.89 us  [shift(): lax.ppermute(array, axis, [(i, (i + step) % count) for i in range(count)])]
    ppermute x8, starting transfers between devices: 11.6 us -> 12.8 us  [swap(): return lax.ppermute(array, axis, [(i, i ^ span) for i in range(count)])]
    ppermute x5, starting transfers between devices: 6.9 us -> 5.67 us  [shift(): lax.ppermute(array, axis, [(i, (i + step) % count) for i in range(count)])]
    ppermute x8, waiting for transfers between devices: 5.9 us -> 6.41 us  [swap(): return lax.ppermute(array, axis, [(i, i ^ span) for i in range(count)])]
  transfers between devices with their start and end apart: 13 -> 14, of which waited for: 6 -> 8; matrix products, arithmetic and copies ran while one was open for 0% -> 0% of each run, Pallas kernels for 6% -> 7%
where the time goes in v5:
time: 38.1 us; the launch traced here: 38 us
  starting transfers between devices  20.9 us (55%)
  waiting for transfers between devices  10.9 us (29%)
  Pallas kernels  4.69 us (12%)
  between operations  0.77 us (2%)
  local copies, waits for them, and re-layouts  0.76 us (2%)
    ppermute x8, starting transfers between devices, swap(): return lax.ppermute(array, axis, [(i, i ^ span) for i in range(count)])  12.8 us
    ppermute x8, waiting for transfers between devices, swap(): return lax.ppermute(array, axis, [(i, i ^ span) for i in range(count)])  6.41 us
    ppermute x5, starting transfers between devices, shift(): lax.ppermute(array, axis, [(i, (i + step) % count) for i in range(count)])  5.67 us
    pallas_call x11, Pallas kernels, vmem_call(): pl.pallas_call(kernel, out_shape=[pltpu.VMEM(shape, dtype) for shape, dty...  3.92 us
    ppermute x1, waiting for transfers between devices, diagonal(): return lax.ppermute(array, ('ep', 'tp'), pairs)  2.57 us
    ppermute x1, starting transfers between devices, diagonal(): return lax.ppermute(array, ('ep', 'tp'), pairs)  2.4 us
    ppermute x5, waiting for transfers between devices, shift(): lax.ppermute(array, axis, [(i, (i + step) % count) for i in range(count)])  1.89 us
    pallas_call x1, Pallas kernels, per_device(): pl.pallas_call(combine_kernel, out_shape=[jax.ShapeDtypeStruct((tok_rows,...  0.77 us
  transfers between devices with their start and end apart: 14, of which 8 were waited for; matrix products, arithmetic and copies ran while one was open for 0% of the time, Pallas kernels for 7%

profile of v5, /device:TPU:0, one launch (start us, length us, event | category | flops | bytes accessed | tf_op | source)
XLA Modules:
  0.0 38.0 jit_solution(14309437346532603277)
XLA Ops:
  0.7 0.7 %copy-done.3 = bf16[8,3072]{1,0:T(8,128)(2,1)S(1)} copy-done((bf16[8,3072]{1,0:T(8,128)(2,1)S(1)}, bf16[8,3072]{1,0:T(8,128)(2,1)}, u32[]{:S(2)}) %copy-start.3) | copy-done | bytes 49176
  1.4 0.1 shard_map.87.refs_0_
  1.6 4.1 %collective-permute-start.1 = (bf16[8,3200]{1,0:T(8,128)(2,1)S(1)}, bf16[8,3200]{1,0:T(8,128)(2,1)S(1)}, u32[]{:S(2)}, u32[]{:S(2)}) collective-permute-start(bf16[8,3200]{1,0:T(8,128)(2,1)S(1)} %shard_map.87.refs_0_), channel_id=1, source_target_pairs={{0,4},{2,6},{4,0},{6,2},{1,5},{3,7},{5,1},{7,3},{8,12},{10,14},{12... | collective-permute-start | bytes 153608 | tf_op jit(solution)/shard_map/ppermute | solution.py:22
  5.7 1.6 %collective-permute-start = (bf16[8,3200]{1,0:T(8,128)(2,1)S(1)}, bf16[8,3200]{1,0:T(8,128)(2,1)S(1)}, u32[]{:S(2)}, u32[]{:S(2)}) collective-permute-start(bf16[8,3200]{1,0:T(8,128)(2,1)S(1)} %shard_map.87.refs_0_), channel_id=1, source_target_pairs={{0,2},{2,0},{4,6},{6,4},{1,3},{3,1},{5,7},{7,5},{8,10},{10,8},{12,... | collective-permute-start | bytes 153608 | tf_op jit(solution)/shard_map/ppermute | solution.py:22
  7.3 1.2 %collective-permute-done.1.refs_2_.refs_1_ = bf16[8,3200]{1,0:T(8,128)(2,1)S(1)} collective-permute-done((bf16[8,3200]{1,0:T(8,128)(2,1)S(1)}, bf16[8,3200]{1,0:T(8,128)(2,1)S(1)}, u32[]{:S(2)}, u32[]{:S(2)}) %collective-permute-start.1) | collective-permute-done | bytes 51232 | tf_op jit(solution)/shard_map/ppermute | solution.py:22
  8.5 1.4 %collective-permute-done.refs_1_.refs_2_ = bf16[8,3200]{1,0:T(8,128)(2,1)S(1)} collective-permute-done((bf16[8,3200]{1,0:T(8,128)(2,1)S(1)}, bf16[8,3200]{1,0:T(8,128)(2,1)S(1)}, u32[]{:S(2)}, u32[]{:S(2)}) %collective-permute-start) | collective-permute-done | bytes 51232 | tf_op jit(solution)/shard_map/ppermute | solution.py:22
  9.8 1.6 %collective-permute-start.7 = (bf16[24,1536]{1,0:T(8,128)(2,1)S(1)}, bf16[24,1536]{1,0:T(8,128)(2,1)S(1)}, u32[]{:S(2)}, u32[]{:S(2)}) collective-permute-start(bf16[24,1536]{1,0:T(8,128)(2,1)S(1)} %get-tuple-element.15.refs_0_), channel_id=1, source_target_pairs={{0,1},{1,0},{2,3},{3,2},{4,5},{5,4},{6,7},{7,6},{8,9},{9,8},{10,11... | collective-permute-start | bytes 221192 | tf_op jit(solution)/shard_map/ppermute | solution.py:18
  11.4 2.4 %collective-permute-start.2 = (bf16[8,3200]{1,0:T(8,128)(2,1)S(1)}, bf16[8,3200]{1,0:T(8,128)(2,1)S(1)}, u32[]{:S(2)}, u32[]{:S(2)}) collective-permute-start(bf16[8,3200]{1,0:T(8,128)(2,1)S(1)} %shard_map.87.refs_0_), channel_id=1, source_target_pairs={{0,6},{2,4},{4,2},{6,0},{1,7},{3,5},{5,3},{7,1},{8,14},{10,12},{12... | collective-permute-start | bytes 153608 | tf_op jit(solution)/shard_map/ppermute | solution.py:22
  13.7 0.5 %collective-permute-start.5 = (bf16[24,1536]{1,0:T(8,128)(2,1)S(1)}, bf16[24,1536]{1,0:T(8,128)(2,1)S(1)}, u32[]{:S(2)}, u32[]{:S(2)}) collective-permute-start(bf16[24,1536]{1,0:T(8,128)(2,1)S(1)} %get-tuple-element.14.refs_1_), channel_id=1, source_target_pairs={{0,1},{1,0},{2,3},{3,2},{4,5},{5,4},{6,7},{7,6},{8,9},{9,8},{10,11... | collective-permute-start | bytes 221192 | tf_op jit(solution)/shard_map/ppermute | solution.py:18
  14.3 2.4 %collective-permute-start.6 = (bf16[8,3072]{1,0:T(8,128)(2,1)S(1)}, bf16[8,3072]{1,0:T(8,128)(2,1)S(1)}, u32[]{:S(2)}, u32[]{:S(2)}) collective-permute-start(bf16[8,3072]{1,0:T(8,128)(2,1)S(1)} %copy-done.3), channel_id=1, source_target_pairs={{0,7},{1,6},{2,5},{3,4},{4,3},{5,2},{6,1},{7,0},{8,15},{9,14},{10,... | collective-permute-start | bytes 147464 | tf_op jit(solution)/shard_map/ppermute | solution.py:31
  16.7 0.6 %collective-permute-done.2.refs_3_.refs_2_ = bf16[8,3200]{1,0:T(8,128)(2,1)S(1)} collective-permute-done((bf16[8,3200]{1,0:T(8,128)(2,1)S(1)}, bf16[8,3200]{1,0:T(8,128)(2,1)S(1)}, u32[]{:S(2)}, u32[]{:S(2)}) %collective-permute-start.2) | collective-permute-done | bytes 51232 | tf_op jit(solution)/shard_map/ppermute | solution.py:22
  17.3 1.2 %shard_map.90 = (f32[32,512]{1,0:T(8,128)S(1)}, f32[32,512]{1,0:T(8,128)S(1)}) custom-call(bf16[24,1536]{1,0:T(8,128)(2,1)S(1)} %get-tuple-element.15.refs_0_, bf16[24,1536]{1,0:T(8,128)(2,1)S(1)} %get-tuple-element.14.refs_1_, bf16[8,3200]{1,0:T(8,128)(2,1)S(1)} %collective-permute-done.2.refs_3_.refs_2_, bf16[6144,512]{1,0:T(8,128)(2,1)S(1)} %bitcast.9, ...), custom_call_target="tpu_custom_call" | custom-call | flops 201326592 | bytes 1048576 | tf_op jit(solution)/shard_map/pallas_call | solution.py:175
  18.5 2.6 %collective-permute-done.6.refs_1_ = bf16[8,3072]{1,0:T(8,128)(2,1)S(1)} collective-permute-done((bf16[8,3072]{1,0:T(8,128)(2,1)S(1)}, bf16[8,3072]{1,0:T(8,128)(2,1)S(1)}, u32[]{:S(2)}, u32[]{:S(2)}) %collective-permute-start.6) | collective-permute-done | bytes 49184 | tf_op jit(solution)/shard_map/ppermute | solution.py:31
  21.1 0.0 collective-permute-done.7.refs_0_
  21.1 0.6 %shard_map.91 = (f32[32,512]{1,0:T(8,128)S(1)}, f32[32,512]{1,0:T(8,128)S(1)}) custom-call(bf16[24,1536]{1,0:T(8,128)(2,1)S(1)} %collective-permute-done.7.refs_0_, bf16[8,3072]{1,0:T(8,128)(2,1)S(1)} %collective-permute-done.6.refs_1_, bf16[6144,512]{1,0:T(8,128)(2,1)S(1)} %bitcast.10, bf16[6144,512]{1,0:T(8,128)(2,1)S(1)} %bitcast.13, ...), custom_call_target="tpu_custom_call" | custom-call | flops 100663296 | bytes 1048576 | tf_op jit(solution)/shard_map/pallas_call | solution.py:175
  21.7 0.0 collective-permute-done.5.refs_0_
  21.7 1.3 %shard_map.92 = (bf16[32,512]{1,0:T(8,128)(2,1)S(1)}, bf16[8,3072]{1,0:T(8,128)(2,1)S(1)}, bf16[8,3072]{1,0:T(8,128)(2,1)S(1)}, bf16[16,3072]{1,0:T(8,128)(2,1)S(1)}) custom-call(bf16[24,1536]{1,0:T(8,128)(2,1)S(1)} %collective-permute-done.5.refs_0_, bf16[8,3072]{1,0:T(8,128)(2,1)S(1)} %collective-permute-done.6.refs_1_, ...), custom_call_target="tpu_custom_call" | custom-call | flops 301989888 | bytes 1048576 | tf_op jit(solution)/shard_map/pallas_call | solution.py:175
  23.0 0.0 copy-start.5
  23.0 1.6 %collective-permute-start.8 = (bf16[16,3072]{1,0:T(8,128)(2,1)S(1)}, bf16[16,3072]{1,0:T(8,128)(2,1)S(1)}, u32[]{:S(2)}, u32[]{:S(2)}) collective-permute-start(bf16[16,3072]{1,0:T(8,128)(2,1)S(1)} %get-tuple-element.21), channel_id=1, source_target_pairs={{0,1},{1,0},{2,3},{3,2},{4,5},{5,4},{6,7},{7,6},{8,9},{9,8},{10,11... | collective-permute-start | bytes 294920 | tf_op jit(solution)/shard_map/ppermute | solution.py:18
  24.6 0.5 %collective-permute-start.10 = (bf16[8,3072]{1,0:T(8,128)(2,1)S(1)}, bf16[8,3072]{1,0:T(8,128)(2,1)S(1)}, u32[]{:S(2)}, u32[]{:S(2)}) collective-permute-start(bf16[8,3072]{1,0:T(8,128)(2,1)S(1)} %get-tuple-element.24), channel_id=1, source_target_pairs={{0,1},{1,0},{2,3},{3,2},{4,5},{5,4},{6,7},{7,6},{8,9},{9,8},{10,11... | collective-permute-start | bytes 147464 | tf_op jit(solution)/shard_map/ppermute | solution.py:18
  25.1 1.5 %collective-permute-start.12 = (bf16[8,3072]{1,0:T(8,128)(2,1)S(1)}, bf16[8,3072]{1,0:T(8,128)(2,1)S(1)}, u32[]{:S(2)}, u32[]{:S(2)}) collective-permute-start(bf16[8,3072]{1,0:T(8,128)(2,1)S(1)} %get-tuple-element.25), channel_id=1, source_target_pairs={{0,1},{1,0},{2,3},{3,2},{4,5},{5,4},{6,7},{7,6},{8,9},{9,8},{10,11... | collective-permute-start | bytes 147464 | tf_op jit(solution)/shard_map/ppermute | solution.py:18
  26.6 0.6 %shard_map.93.mine_ref = f32[32,3072]{1,0:T(8,128)S(1)} custom-call(bf16[32,512]{1,0:T(8,128)(2,1)S(1)} %get-tuple-element.20.hidden_ref, bf16[512,6144]{1,0:T(8,128)(2,1)S(1)} %bitcast.8), custom_call_target="tpu_custom_call" | custom-call | flops 100663296 | bytes 1048576 | tf_op jit(solution)/shard_map/pallas_call | solution.py:175
  27.2 1.4 %collective-permute-done.10.refs_0_ = bf16[8,3072]{1,0:T(8,128)(2,1)S(1)} collective-permute-done((bf16[8,3072]{1,0:T(8,128)(2,1)S(1)}, bf16[8,3072]{1,0:T(8,128)(2,1)S(1)}, u32[]{:S(2)}, u32[]{:S(2)}) %collective-permute-start.10) | collective-permute-done | bytes 49184 | tf_op jit(solution)/shard_map/ppermute | solution.py:18
  28.7 0.1 collective-permute-start.11
  28.8 0.4 %collective-permute-done.12.refs_0_ = bf16[8,3072]{1,0:T(8,128)(2,1)S(1)} collective-permute-done((bf16[8,3072]{1,0:T(8,128)(2,1)S(1)}, bf16[8,3072]{1,0:T(8,128)(2,1)S(1)}, u32[]{:S(2)}, u32[]{:S(2)}) %collective-permute-start.12) | collective-permute-done | bytes 49184 | tf_op jit(solution)/shard_map/ppermute | solution.py:18
  29.2 1.5 %collective-permute-start.13 = (bf16[8,3072]{1,0:T(8,128)(2,1)S(1)}, bf16[8,3072]{1,0:T(8,128)(2,1)S(1)}, u32[]{:S(2)}, u32[]{:S(2)}) collective-permute-start(bf16[8,3072]{1,0:T(8,128)(2,1)S(1)} %shard_map.96), channel_id=1, source_target_pairs={{0,6},{2,4},{4,2},{6,0},{1,7},{3,5},{5,3},{7,1},{8,14},{10,12},{12... | collective-permute-start | bytes 147464 | tf_op jit(solution)/shard_map/ppermute | solution.py:22
  30.8 1.6 %collective-permute-start.9 = (bf16[8,3072]{1,0:T(8,128)(2,1)S(1)}, bf16[8,3072]{1,0:T(8,128)(2,1)S(1)}, u32[]{:S(2)}, u32[]{:S(2)}) collective-permute-start(bf16[8,3072]{1,0:T(8,128)(2,1)S(1)} %get-tuple-element.23), channel_id=1, source_target_pairs={{0,2},{2,0},{4,6},{6,4},{1,3},{3,1},{5,7},{7,5},{8,10},{10,8},{12,... | collective-permute-start | bytes 147464 | tf_op jit(solution)/shard_map/ppermute | solution.py:22
  32.4 1.2 %collective-permute-done.3 = s32[8,128]{1,0:T(8,128)S(1)} collective-permute-done((s32[8,128]{1,0:T(8,128)S(1)}, s32[8,128]{1,0:T(8,128)S(1)}, u32[]{:S(2)}, u32[]{:S(2)}) %collective-permute-start.3) | collective-permute-done | bytes 4128 | tf_op jit(solution)/shard_map/ppermute | solution.py:22
  33.6 1.5 %collective-permute-start.4 = (s32[8,128]{1,0:T(8,128)S(1)}, s32[8,128]{1,0:T(8,128)S(1)}, u32[]{:S(2)}, u32[]{:S(2)}) collective-permute-start(s32[8,128]{1,0:T(8,128)S(1)} %add.3.sum_ref), channel_id=1, source_target_pairs={{0,16},{8,24},{16,0},{24,8},{1,17},{9,25},{17,1},{25,9},{2,18},{10... | collective-permute-start | bytes 12296 | tf_op jit(solution)/shard_map/ppermute | solution.py:22
  35.1 2.1 %collective-permute-done.4.swapped_ref = s32[8,128]{1,0:T(8,128)S(1)} collective-permute-done((s32[8,128]{1,0:T(8,128)S(1)}, s32[8,128]{1,0:T(8,128)S(1)}, u32[]{:S(2)}, u32[]{:S(2)}) %collective-permute-start.4) | collective-permute-done | bytes 4128 | tf_op jit(solution)/shard_map/ppermute | solution.py:22
  37.2 0.0 collective-permute-done.11.refs_2_
  37.2 0.8 %combine.1 = (bf16[8,3072]{1,0:T(8,128)(2,1)}, s32[4,4]{1,0:T(4,128)}) custom-call(s32[2,8]{1,0:T(2,128)S(1)} %bitcast.16, f32[2,8]{1,0:T(2,128)S(1)} %bitcast.17, s32[8,128]{1,0:T(8,128)S(1)} %add.3.sum_ref, s32[8,128]{1,0:T(8,128)S(1)} %collective-permute-done.4.swapped_ref, bf16[8,3072]{1,0:T(8,128)(2,1)S(1)} %get-tuple-element.22.refs_0_, ...), custom_call_target="tpu_custom_call" | custom-call | tf_op jit(solution)/shard_map/combine/pallas_call | solution.py:266
  (23 shorter events, 0.1 us)
Async XLA Ops:
  0.6 0.8 %copy-start.3 = (bf16[8,3072]{1,0:T(8,128)(2,1)S(1)}, bf16[8,3072]{1,0:T(8,128)(2,1)}, u32[]{:S(2)}) copy-start(bf16[8,3072]{1,0:T(8,128)(2,1)} %tokens_ref.1) | copy-start | bytes 147460
  0.6 0.8 %copy-start.6 = (s32[8,2]{0,1:T(2,128)S(1)}, s32[8,2]{0,1:T(2,128)}, u32[]{:S(2)}) copy-start(s32[8,2]{0,1:T(2,128)} %param.9) | copy-start | bytes 196
  0.7 0.8 %copy-start.4 = (s32[8,2]{0,1:T(2,128)S(1)}, s32[8,2]{0,1:T(2,128)}, u32[]{:S(2)}) copy-start(s32[8,2]{0,1:T(2,128)} %param.8) | copy-start | bytes 196
  0.7 16.7 %copy-start = (bf16[1,512,6144]{2,1,0:T(8,128)(2,1)S(1)}, bf16[1,512,6144]{2,1,0:T(8,128)(2,1)}, u32[]{:S(2)}) copy-start(bf16[1,512,6144]{2,1,0:T(8,128)(2,1)} %param.13) | copy-start | bytes 18874372
  0.7 16.6 %copy-start.2 = (bf16[1,6144,512]{2,1,0:T(8,128)(2,1)S(1)}, bf16[1,6144,512]{2,1,0:T(8,128)(2,1)}, u32[]{:S(2)}) copy-start(bf16[1,6144,512]{2,1,0:T(8,128)(2,1)} %param.12) | copy-start | bytes 18874372
  0.7 16.6 %copy-start.1 = (bf16[1,6144,512]{2,1,0:T(8,128)(2,1)S(1)}, bf16[1,6144,512]{2,1,0:T(8,128)(2,1)}, u32[]{:S(2)}) copy-start(bf16[1,6144,512]{2,1,0:T(8,128)(2,1)} %param.11) | copy-start | bytes 18874372
  1.6 6.9 %collective-permute-start.1 = (bf16[8,3200]{1,0:T(8,128)(2,1)S(1)}, bf16[8,3200]{1,0:T(8,128)(2,1)S(1)}, u32[]{:S(2)}, u32[]{:S(2)}) collective-permute-start(bf16[8,3200]{1,0:T(8,128)(2,1)S(1)} %shard_map.87.refs_0_), channel_id=1, source_target_pairs={{0,4},{2,6},{4,0},{6,2},{1,5},{3,7},{5,1},{7,3},{8,12},{10,14},{12... | collective-permute-start | bytes 153608 | tf_op jit(solution)/shard_map/ppermute | solution.py:22
  5.7 4.1 %collective-permute-start = (bf16[8,3200]{1,0:T(8,128)(2,1)S(1)}, bf16[8,3200]{1,0:T(8,128)(2,1)S(1)}, u32[]{:S(2)}, u32[]{:S(2)}) collective-permute-start(bf16[8,3200]{1,0:T(8,128)(2,1)S(1)} %shard_map.87.refs_0_), channel_id=1, source_target_pairs={{0,2},{2,0},{4,6},{6,4},{1,3},{3,1},{5,7},{7,5},{8,10},{10,8},{12,... | collective-permute-start | bytes 153608 | tf_op jit(solution)/shard_map/ppermute | solution.py:22
  9.8 11.2 %collective-permute-start.7 = (bf16[24,1536]{1,0:T(8,128)(2,1)S(1)}, bf16[24,1536]{1,0:T(8,128)(2,1)S(1)}, u32[]{:S(2)}, u32[]{:S(2)}) collective-permute-start(bf16[24,1536]{1,0:T(8,128)(2,1)S(1)} %get-tuple-element.15.refs_0_), channel_id=1, source_target_pairs={{0,1},{1,0},{2,3},{3,2},{4,5},{5,4},{6,7},{7,6},{8,9},{9,8},{10,11... | collective-permute-start | bytes 221192 | tf_op jit(solution)/shard_map/ppermute | solution.py:18
  11.4 5.9 %collective-permute-start.2 = (bf16[8,3200]{1,0:T(8,128)(2,1)S(1)}, bf16[8,3200]{1,0:T(8,128)(2,1)S(1)}, u32[]{:S(2)}, u32[]{:S(2)}) collective-permute-start(bf16[8,3200]{1,0:T(8,128)(2,1)S(1)} %shard_map.87.refs_0_), channel_id=1, source_target_pairs={{0,6},{2,4},{4,2},{6,0},{1,7},{3,5},{5,3},{7,1},{8,14},{10,12},{12... | collective-permute-start | bytes 153608 | tf_op jit(solution)/shard_map/ppermute | solution.py:22
  13.7 8.0 %collective-permute-start.5 = (bf16[24,1536]{1,0:T(8,128)(2,1)S(1)}, bf16[24,1536]{1,0:T(8,128)(2,1)S(1)}, u32[]{:S(2)}, u32[]{:S(2)}) collective-permute-start(bf16[24,1536]{1,0:T(8,128)(2,1)S(1)} %get-tuple-element.14.refs_1_), channel_id=1, source_target_pairs={{0,1},{1,0},{2,3},{3,2},{4,5},{5,4},{6,7},{7,6},{8,9},{9,8},{10,11... | collective-permute-start | bytes 221192 | tf_op jit(solution)/shard_map/ppermute | solution.py:18
  14.3 6.8 %collective-permute-start.6 = (bf16[8,3072]{1,0:T(8,128)(2,1)S(1)}, bf16[8,3072]{1,0:T(8,128)(2,1)S(1)}, u32[]{:S(2)}, u32[]{:S(2)}) collective-permute-start(bf16[8,3072]{1,0:T(8,128)(2,1)S(1)} %copy-done.3), channel_id=1, source_target_pairs={{0,7},{1,6},{2,5},{3,4},{4,3},{5,2},{6,1},{7,0},{8,15},{9,14},{10,... | collective-permute-start | bytes 147464 | tf_op jit(solution)/shard_map/ppermute | solution.py:31
  23.0 14.2 %copy-start.5 = (f32[8,2]{0,1:T(2,128)S(1)}, f32[8,2]{0,1:T(2,128)}, u32[]{:S(2)}) copy-start(f32[8,2]{0,1:T(2,128)} %param.10) | copy-start | bytes 196
  23.0 7.7 %collective-permute-start.8 = (bf16[16,3072]{1,0:T(8,128)(2,1)S(1)}, bf16[16,3072]{1,0:T(8,128)(2,1)S(1)}, u32[]{:S(2)}, u32[]{:S(2)}) collective-permute-start(bf16[16,3072]{1,0:T(8,128)(2,1)S(1)} %get-tuple-element.21), channel_id=1, source_target_pairs={{0,1},{1,0},{2,3},{3,2},{4,5},{5,4},{6,7},{7,6},{8,9},{9,8},{10,11... | collective-permute-start | bytes 294920 | tf_op jit(solution)/shard_map/ppermute | solution.py:18
  24.6 4.1 %collective-permute-start.10 = (bf16[8,3072]{1,0:T(8,128)(2,1)S(1)}, bf16[8,3072]{1,0:T(8,128)(2,1)S(1)}, u32[]{:S(2)}, u32[]{:S(2)}) collective-permute-start(bf16[8,3072]{1,0:T(8,128)(2,1)S(1)} %get-tuple-element.24), channel_id=1, source_target_pairs={{0,1},{1,0},{2,3},{3,2},{4,5},{5,4},{6,7},{7,6},{8,9},{9,8},{10,11... | collective-permute-start | bytes 147464 | tf_op jit(solution)/shard_map/ppermute | solution.py:18
  25.1 4.1 %collective-permute-start.12 = (bf16[8,3072]{1,0:T(8,128)(2,1)S(1)}, bf16[8,3072]{1,0:T(8,128)(2,1)S(1)}, u32[]{:S(2)}, u32[]{:S(2)}) collective-permute-start(bf16[8,3072]{1,0:T(8,128)(2,1)S(1)} %get-tuple-element.25), channel_id=1, source_target_pairs={{0,1},{1,0},{2,3},{3,2},{4,5},{5,4},{6,7},{7,6},{8,9},{9,8},{10,11... | collective-permute-start | bytes 147464 | tf_op jit(solution)/shard_map/ppermute | solution.py:18
  28.7 8.5 %collective-permute-start.11 = (bf16[8,3072]{1,0:T(8,128)(2,1)S(1)}, bf16[8,3072]{1,0:T(8,128)(2,1)S(1)}, u32[]{:S(2)}, u32[]{:S(2)}) collective-permute-start(bf16[8,3072]{1,0:T(8,128)(2,1)S(1)} %shard_map.95), channel_id=1, source_target_pairs={{0,4},{2,6},{4,0},{6,2},{1,5},{3,7},{5,1},{7,3},{8,12},{10,14},{12... | collective-permute-start | bytes 147464 | tf_op jit(solution)/shard_map/ppermute | solution.py:22
  29.2 8.0 %collective-permute-start.13 = (bf16[8,3072]{1,0:T(8,128)(2,1)S(1)}, bf16[8,3072]{1,0:T(8,128)(2,1)S(1)}, u32[]{:S(2)}, u32[]{:S(2)}) collective-permute-start(bf16[8,3072]{1,0:T(8,128)(2,1)S(1)} %shard_map.96), channel_id=1, source_target_pairs={{0,6},{2,4},{4,2},{6,0},{1,7},{3,5},{5,3},{7,1},{8,14},{10,12},{12... | collective-permute-start | bytes 147464 | tf_op jit(solution)/shard_map/ppermute | solution.py:22
  30.8 6.4 %collective-permute-start.9 = (bf16[8,3072]{1,0:T(8,128)(2,1)S(1)}, bf16[8,3072]{1,0:T(8,128)(2,1)S(1)}, u32[]{:S(2)}, u32[]{:S(2)}) collective-permute-start(bf16[8,3072]{1,0:T(8,128)(2,1)S(1)} %get-tuple-element.23), channel_id=1, source_target_pairs={{0,2},{2,0},{4,6},{6,4},{1,3},{3,1},{5,7},{7,5},{8,10},{10,8},{12,... | collective-permute-start | bytes 147464 | tf_op jit(solution)/shard_map/ppermute | solution.py:22
  32.4 1.2 %collective-permute-start.3 = (s32[8,128]{1,0:T(8,128)S(1)}, s32[8,128]{1,0:T(8,128)S(1)}, u32[]{:S(2)}, u32[]{:S(2)}) collective-permute-start(s32[8,128]{1,0:T(8,128)S(1)} %shard_map.88), channel_id=1, source_target_pairs={{0,8},{8,0},{16,24},{24,16},{1,9},{9,1},{17,25},{25,17},{2,10},{10... | collective-permute-start | bytes 12296 | tf_op jit(solution)/shard_map/ppermute | solution.py:22
  33.6 3.6 %collective-permute-start.4 = (s32[8,128]{1,0:T(8,128)S(1)}, s32[8,128]{1,0:T(8,128)S(1)}, u32[]{:S(2)}, u32[]{:S(2)}) collective-permute-start(s32[8,128]{1,0:T(8,128)S(1)} %add.3.sum_ref), channel_id=1, source_target_pairs={{0,16},{8,24},{16,0},{24,8},{1,17},{9,25},{17,1},{25,9},{2,18},{10... | collective-permute-start | bytes 12296 | tf_op jit(solution)/shard_map/ppermute | solution.py:22

commit v6 on v5

--- a/solution.py
+++ b/solution.py
@@ -147,23 +147,33 @@
         out[...] = total.astype(jnp.bfloat16)
 
 
-def combine_kernel(ids_ref, scores_ref, sum_ref, swapped_ref, *refs):
-    pieces, (out_ref, counts_ref) = refs[:-2], refs[-2:]
-    ep_count = len(pieces)
-    tok_rows, part = out_ref.shape
+def coefficient_kernel(ids_ref, scores_ref, out_ref):
+    tok_rows = ids_ref.shape[1]
     me = lax.axis_index("ep")
     gains = jax.nn.sigmoid(scores_ref[...])
     weights = gains / jnp.sum(gains, 0, keepdims=True) * route_scale
     ids = ids_ref[...]
-    total = jnp.zeros((tok_rows, part), jnp.float32)
     diagonal = lax.broadcasted_iota(jnp.int32, (tok_rows, tok_rows), 0) == (
         lax.broadcasted_iota(jnp.int32, (tok_rows, tok_rows), 1)
     )
-    for s, piece in enumerate(pieces):
+    for s in range(out_ref.shape[0] // tok_rows):
         row = jnp.sum(jnp.where(ids == (me ^ s), weights, 0.0), 0, keepdims=True)
         column = jnp.sum(jnp.where(diagonal, row, 0.0), 1, keepdims=True)
-        total += column * piece[...].astype(jnp.float32)
-    out_ref[...] = total.astype(jnp.bfloat16)
+        out_ref[pl.ds(s * tok_rows, tok_rows), :] = jnp.broadcast_to(column, (tok_rows, LANES))
+
+
+def combine_kernel(coefficient_ref, sum_ref, swapped_ref, *refs):
+    pieces, (out_ref, counts_ref) = refs[:-2], refs[-2:]
+    ep_count = len(pieces)
+    tok_rows, part = out_ref.shape
+    coefficients = [
+        coefficient_ref[pl.ds(s * tok_rows, tok_rows), :] for s in range(ep_count)
+    ]
+    for lane in range(0, part, LANES):
+        total = 0.0
+        for coefficient, piece in zip(coefficients, pieces):
+            total += coefficient * piece[:, lane : lane + LANES].astype(jnp.float32)
+        out_ref[:, lane : lane + LANES] = total.astype(jnp.bfloat16)
     counts = sum_ref[...] + swapped_ref[...]
     for group in range(0, counts_ref.shape[0], tok_rows):
         size = min(tok_rows, counts_ref.shape[0] - group)
@@ -226,7 +236,7 @@
     swapped = jnp.zeros_like(counts)
     for bit in range(rep_count.bit_length() - 1):
         counts = counts + swapped
-        swapped = swap(counts, "rep", rep_count, 1 << bit)
+        swapped = swap(counts, "rep", rep_count, rep_count >> (bit + 1))
     dot_flops = 2 * rows * part * ffe
     gate_acc, up_acc = vmem_call(
         own_kernel,
@@ -263,6 +273,7 @@
         )
         for s, piece in zip(group, outgoing):
             back[s] = swap(piece, "ep", ep_count, s) if s else piece
+    (coefficients,) = vmem_call(coefficient_kernel, [((rows, LANES), f32)], (ids, gains), 1000)
     return pl.pallas_call(
         combine_kernel,
         out_shape=[
@@ -271,7 +282,7 @@
         ],
         compiler_params=pltpu.CompilerParams(vmem_limit_bytes=8 * MIB),
         name="combine",
-    )(ids, gains, counts, swapped, *back)
+    )(coefficients, counts, swapped, *back)
 
 
 def row_groups(ep_count):

time: 38.1 us -> 38 us (level)
    pallas_call x11 -> x12, Pallas kernels: 3.92 us -> 4.03 us  [vmem_call(): pl.pallas_call(kernel, out_shape=[pltpu.VMEM(shape, dtype) for shape, dty...]
where the time goes in v6:
time: 38 us; the launch traced here: 37.9 us
  starting transfers between devices  20.9 us (55%)
  waiting for transfers between devices  10.8 us (28%)
  Pallas kernels  4.7 us (12%)
  local copies, waits for them, and re-layouts  0.76 us (2%)
  between operations  0.76 us (2%)
    ppermute x8, starting transfers between devices, swap(): return lax.ppermute(array, axis, [(i, i ^ span) for i in range(count)])  12.8 us
    ppermute x8, waiting for transfers between devices, swap(): return lax.ppermute(array, axis, [(i, i ^ span) for i in range(count)])  6.31 us
    ppermute x5, starting transfers between devices, shift(): lax.ppermute(array, axis, [(i, (i + step) % count) for i in range(count)])  5.67 us
    pallas_call x12, Pallas kernels, vmem_call(): pl.pallas_call(kernel, out_shape=[pltpu.VMEM(shape, dtype) for shape, dty...  4.03 us
    ppermute x1, waiting for transfers between devices, diagonal(): return lax.ppermute(array, ('ep', 'tp'), pairs)  2.57 us
    ppermute x1, starting transfers between devices, diagonal(): return lax.ppermute(array, ('ep', 'tp'), pairs)  2.4 us
    ppermute x5, waiting for transfers between devices, shift(): lax.ppermute(array, axis, [(i, (i + step) % count) for i in range(count)])  1.89 us
  transfers between devices with their start and end apart: 14, of which 8 were waited for; matrix products, arithmetic and copies ran while one was open for 0% of the time, Pallas kernels for 7%

profile of v6, /device:TPU:0, one launch (start us, length us, event | category | flops | bytes accessed | tf_op | source)
XLA Modules:
  0.0 37.9 jit_solution(10305794693126649777)
XLA Ops:
  0.7 0.7 %copy-done.3 = bf16[8,3072]{1,0:T(8,128)(2,1)S(1)} copy-done((bf16[8,3072]{1,0:T(8,128)(2,1)S(1)}, bf16[8,3072]{1,0:T(8,128)(2,1)}, u32[]{:S(2)}) %copy-start.3) | copy-done | bytes 49176
  1.4 0.1 shard_map.88.refs_0_
  1.6 4.1 %collective-permute-start.1 = (bf16[8,3200]{1,0:T(8,128)(2,1)S(1)}, bf16[8,3200]{1,0:T(8,128)(2,1)S(1)}, u32[]{:S(2)}, u32[]{:S(2)}) collective-permute-start(bf16[8,3200]{1,0:T(8,128)(2,1)S(1)} %shard_map.88.refs_0_), channel_id=1, source_target_pairs={{0,4},{2,6},{4,0},{6,2},{1,5},{3,7},{5,1},{7,3},{8,12},{10,14},{12... | collective-permute-start | bytes 153608 | tf_op jit(solution)/shard_map/ppermute | solution.py:22
  5.7 1.6 %collective-permute-start = (bf16[8,3200]{1,0:T(8,128)(2,1)S(1)}, bf16[8,3200]{1,0:T(8,128)(2,1)S(1)}, u32[]{:S(2)}, u32[]{:S(2)}) collective-permute-start(bf16[8,3200]{1,0:T(8,128)(2,1)S(1)} %shard_map.88.refs_0_), channel_id=1, source_target_pairs={{0,2},{2,0},{4,6},{6,4},{1,3},{3,1},{5,7},{7,5},{8,10},{10,8},{12,... | collective-permute-start | bytes 153608 | tf_op jit(solution)/shard_map/ppermute | solution.py:22
  7.3 1.2 %collective-permute-done.1.refs_2_.refs_1_ = bf16[8,3200]{1,0:T(8,128)(2,1)S(1)} collective-permute-done((bf16[8,3200]{1,0:T(8,128)(2,1)S(1)}, bf16[8,3200]{1,0:T(8,128)(2,1)S(1)}, u32[]{:S(2)}, u32[]{:S(2)}) %collective-permute-start.1) | collective-permute-done | bytes 51232 | tf_op jit(solution)/shard_map/ppermute | solution.py:22
  8.5 1.4 %collective-permute-done.refs_1_.refs_2_ = bf16[8,3200]{1,0:T(8,128)(2,1)S(1)} collective-permute-done((bf16[8,3200]{1,0:T(8,128)(2,1)S(1)}, bf16[8,3200]{1,0:T(8,128)(2,1)S(1)}, u32[]{:S(2)}, u32[]{:S(2)}) %collective-permute-start) | collective-permute-done | bytes 51232 | tf_op jit(solution)/shard_map/ppermute | solution.py:22
  9.8 1.6 %collective-permute-start.7 = (bf16[24,1536]{1,0:T(8,128)(2,1)S(1)}, bf16[24,1536]{1,0:T(8,128)(2,1)S(1)}, u32[]{:S(2)}, u32[]{:S(2)}) collective-permute-start(bf16[24,1536]{1,0:T(8,128)(2,1)S(1)} %get-tuple-element.15.refs_0_), channel_id=1, source_target_pairs={{0,1},{1,0},{2,3},{3,2},{4,5},{5,4},{6,7},{7,6},{8,9},{9,8},{10,11... | collective-permute-start | bytes 221192 | tf_op jit(solution)/shard_map/ppermute | solution.py:18
  11.4 2.4 %collective-permute-start.2 = (bf16[8,3200]{1,0:T(8,128)(2,1)S(1)}, bf16[8,3200]{1,0:T(8,128)(2,1)S(1)}, u32[]{:S(2)}, u32[]{:S(2)}) collective-permute-start(bf16[8,3200]{1,0:T(8,128)(2,1)S(1)} %shard_map.88.refs_0_), channel_id=1, source_target_pairs={{0,6},{2,4},{4,2},{6,0},{1,7},{3,5},{5,3},{7,1},{8,14},{10,12},{12... | collective-permute-start | bytes 153608 | tf_op jit(solution)/shard_map/ppermute | solution.py:22
  13.7 0.5 %collective-permute-start.5 = (bf16[24,1536]{1,0:T(8,128)(2,1)S(1)}, bf16[24,1536]{1,0:T(8,128)(2,1)S(1)}, u32[]{:S(2)}, u32[]{:S(2)}) collective-permute-start(bf16[24,1536]{1,0:T(8,128)(2,1)S(1)} %get-tuple-element.14.refs_1_), channel_id=1, source_target_pairs={{0,1},{1,0},{2,3},{3,2},{4,5},{5,4},{6,7},{7,6},{8,9},{9,8},{10,11... | collective-permute-start | bytes 221192 | tf_op jit(solution)/shard_map/ppermute | solution.py:18
  14.3 2.4 %collective-permute-start.6 = (bf16[8,3072]{1,0:T(8,128)(2,1)S(1)}, bf16[8,3072]{1,0:T(8,128)(2,1)S(1)}, u32[]{:S(2)}, u32[]{:S(2)}) collective-permute-start(bf16[8,3072]{1,0:T(8,128)(2,1)S(1)} %copy-done.3), channel_id=1, source_target_pairs={{0,7},{1,6},{2,5},{3,4},{4,3},{5,2},{6,1},{7,0},{8,15},{9,14},{10,... | collective-permute-start | bytes 147464 | tf_op jit(solution)/shard_map/ppermute | solution.py:31
  16.7 0.6 %collective-permute-done.2.refs_3_.refs_2_ = bf16[8,3200]{1,0:T(8,128)(2,1)S(1)} collective-permute-done((bf16[8,3200]{1,0:T(8,128)(2,1)S(1)}, bf16[8,3200]{1,0:T(8,128)(2,1)S(1)}, u32[]{:S(2)}, u32[]{:S(2)}) %collective-permute-start.2) | collective-permute-done | bytes 51232 | tf_op jit(solution)/shard_map/ppermute | solution.py:22
  17.3 1.2 %shard_map.91 = (f32[32,512]{1,0:T(8,128)S(1)}, f32[32,512]{1,0:T(8,128)S(1)}) custom-call(bf16[24,1536]{1,0:T(8,128)(2,1)S(1)} %get-tuple-element.15.refs_0_, bf16[24,1536]{1,0:T(8,128)(2,1)S(1)} %get-tuple-element.14.refs_1_, bf16[8,3200]{1,0:T(8,128)(2,1)S(1)} %collective-permute-done.2.refs_3_.refs_2_, bf16[6144,512]{1,0:T(8,128)(2,1)S(1)} %bitcast.9, ...), custom_call_target="tpu_custom_call" | custom-call | flops 201326592 | bytes 1048576 | tf_op jit(solution)/shard_map/pallas_call | solution.py:185
  18.5 2.6 %collective-permute-done.6.refs_1_ = bf16[8,3072]{1,0:T(8,128)(2,1)S(1)} collective-permute-done((bf16[8,3072]{1,0:T(8,128)(2,1)S(1)}, bf16[8,3072]{1,0:T(8,128)(2,1)S(1)}, u32[]{:S(2)}, u32[]{:S(2)}) %collective-permute-start.6) | collective-permute-done | bytes 49184 | tf_op jit(solution)/shard_map/ppermute | solution.py:31
  21.1 0.0 collective-permute-done.7.refs_0_
  21.1 0.6 %shard_map.92 = (f32[32,512]{1,0:T(8,128)S(1)}, f32[32,512]{1,0:T(8,128)S(1)}) custom-call(bf16[24,1536]{1,0:T(8,128)(2,1)S(1)} %collective-permute-done.7.refs_0_, bf16[8,3072]{1,0:T(8,128)(2,1)S(1)} %collective-permute-done.6.refs_1_, bf16[6144,512]{1,0:T(8,128)(2,1)S(1)} %bitcast.10, bf16[6144,512]{1,0:T(8,128)(2,1)S(1)} %bitcast.13, ...), custom_call_target="tpu_custom_call" | custom-call | flops 100663296 | bytes 1048576 | tf_op jit(solution)/shard_map/pallas_call | solution.py:185
  21.7 0.0 collective-permute-done.5.refs_0_
  21.7 1.3 %shard_map.93 = (bf16[32,512]{1,0:T(8,128)(2,1)S(1)}, bf16[8,3072]{1,0:T(8,128)(2,1)S(1)}, bf16[8,3072]{1,0:T(8,128)(2,1)S(1)}, bf16[16,3072]{1,0:T(8,128)(2,1)S(1)}) custom-call(bf16[24,1536]{1,0:T(8,128)(2,1)S(1)} %collective-permute-done.5.refs_0_, bf16[8,3072]{1,0:T(8,128)(2,1)S(1)} %collective-permute-done.6.refs_1_, ...), custom_call_target="tpu_custom_call" | custom-call | flops 301989888 | bytes 1048576 | tf_op jit(solution)/shard_map/pallas_call | solution.py:185
  23.0 0.0 copy-start.5
  23.0 1.6 %collective-permute-start.8 = (bf16[16,3072]{1,0:T(8,128)(2,1)S(1)}, bf16[16,3072]{1,0:T(8,128)(2,1)S(1)}, u32[]{:S(2)}, u32[]{:S(2)}) collective-permute-start(bf16[16,3072]{1,0:T(8,128)(2,1)S(1)} %get-tuple-element.21), channel_id=1, source_target_pairs={{0,1},{1,0},{2,3},{3,2},{4,5},{5,4},{6,7},{7,6},{8,9},{9,8},{10,11... | collective-permute-start | bytes 294920 | tf_op jit(solution)/shard_map/ppermute | solution.py:18
  24.6 0.5 %collective-permute-start.10 = (bf16[8,3072]{1,0:T(8,128)(2,1)S(1)}, bf16[8,3072]{1,0:T(8,128)(2,1)S(1)}, u32[]{:S(2)}, u32[]{:S(2)}) collective-permute-start(bf16[8,3072]{1,0:T(8,128)(2,1)S(1)} %get-tuple-element.24), channel_id=1, source_target_pairs={{0,1},{1,0},{2,3},{3,2},{4,5},{5,4},{6,7},{7,6},{8,9},{9,8},{10,11... | collective-permute-start | bytes 147464 | tf_op jit(solution)/shard_map/ppermute | solution.py:18
  25.1 1.5 %collective-permute-start.12 = (bf16[8,3072]{1,0:T(8,128)(2,1)S(1)}, bf16[8,3072]{1,0:T(8,128)(2,1)S(1)}, u32[]{:S(2)}, u32[]{:S(2)}) collective-permute-start(bf16[8,3072]{1,0:T(8,128)(2,1)S(1)} %get-tuple-element.25), channel_id=1, source_target_pairs={{0,1},{1,0},{2,3},{3,2},{4,5},{5,4},{6,7},{7,6},{8,9},{9,8},{10,11... | collective-permute-start | bytes 147464 | tf_op jit(solution)/shard_map/ppermute | solution.py:18
  26.6 0.6 %shard_map.94.mine_ref = f32[32,3072]{1,0:T(8,128)S(1)} custom-call(bf16[32,512]{1,0:T(8,128)(2,1)S(1)} %get-tuple-element.20.hidden_ref, bf16[512,6144]{1,0:T(8,128)(2,1)S(1)} %bitcast.8), custom_call_target="tpu_custom_call" | custom-call | flops 100663296 | bytes 1048576 | tf_op jit(solution)/shard_map/pallas_call | solution.py:185
  27.2 1.4 %collective-permute-done.10.refs_0_ = bf16[8,3072]{1,0:T(8,128)(2,1)S(1)} collective-permute-done((bf16[8,3072]{1,0:T(8,128)(2,1)S(1)}, bf16[8,3072]{1,0:T(8,128)(2,1)S(1)}, u32[]{:S(2)}, u32[]{:S(2)}) %collective-permute-start.10) | collective-permute-done | bytes 49184 | tf_op jit(solution)/shard_map/ppermute | solution.py:18
  28.7 0.1 collective-permute-start.11
  28.8 0.4 %collective-permute-done.12.refs_0_ = bf16[8,3072]{1,0:T(8,128)(2,1)S(1)} collective-permute-done((bf16[8,3072]{1,0:T(8,128)(2,1)S(1)}, bf16[8,3072]{1,0:T(8,128)(2,1)S(1)}, u32[]{:S(2)}, u32[]{:S(2)}) %collective-permute-start.12) | collective-permute-done | bytes 49184 | tf_op jit(solution)/shard_map/ppermute | solution.py:18
  29.2 1.5 %collective-permute-start.13 = (bf16[8,3072]{1,0:T(8,128)(2,1)S(1)}, bf16[8,3072]{1,0:T(8,128)(2,1)S(1)}, u32[]{:S(2)}, u32[]{:S(2)}) collective-permute-start(bf16[8,3072]{1,0:T(8,128)(2,1)S(1)} %shard_map.97), channel_id=1, source_target_pairs={{0,6},{2,4},{4,2},{6,0},{1,7},{3,5},{5,3},{7,1},{8,14},{10,12},{12... | collective-permute-start | bytes 147464 | tf_op jit(solution)/shard_map/ppermute | solution.py:22
  30.8 1.6 %collective-permute-start.9 = (bf16[8,3072]{1,0:T(8,128)(2,1)S(1)}, bf16[8,3072]{1,0:T(8,128)(2,1)S(1)}, u32[]{:S(2)}, u32[]{:S(2)}) collective-permute-start(bf16[8,3072]{1,0:T(8,128)(2,1)S(1)} %get-tuple-element.23), channel_id=1, source_target_pairs={{0,2},{2,0},{4,6},{6,4},{1,3},{3,1},{5,7},{7,5},{8,10},{10,8},{12,... | collective-permute-start | bytes 147464 | tf_op jit(solution)/shard_map/ppermute | solution.py:22
  32.4 1.5 %collective-permute-start.3 = (s32[8,128]{1,0:T(8,128)S(1)}, s32[8,128]{1,0:T(8,128)S(1)}, u32[]{:S(2)}, u32[]{:S(2)}) collective-permute-start(s32[8,128]{1,0:T(8,128)S(1)} %shard_map.89), channel_id=1, source_target_pairs={{0,16},{8,24},{16,0},{24,8},{1,17},{9,25},{17,1},{25,9},{2,18},{10... | collective-permute-start | bytes 12296 | tf_op jit(solution)/shard_map/ppermute | solution.py:22
  33.9 2.1 %collective-permute-done.3 = s32[8,128]{1,0:T(8,128)S(1)} collective-permute-done((s32[8,128]{1,0:T(8,128)S(1)}, s32[8,128]{1,0:T(8,128)S(1)}, u32[]{:S(2)}, u32[]{:S(2)}) %collective-permute-start.3) | collective-permute-done | bytes 4128 | tf_op jit(solution)/shard_map/ppermute | solution.py:22
  36.0 0.1 shard_map.86.coefficient_ref
  36.1 1.1 %collective-permute-done.4.swapped_ref = s32[8,128]{1,0:T(8,128)S(1)} collective-permute-done((s32[8,128]{1,0:T(8,128)S(1)}, s32[8,128]{1,0:T(8,128)S(1)}, u32[]{:S(2)}, u32[]{:S(2)}) %collective-permute-start.4) | collective-permute-done | bytes 4128 | tf_op jit(solution)/shard_map/ppermute | solution.py:22
  37.2 0.7 %combine.1 = (bf16[8,3072]{1,0:T(8,128)(2,1)}, s32[4,4]{1,0:T(4,128)}) custom-call(f32[32,128]{1,0:T(8,128)S(1)} %shard_map.86.coefficient_ref, s32[8,128]{1,0:T(8,128)S(1)} %add.3.sum_ref, s32[8,128]{1,0:T(8,128)S(1)} %collective-permute-done.4.swapped_ref, bf16[8,3072]{1,0:T(8,128)(2,1)S(1)} %get-tuple-element.22.refs_0_, ...), custom_call_target="tpu_custom_call" | custom-call | tf_op jit(solution)/shard_map/combine/pallas_call | solution.py:277
  (24 shorter events, 0.1 us)
Async XLA Ops:
  0.6 0.8 %copy-start.3 = (bf16[8,3072]{1,0:T(8,128)(2,1)S(1)}, bf16[8,3072]{1,0:T(8,128)(2,1)}, u32[]{:S(2)}) copy-start(bf16[8,3072]{1,0:T(8,128)(2,1)} %tokens_ref.1) | copy-start | bytes 147460
  0.6 0.8 %copy-start.6 = (s32[8,2]{0,1:T(2,128)S(1)}, s32[8,2]{0,1:T(2,128)}, u32[]{:S(2)}) copy-start(s32[8,2]{0,1:T(2,128)} %param.9) | copy-start | bytes 196
  0.7 0.8 %copy-start.4 = (s32[8,2]{0,1:T(2,128)S(1)}, s32[8,2]{0,1:T(2,128)}, u32[]{:S(2)}) copy-start(s32[8,2]{0,1:T(2,128)} %param.8) | copy-start | bytes 196
  0.7 16.7 %copy-start = (bf16[1,512,6144]{2,1,0:T(8,128)(2,1)S(1)}, bf16[1,512,6144]{2,1,0:T(8,128)(2,1)}, u32[]{:S(2)}) copy-start(bf16[1,512,6144]{2,1,0:T(8,128)(2,1)} %param.13) | copy-start | bytes 18874372
  0.7 16.6 %copy-start.2 = (bf16[1,6144,512]{2,1,0:T(8,128)(2,1)S(1)}, bf16[1,6144,512]{2,1,0:T(8,128)(2,1)}, u32[]{:S(2)}) copy-start(bf16[1,6144,512]{2,1,0:T(8,128)(2,1)} %param.12) | copy-start | bytes 18874372
  0.7 16.6 %copy-start.1 = (bf16[1,6144,512]{2,1,0:T(8,128)(2,1)S(1)}, bf16[1,6144,512]{2,1,0:T(8,128)(2,1)}, u32[]{:S(2)}) copy-start(bf16[1,6144,512]{2,1,0:T(8,128)(2,1)} %param.11) | copy-start | bytes 18874372
  1.6 6.9 %collective-permute-start.1 = (bf16[8,3200]{1,0:T(8,128)(2,1)S(1)}, bf16[8,3200]{1,0:T(8,128)(2,1)S(1)}, u32[]{:S(2)}, u32[]{:S(2)}) collective-permute-start(bf16[8,3200]{1,0:T(8,128)(2,1)S(1)} %shard_map.88.refs_0_), channel_id=1, source_target_pairs={{0,4},{2,6},{4,0},{6,2},{1,5},{3,7},{5,1},{7,3},{8,12},{10,14},{12... | collective-permute-start | bytes 153608 | tf_op jit(solution)/shard_map/ppermute | solution.py:22
  5.7 4.1 %collective-permute-start = (bf16[8,3200]{1,0:T(8,128)(2,1)S(1)}, bf16[8,3200]{1,0:T(8,128)(2,1)S(1)}, u32[]{:S(2)}, u32[]{:S(2)}) collective-permute-start(bf16[8,3200]{1,0:T(8,128)(2,1)S(1)} %shard_map.88.refs_0_), channel_id=1, source_target_pairs={{0,2},{2,0},{4,6},{6,4},{1,3},{3,1},{5,7},{7,5},{8,10},{10,8},{12,... | collective-permute-start | bytes 153608 | tf_op jit(solution)/shard_map/ppermute | solution.py:22
  9.8 11.2 %collective-permute-start.7 = (bf16[24,1536]{1,0:T(8,128)(2,1)S(1)}, bf16[24,1536]{1,0:T(8,128)(2,1)S(1)}, u32[]{:S(2)}, u32[]{:S(2)}) collective-permute-start(bf16[24,1536]{1,0:T(8,128)(2,1)S(1)} %get-tuple-element.15.refs_0_), channel_id=1, source_target_pairs={{0,1},{1,0},{2,3},{3,2},{4,5},{5,4},{6,7},{7,6},{8,9},{9,8},{10,11... | collective-permute-start | bytes 221192 | tf_op jit(solution)/shard_map/ppermute | solution.py:18
  11.4 5.9 %collective-permute-start.2 = (bf16[8,3200]{1,0:T(8,128)(2,1)S(1)}, bf16[8,3200]{1,0:T(8,128)(2,1)S(1)}, u32[]{:S(2)}, u32[]{:S(2)}) collective-permute-start(bf16[8,3200]{1,0:T(8,128)(2,1)S(1)} %shard_map.88.refs_0_), channel_id=1, source_target_pairs={{0,6},{2,4},{4,2},{6,0},{1,7},{3,5},{5,3},{7,1},{8,14},{10,12},{12... | collective-permute-start | bytes 153608 | tf_op jit(solution)/shard_map/ppermute | solution.py:22
  13.7 8.0 %collective-permute-start.5 = (bf16[24,1536]{1,0:T(8,128)(2,1)S(1)}, bf16[24,1536]{1,0:T(8,128)(2,1)S(1)}, u32[]{:S(2)}, u32[]{:S(2)}) collective-permute-start(bf16[24,1536]{1,0:T(8,128)(2,1)S(1)} %get-tuple-element.14.refs_1_), channel_id=1, source_target_pairs={{0,1},{1,0},{2,3},{3,2},{4,5},{5,4},{6,7},{7,6},{8,9},{9,8},{10,11... | collective-permute-start | bytes 221192 | tf_op jit(solution)/shard_map/ppermute | solution.py:18
  14.3 6.8 %collective-permute-start.6 = (bf16[8,3072]{1,0:T(8,128)(2,1)S(1)}, bf16[8,3072]{1,0:T(8,128)(2,1)S(1)}, u32[]{:S(2)}, u32[]{:S(2)}) collective-permute-start(bf16[8,3072]{1,0:T(8,128)(2,1)S(1)} %copy-done.3), channel_id=1, source_target_pairs={{0,7},{1,6},{2,5},{3,4},{4,3},{5,2},{6,1},{7,0},{8,15},{9,14},{10,... | collective-permute-start | bytes 147464 | tf_op jit(solution)/shard_map/ppermute | solution.py:31
  23.0 13.0 %copy-start.5 = (f32[8,2]{0,1:T(2,128)S(1)}, f32[8,2]{0,1:T(2,128)}, u32[]{:S(2)}) copy-start(f32[8,2]{0,1:T(2,128)} %param.10) | copy-start | bytes 196
  23.0 7.7 %collective-permute-start.8 = (bf16[16,3072]{1,0:T(8,128)(2,1)S(1)}, bf16[16,3072]{1,0:T(8,128)(2,1)S(1)}, u32[]{:S(2)}, u32[]{:S(2)}) collective-permute-start(bf16[16,3072]{1,0:T(8,128)(2,1)S(1)} %get-tuple-element.21), channel_id=1, source_target_pairs={{0,1},{1,0},{2,3},{3,2},{4,5},{5,4},{6,7},{7,6},{8,9},{9,8},{10,11... | collective-permute-start | bytes 294920 | tf_op jit(solution)/shard_map/ppermute | solution.py:18
  24.6 4.1 %collective-permute-start.10 = (bf16[8,3072]{1,0:T(8,128)(2,1)S(1)}, bf16[8,3072]{1,0:T(8,128)(2,1)S(1)}, u32[]{:S(2)}, u32[]{:S(2)}) collective-permute-start(bf16[8,3072]{1,0:T(8,128)(2,1)S(1)} %get-tuple-element.24), channel_id=1, source_target_pairs={{0,1},{1,0},{2,3},{3,2},{4,5},{5,4},{6,7},{7,6},{8,9},{9,8},{10,11... | collective-permute-start | bytes 147464 | tf_op jit(solution)/shard_map/ppermute | solution.py:18
  25.1 4.1 %collective-permute-start.12 = (bf16[8,3072]{1,0:T(8,128)(2,1)S(1)}, bf16[8,3072]{1,0:T(8,128)(2,1)S(1)}, u32[]{:S(2)}, u32[]{:S(2)}) collective-permute-start(bf16[8,3072]{1,0:T(8,128)(2,1)S(1)} %get-tuple-element.25), channel_id=1, source_target_pairs={{0,1},{1,0},{2,3},{3,2},{4,5},{5,4},{6,7},{7,6},{8,9},{9,8},{10,11... | collective-permute-start | bytes 147464 | tf_op jit(solution)/shard_map/ppermute | solution.py:18
  28.7 8.5 %collective-permute-start.11 = (bf16[8,3072]{1,0:T(8,128)(2,1)S(1)}, bf16[8,3072]{1,0:T(8,128)(2,1)S(1)}, u32[]{:S(2)}, u32[]{:S(2)}) collective-permute-start(bf16[8,3072]{1,0:T(8,128)(2,1)S(1)} %shard_map.96), channel_id=1, source_target_pairs={{0,4},{2,6},{4,0},{6,2},{1,5},{3,7},{5,1},{7,3},{8,12},{10,14},{12... | collective-permute-start | bytes 147464 | tf_op jit(solution)/shard_map/ppermute | solution.py:22
  29.2 8.0 %collective-permute-start.13 = (bf16[8,3072]{1,0:T(8,128)(2,1)S(1)}, bf16[8,3072]{1,0:T(8,128)(2,1)S(1)}, u32[]{:S(2)}, u32[]{:S(2)}) collective-permute-start(bf16[8,3072]{1,0:T(8,128)(2,1)S(1)} %shard_map.97), channel_id=1, source_target_pairs={{0,6},{2,4},{4,2},{6,0},{1,7},{3,5},{5,3},{7,1},{8,14},{10,12},{12... | collective-permute-start | bytes 147464 | tf_op jit(solution)/shard_map/ppermute | solution.py:22
  30.8 6.4 %collective-permute-start.9 = (bf16[8,3072]{1,0:T(8,128)(2,1)S(1)}, bf16[8,3072]{1,0:T(8,128)(2,1)S(1)}, u32[]{:S(2)}, u32[]{:S(2)}) collective-permute-start(bf16[8,3072]{1,0:T(8,128)(2,1)S(1)} %get-tuple-element.23), channel_id=1, source_target_pairs={{0,2},{2,0},{4,6},{6,4},{1,3},{3,1},{5,7},{7,5},{8,10},{10,8},{12,... | collective-permute-start | bytes 147464 | tf_op jit(solution)/shard_map/ppermute | solution.py:22
  32.4 3.6 %collective-permute-start.3 = (s32[8,128]{1,0:T(8,128)S(1)}, s32[8,128]{1,0:T(8,128)S(1)}, u32[]{:S(2)}, u32[]{:S(2)}) collective-permute-start(s32[8,128]{1,0:T(8,128)S(1)} %shard_map.89), channel_id=1, source_target_pairs={{0,16},{8,24},{16,0},{24,8},{1,17},{9,25},{17,1},{25,9},{2,18},{10... | collective-permute-start | bytes 12296 | tf_op jit(solution)/shard_map/ppermute | solution.py:22
  36.0 1.2 %collective-permute-start.4 = (s32[8,128]{1,0:T(8,128)S(1)}, s32[8,128]{1,0:T(8,128)S(1)}, u32[]{:S(2)}, u32[]{:S(2)}) collective-permute-start(s32[8,128]{1,0:T(8,128)S(1)} %add.3.sum_ref), channel_id=1, source_target_pairs={{0,8},{8,0},{16,24},{24,16},{1,9},{9,1},{17,25},{25,17},{2,10},{10... | collective-permute-start | bytes 12296 | tf_op jit(solution)/shard_map/ppermute | solution.py:22

commit v7 on v6

--- a/solution.py
+++ b/solution.py
@@ -45,10 +45,12 @@
 
 def intake_kernel(rep_count, tokens_ref, ids_ref, picks_ref, ready_ref, out_ref):
     part = tokens_ref.shape[1]
-    group = lax.rem(lax.axis_index("rep") + picks_ref[...] * (rep_count // REPL), rep_count)
+    group = (lax.axis_index("rep") + picks_ref[...] * (rep_count // REPL)) & (rep_count - 1)
     ids = ids_ref[...]
     rows, lanes = out_ref.shape[0], out_ref.shape[1] - part
-    cells = lax.rem(group, rows) * lanes + (group // rows) * LANES + ids
+    cells = group * lanes + ids
+    for wrap in range(rows, rep_count, rows):
+        cells += jnp.where(group >= wrap, LANES - rows * lanes, 0)
     position = lax.broadcasted_iota(jnp.int32, (rows, lanes), 0) * lanes
     position = position + lax.broadcasted_iota(jnp.int32, (rows, lanes), 1)
     total = jnp.zeros((rows, lanes), jnp.float32)
@@ -162,23 +164,25 @@
         out_ref[pl.ds(s * tok_rows, tok_rows), :] = jnp.broadcast_to(column, (tok_rows, LANES))
 
 
-def combine_kernel(coefficient_ref, sum_ref, swapped_ref, *refs):
-    pieces, (out_ref, counts_ref) = refs[:-2], refs[-2:]
-    ep_count = len(pieces)
-    tok_rows, part = out_ref.shape
-    coefficients = [
-        coefficient_ref[pl.ds(s * tok_rows, tok_rows), :] for s in range(ep_count)
-    ]
-    for lane in range(0, part, LANES):
-        total = 0.0
-        for coefficient, piece in zip(coefficients, pieces):
-            total += coefficient * piece[:, lane : lane + LANES].astype(jnp.float32)
-        out_ref[:, lane : lane + LANES] = total.astype(jnp.bfloat16)
+def table_kernel(ep_count, sum_ref, swapped_ref, counts_ref):
     counts = sum_ref[...] + swapped_ref[...]
+    tok_rows = counts.shape[0]
     for group in range(0, counts_ref.shape[0], tok_rows):
         size = min(tok_rows, counts_ref.shape[0] - group)
         start = group // tok_rows * LANES
         counts_ref[pl.ds(group, size), :] = counts[:size, start : start + ep_count]
+
+
+def weighted_kernel(blocks, has_start, coefficient_ref, *refs):
+    start, pieces, out_ref = refs[:has_start], refs[has_start:-1], refs[-1]
+    tok_rows, part = out_ref.shape
+    coefficients = [coefficient_ref[pl.ds(s * tok_rows, tok_rows), :] for s in blocks]
+    for lane in range(0, part, LANES):
+        span = slice(lane, lane + LANES)
+        total = start[0][:, span] if start else 0.0
+        for coefficient, piece in zip(coefficients, pieces):
+            total += coefficient * piece[:, span].astype(jnp.float32)
+        out_ref[:, span] = total.astype(out_ref.dtype)
 
 
 def vmem_call(kernel, outs, args, flops):
@@ -189,6 +193,14 @@
         out_specs=[pl.BlockSpec(memory_space=pltpu.VMEM)] * len(outs),
         compiler_params=pltpu.CompilerParams(vmem_limit_bytes=24 * MIB),
         cost_estimate=pl.CostEstimate(flops=flops, bytes_accessed=MIB, transcendentals=0),
+    )(*args)
+
+
+def output_call(kernel, shape, dtype, args):
+    return pl.pallas_call(
+        kernel,
+        out_shape=jax.ShapeDtypeStruct(shape, dtype),
+        compiler_params=pltpu.CompilerParams(vmem_limit_bytes=8 * MIB),
     )(*args)
 
 
@@ -274,15 +286,24 @@
         for s, piece in zip(group, outgoing):
             back[s] = swap(piece, "ep", ep_count, s) if s else piece
     (coefficients,) = vmem_call(coefficient_kernel, [((rows, LANES), f32)], (ids, gains), 1000)
-    return pl.pallas_call(
-        combine_kernel,
-        out_shape=[
-            jax.ShapeDtypeStruct((tok_rows, part), bf16),
-            jax.ShapeDtypeStruct((rep_count, ep_count), i32),
-        ],
-        compiler_params=pltpu.CompilerParams(vmem_limit_bytes=8 * MIB),
-        name="combine",
-    )(coefficients, counts, swapped, *back)
+    load_counts = output_call(
+        functools.partial(table_kernel, ep_count), (rep_count, ep_count), i32, (counts, swapped)
+    )
+    first = [0, *out_groups[0]]
+    (begun,) = vmem_call(
+        functools.partial(weighted_kernel, first, 0),
+        [((tok_rows, part), f32)],
+        (coefficients, *[back[s] for s in first]),
+        1000,
+    )
+    later = [s for s in range(ep_count) if s not in first]
+    moe_out = output_call(
+        functools.partial(weighted_kernel, later, 1),
+        (tok_rows, part),
+        bf16,
+        (coefficients, begun, *[back[s] for s in later]),
+    )
+    return moe_out, load_counts
 
 
 def row_groups(ep_count):

time: 38 us -> 38.8 us (1.021)
  Pallas kernels: 4.7 us -> 5.26 us
    ppermute x8, waiting for transfers between devices: 6.31 us -> 7.25 us  [swap(): return lax.ppermute(array, axis, [(i, i ^ span) for i in range(count)])]
    ppermute x1, waiting for transfers between devices: 2.57 us -> 1.79 us  [diagonal(): return lax.ppermute(array, ('ep', 'tp'), pairs)]
    pallas_call x1 -> x2, Pallas kernels: 0.67 us -> 1.23 us  [output_call(): pl.pallas_call(kernel, out_shape=jax.ShapeDtypeStruct(shape, dtype), comp...]
    pallas_call x12 -> x13, Pallas kernels: 4.03 us -> 4.03 us  [vmem_call(): pl.pallas_call(kernel, out_shape=[pltpu.VMEM(shape, dtype) for shape, dty...]
  transfers between devices with their start and end apart: 14 -> 14, of which waited for: 8 -> 7; matrix products, arithmetic and copies ran while one was open for 0% -> 0% of each run, Pallas kernels for 7% -> 8%
where the time goes in v7:
time: 38.8 us; the launch traced here: 38.6 us
  starting transfers between devices  20.9 us (54%)
  waiting for transfers between devices  10.9 us (28%)
  Pallas kernels  5.26 us (14%)
  between operations  0.78 us (2%)
  local copies, waits for them, and re-layouts  0.76 us (2%)
    ppermute x8, starting transfers between devices, swap(): return lax.ppermute(array, axis, [(i, i ^ span) for i in range(count)])  12.5 us
    ppermute x8, waiting for transfers between devices, swap(): return lax.ppermute(array, axis, [(i, i ^ span) for i in range(count)])  7.25 us
    ppermute x5, starting transfers between devices, shift(): lax.ppermute(array, axis, [(i, (i + step) % count) for i in range(count)])  5.68 us
    pallas_call x13, Pallas kernels, vmem_call(): pl.pallas_call(kernel, out_shape=[pltpu.VMEM(shape, dtype) for shape, dty...  4.03 us
    ppermute x1, starting transfers between devices, diagonal(): return lax.ppermute(array, ('ep', 'tp'), pairs)  2.68 us
    ppermute x5, waiting for transfers between devices, shift(): lax.ppermute(array, axis, [(i, (i + step) % count) for i in range(count)])  1.88 us
    ppermute x1, waiting for transfers between devices, diagonal(): return lax.ppermute(array, ('ep', 'tp'), pairs)  1.79 us
    pallas_call x2, Pallas kernels, output_call(): pl.pallas_call(kernel, out_shape=jax.ShapeDtypeStruct(shape, dtype), comp...  1.23 us
  transfers between devices with their start and end apart: 14, of which 7 were waited for; matrix products, arithmetic and copies ran while one was open for 0% of the time, Pallas kernels for 8%

profile of v7, /device:TPU:0, one launch (start us, length us, event | category | flops | bytes accessed | tf_op | source)
XLA Modules:
  0.0 38.6 jit_solution(8897595977600694304)
XLA Ops:
  0.7 0.7 %copy-done.3 = bf16[8,3072]{1,0:T(8,128)(2,1)S(1)} copy-done((bf16[8,3072]{1,0:T(8,128)(2,1)S(1)}, bf16[8,3072]{1,0:T(8,128)(2,1)}, u32[]{:S(2)}) %copy-start.3) | copy-done | bytes 49176
  1.4 0.1 shard_map.88.refs_0_
  1.6 3.1 %collective-permute-start.1 = (bf16[8,3200]{1,0:T(8,128)(2,1)S(1)}, bf16[8,3200]{1,0:T(8,128)(2,1)S(1)}, u32[]{:S(2)}, u32[]{:S(2)}) collective-permute-start(bf16[8,3200]{1,0:T(8,128)(2,1)S(1)} %shard_map.88.refs_0_), channel_id=1, source_target_pairs={{0,2},{2,0},{4,6},{6,4},{1,3},{3,1},{5,7},{7,5},{8,10},{10,8},{12,... | collective-permute-start | bytes 153608 | tf_op jit(solution)/shard_map/ppermute | solution.py:22
  4.7 2.6 %collective-permute-start = (bf16[8,3200]{1,0:T(8,128)(2,1)S(1)}, bf16[8,3200]{1,0:T(8,128)(2,1)S(1)}, u32[]{:S(2)}, u32[]{:S(2)}) collective-permute-start(bf16[8,3200]{1,0:T(8,128)(2,1)S(1)} %shard_map.88.refs_0_), channel_id=1, source_target_pairs={{0,4},{2,6},{4,0},{6,2},{1,5},{3,7},{5,1},{7,3},{8,12},{10,14},{12... | collective-permute-start | bytes 153608 | tf_op jit(solution)/shard_map/ppermute | solution.py:22
  7.3 0.0 collective-permute-done.1.refs_2_.refs_1_
  7.3 3.0 %collective-permute-done.refs_1_.refs_2_ = bf16[8,3200]{1,0:T(8,128)(2,1)S(1)} collective-permute-done((bf16[8,3200]{1,0:T(8,128)(2,1)S(1)}, bf16[8,3200]{1,0:T(8,128)(2,1)S(1)}, u32[]{:S(2)}, u32[]{:S(2)}) %collective-permute-start) | collective-permute-done | bytes 51232 | tf_op jit(solution)/shard_map/ppermute | solution.py:22
  10.3 1.6 %collective-permute-start.4 = (bf16[24,1536]{1,0:T(8,128)(2,1)S(1)}, bf16[24,1536]{1,0:T(8,128)(2,1)S(1)}, u32[]{:S(2)}, u32[]{:S(2)}) collective-permute-start(bf16[24,1536]{1,0:T(8,128)(2,1)S(1)} %get-tuple-element.15.refs_0_), channel_id=1, source_target_pairs={{0,1},{1,0},{2,3},{3,2},{4,5},{5,4},{6,7},{7,6},{8,9},{9,8},{10,11... | collective-permute-start | bytes 221192 | tf_op jit(solution)/shard_map/ppermute | solution.py:18
  11.8 2.1 %collective-permute-start.5 = (bf16[8,3200]{1,0:T(8,128)(2,1)S(1)}, bf16[8,3200]{1,0:T(8,128)(2,1)S(1)}, u32[]{:S(2)}, u32[]{:S(2)}) collective-permute-start(bf16[8,3200]{1,0:T(8,128)(2,1)S(1)} %shard_map.88.refs_0_), channel_id=1, source_target_pairs={{0,6},{2,4},{4,2},{6,0},{1,7},{3,5},{5,3},{7,1},{8,14},{10,12},{12... | collective-permute-start | bytes 153608 | tf_op jit(solution)/shard_map/ppermute | solution.py:22
  13.9 0.5 %collective-permute-start.2 = (bf16[24,1536]{1,0:T(8,128)(2,1)S(1)}, bf16[24,1536]{1,0:T(8,128)(2,1)S(1)}, u32[]{:S(2)}, u32[]{:S(2)}) collective-permute-start(bf16[24,1536]{1,0:T(8,128)(2,1)S(1)} %get-tuple-element.14.refs_1_), channel_id=1, source_target_pairs={{0,1},{1,0},{2,3},{3,2},{4,5},{5,4},{6,7},{7,6},{8,9},{9,8},{10,11... | collective-permute-start | bytes 221192 | tf_op jit(solution)/shard_map/ppermute | solution.py:18
  14.4 2.7 %collective-permute-start.3 = (bf16[8,3072]{1,0:T(8,128)(2,1)S(1)}, bf16[8,3072]{1,0:T(8,128)(2,1)S(1)}, u32[]{:S(2)}, u32[]{:S(2)}) collective-permute-start(bf16[8,3072]{1,0:T(8,128)(2,1)S(1)} %copy-done.3), channel_id=1, source_target_pairs={{0,7},{1,6},{2,5},{3,4},{4,3},{5,2},{6,1},{7,0},{8,15},{9,14},{10,... | collective-permute-start | bytes 147464 | tf_op jit(solution)/shard_map/ppermute | solution.py:31
  17.1 1.1 %collective-permute-done.5.refs_2_.refs_3_ = bf16[8,3200]{1,0:T(8,128)(2,1)S(1)} collective-permute-done((bf16[8,3200]{1,0:T(8,128)(2,1)S(1)}, bf16[8,3200]{1,0:T(8,128)(2,1)S(1)}, u32[]{:S(2)}, u32[]{:S(2)}) %collective-permute-start.5) | collective-permute-done | bytes 51232 | tf_op jit(solution)/shard_map/ppermute | solution.py:22
  18.3 1.2 %shard_map.90 = (f32[32,512]{1,0:T(8,128)S(1)}, f32[32,512]{1,0:T(8,128)S(1)}) custom-call(bf16[24,1536]{1,0:T(8,128)(2,1)S(1)} %get-tuple-element.15.refs_0_, bf16[24,1536]{1,0:T(8,128)(2,1)S(1)} %get-tuple-element.14.refs_1_, bf16[8,3200]{1,0:T(8,128)(2,1)S(1)} %collective-permute-done.5.refs_2_.refs_3_, bf16[6144,512]{1,0:T(8,128)(2,1)S(1)} %bitcast.9, ...), custom_call_target="tpu_custom_call" | custom-call | flops 201326592 | bytes 1048576 | tf_op jit(solution)/shard_map/pallas_call | solution.py:189
  19.4 1.8 %collective-permute-done.3.refs_1_ = bf16[8,3072]{1,0:T(8,128)(2,1)S(1)} collective-permute-done((bf16[8,3072]{1,0:T(8,128)(2,1)S(1)}, bf16[8,3072]{1,0:T(8,128)(2,1)S(1)}, u32[]{:S(2)}, u32[]{:S(2)}) %collective-permute-start.3) | collective-permute-done | bytes 49184 | tf_op jit(solution)/shard_map/ppermute | solution.py:31
  21.2 0.6 %shard_map.91 = (f32[32,512]{1,0:T(8,128)S(1)}, f32[32,512]{1,0:T(8,128)S(1)}) custom-call(bf16[24,1536]{1,0:T(8,128)(2,1)S(1)} %collective-permute-done.4.refs_0_, bf16[8,3072]{1,0:T(8,128)(2,1)S(1)} %collective-permute-done.3.refs_1_, bf16[6144,512]{1,0:T(8,128)(2,1)S(1)} %bitcast.10, bf16[6144,512]{1,0:T(8,128)(2,1)S(1)} %bitcast.13, ...), custom_call_target="tpu_custom_call" | custom-call | flops 100663296 | bytes 1048576 | tf_op jit(solution)/shard_map/pallas_call | solution.py:189
  21.9 0.0 collective-permute-done.2.refs_0_
  21.9 1.3 %shard_map.92 = (bf16[32,512]{1,0:T(8,128)(2,1)S(1)}, bf16[8,3072]{1,0:T(8,128)(2,1)S(1)}, bf16[8,3072]{1,0:T(8,128)(2,1)S(1)}, bf16[16,3072]{1,0:T(8,128)(2,1)S(1)}) custom-call(bf16[24,1536]{1,0:T(8,128)(2,1)S(1)} %collective-permute-done.2.refs_0_, bf16[8,3072]{1,0:T(8,128)(2,1)S(1)} %collective-permute-done.3.refs_1_, ...), custom_call_target="tpu_custom_call" | custom-call | flops 301989888 | bytes 1048576 | tf_op jit(solution)/shard_map/pallas_call | solution.py:189
  23.1 0.0 copy-start.5
  23.2 1.6 %collective-permute-start.6 = (bf16[16,3072]{1,0:T(8,128)(2,1)S(1)}, bf16[16,3072]{1,0:T(8,128)(2,1)S(1)}, u32[]{:S(2)}, u32[]{:S(2)}) collective-permute-start(bf16[16,3072]{1,0:T(8,128)(2,1)S(1)} %get-tuple-element.21), channel_id=1, source_target_pairs={{0,1},{1,0},{2,3},{3,2},{4,5},{5,4},{6,7},{7,6},{8,9},{9,8},{10,11... | collective-permute-start | bytes 294920 | tf_op jit(solution)/shard_map/ppermute | solution.py:18
  24.7 0.5 %collective-permute-start.7 = (bf16[8,3072]{1,0:T(8,128)(2,1)S(1)}, bf16[8,3072]{1,0:T(8,128)(2,1)S(1)}, u32[]{:S(2)}, u32[]{:S(2)}) collective-permute-start(bf16[8,3072]{1,0:T(8,128)(2,1)S(1)} %get-tuple-element.23), channel_id=1, source_target_pairs={{0,1},{1,0},{2,3},{3,2},{4,5},{5,4},{6,7},{7,6},{8,9},{9,8},{10,11... | collective-permute-start | bytes 147464 | tf_op jit(solution)/shard_map/ppermute | solution.py:18
  25.2 1.5 %collective-permute-start.10 = (bf16[8,3072]{1,0:T(8,128)(2,1)S(1)}, bf16[8,3072]{1,0:T(8,128)(2,1)S(1)}, u32[]{:S(2)}, u32[]{:S(2)}) collective-permute-start(bf16[8,3072]{1,0:T(8,128)(2,1)S(1)} %get-tuple-element.25), channel_id=1, source_target_pairs={{0,1},{1,0},{2,3},{3,2},{4,5},{5,4},{6,7},{7,6},{8,9},{9,8},{10,11... | collective-permute-start | bytes 147464 | tf_op jit(solution)/shard_map/ppermute | solution.py:18
  26.7 0.6 %shard_map.93.mine_ref = f32[32,3072]{1,0:T(8,128)S(1)} custom-call(bf16[32,512]{1,0:T(8,128)(2,1)S(1)} %get-tuple-element.20.hidden_ref, bf16[512,6144]{1,0:T(8,128)(2,1)S(1)} %bitcast.8), custom_call_target="tpu_custom_call" | custom-call | flops 100663296 | bytes 1048576 | tf_op jit(solution)/shard_map/pallas_call | solution.py:189
  27.4 1.4 %collective-permute-done.7.refs_0_ = bf16[8,3072]{1,0:T(8,128)(2,1)S(1)} collective-permute-done((bf16[8,3072]{1,0:T(8,128)(2,1)S(1)}, bf16[8,3072]{1,0:T(8,128)(2,1)S(1)}, u32[]{:S(2)}, u32[]{:S(2)}) %collective-permute-start.7) | collective-permute-done | bytes 49184 | tf_op jit(solution)/shard_map/ppermute | solution.py:18
  28.8 0.1 collective-permute-start.8
  28.9 0.4 %collective-permute-done.10.refs_0_ = bf16[8,3072]{1,0:T(8,128)(2,1)S(1)} collective-permute-done((bf16[8,3072]{1,0:T(8,128)(2,1)S(1)}, bf16[8,3072]{1,0:T(8,128)(2,1)S(1)}, u32[]{:S(2)}, u32[]{:S(2)}) %collective-permute-start.10) | collective-permute-done | bytes 49184 | tf_op jit(solution)/shard_map/ppermute | solution.py:18
  29.3 1.8 %collective-permute-start.11 = (bf16[8,3072]{1,0:T(8,128)(2,1)S(1)}, bf16[8,3072]{1,0:T(8,128)(2,1)S(1)}, u32[]{:S(2)}, u32[]{:S(2)}) collective-permute-start(bf16[8,3072]{1,0:T(8,128)(2,1)S(1)} %shard_map.97), channel_id=1, source_target_pairs={{0,6},{2,4},{4,2},{6,0},{1,7},{3,5},{5,3},{7,1},{8,14},{10,12},{12... | collective-permute-start | bytes 147464 | tf_op jit(solution)/shard_map/ppermute | solution.py:22
  31.2 1.4 %collective-permute-start.9 = (bf16[8,3072]{1,0:T(8,128)(2,1)S(1)}, bf16[8,3072]{1,0:T(8,128)(2,1)S(1)}, u32[]{:S(2)}, u32[]{:S(2)}) collective-permute-start(bf16[8,3072]{1,0:T(8,128)(2,1)S(1)} %get-tuple-element.24), channel_id=1, source_target_pairs={{0,2},{2,0},{4,6},{6,4},{1,3},{3,1},{5,7},{7,5},{8,10},{10,8},{12,... | collective-permute-start | bytes 147464 | tf_op jit(solution)/shard_map/ppermute | solution.py:22
  32.6 1.5 %collective-permute-start.12 = (s32[8,128]{1,0:T(8,128)S(1)}, s32[8,128]{1,0:T(8,128)S(1)}, u32[]{:S(2)}, u32[]{:S(2)}) collective-permute-start(s32[8,128]{1,0:T(8,128)S(1)} %shard_map.99), channel_id=1, source_target_pairs={{0,16},{8,24},{16,0},{24,8},{1,17},{9,25},{17,1},{25,9},{2,18},{10... | collective-permute-start | bytes 12296 | tf_op jit(solution)/shard_map/ppermute | solution.py:22
  34.1 2.1 %collective-permute-done.12 = s32[8,128]{1,0:T(8,128)S(1)} collective-permute-done((s32[8,128]{1,0:T(8,128)S(1)}, s32[8,128]{1,0:T(8,128)S(1)}, u32[]{:S(2)}, u32[]{:S(2)}) %collective-permute-start.12) | collective-permute-done | bytes 4128 | tf_op jit(solution)/shard_map/ppermute | solution.py:22
  36.2 0.1 shard_map.86.coefficient_ref
  36.3 1.1 %collective-permute-done.13.swapped_ref = s32[8,128]{1,0:T(8,128)S(1)} collective-permute-done((s32[8,128]{1,0:T(8,128)S(1)}, s32[8,128]{1,0:T(8,128)S(1)}, u32[]{:S(2)}, u32[]{:S(2)}) %collective-permute-start.13) | collective-permute-done | bytes 4128 | tf_op jit(solution)/shard_map/ppermute | solution.py:22
  37.3 0.6 %shard_map.100 = s32[4,4]{1,0:T(4,128)} custom-call(s32[8,128]{1,0:T(8,128)S(1)} %add.3.sum_ref, s32[8,128]{1,0:T(8,128)S(1)} %collective-permute-done.13.swapped_ref), custom_call_target="tpu_custom_call" | custom-call | tf_op jit(solution)/shard_map/pallas_call | solution.py:200
  38.0 0.6 %shard_map.98 = bf16[8,3072]{1,0:T(8,128)(2,1)} custom-call(f32[32,128]{1,0:T(8,128)S(1)} %shard_map.86.coefficient_ref, f32[8,3072]{1,0:T(8,128)S(1)} %shard_map.96.refs_0_, bf16[8,3072]{1,0:T(8,128)(2,1)S(1)} %collective-permute-done.9.refs_1_, bf16[8,3072]{1,0:T(8,128)(2,1)S(1)} %collective-permute-done.11.refs_2_), custom_call_target="tpu_custom_call" | custom-call | tf_op jit(solution)/shard_map/pallas_call | solution.py:200
  (26 shorter events, 0.1 us)
Async XLA Ops:
  0.6 0.8 %copy-start.3 = (bf16[8,3072]{1,0:T(8,128)(2,1)S(1)}, bf16[8,3072]{1,0:T(8,128)(2,1)}, u32[]{:S(2)}) copy-start(bf16[8,3072]{1,0:T(8,128)(2,1)} %tokens_ref.1) | copy-start | bytes 147460
  0.6 0.8 %copy-start.6 = (s32[8,2]{0,1:T(2,128)S(1)}, s32[8,2]{0,1:T(2,128)}, u32[]{:S(2)}) copy-start(s32[8,2]{0,1:T(2,128)} %param.9) | copy-start | bytes 196
  0.7 0.8 %copy-start.4 = (s32[8,2]{0,1:T(2,128)S(1)}, s32[8,2]{0,1:T(2,128)}, u32[]{:S(2)}) copy-start(s32[8,2]{0,1:T(2,128)} %param.8) | copy-start | bytes 196
  0.7 17.6 %copy-start = (bf16[1,512,6144]{2,1,0:T(8,128)(2,1)S(1)}, bf16[1,512,6144]{2,1,0:T(8,128)(2,1)}, u32[]{:S(2)}) copy-start(bf16[1,512,6144]{2,1,0:T(8,128)(2,1)} %param.13) | copy-start | bytes 18874372
  0.7 17.6 %copy-start.2 = (bf16[1,6144,512]{2,1,0:T(8,128)(2,1)S(1)}, bf16[1,6144,512]{2,1,0:T(8,128)(2,1)}, u32[]{:S(2)}) copy-start(bf16[1,6144,512]{2,1,0:T(8,128)(2,1)} %param.12) | copy-start | bytes 18874372
  0.7 17.6 %copy-start.1 = (bf16[1,6144,512]{2,1,0:T(8,128)(2,1)S(1)}, bf16[1,6144,512]{2,1,0:T(8,128)(2,1)}, u32[]{:S(2)}) copy-start(bf16[1,6144,512]{2,1,0:T(8,128)(2,1)} %param.11) | copy-start | bytes 18874372
  1.6 5.7 %collective-permute-start.1 = (bf16[8,3200]{1,0:T(8,128)(2,1)S(1)}, bf16[8,3200]{1,0:T(8,128)(2,1)S(1)}, u32[]{:S(2)}, u32[]{:S(2)}) collective-permute-start(bf16[8,3200]{1,0:T(8,128)(2,1)S(1)} %shard_map.88.refs_0_), channel_id=1, source_target_pairs={{0,2},{2,0},{4,6},{6,4},{1,3},{3,1},{5,7},{7,5},{8,10},{10,8},{12,... | collective-permute-start | bytes 153608 | tf_op jit(solution)/shard_map/ppermute | solution.py:22
  4.7 5.6 %collective-permute-start = (bf16[8,3200]{1,0:T(8,128)(2,1)S(1)}, bf16[8,3200]{1,0:T(8,128)(2,1)S(1)}, u32[]{:S(2)}, u32[]{:S(2)}) collective-permute-start(bf16[8,3200]{1,0:T(8,128)(2,1)S(1)} %shard_map.88.refs_0_), channel_id=1, source_target_pairs={{0,4},{2,6},{4,0},{6,2},{1,5},{3,7},{5,1},{7,3},{8,12},{10,14},{12... | collective-permute-start | bytes 153608 | tf_op jit(solution)/shard_map/ppermute | solution.py:22
  10.3 11.0 %collective-permute-start.4 = (bf16[24,1536]{1,0:T(8,128)(2,1)S(1)}, bf16[24,1536]{1,0:T(8,128)(2,1)S(1)}, u32[]{:S(2)}, u32[]{:S(2)}) collective-permute-start(bf16[24,1536]{1,0:T(8,128)(2,1)S(1)} %get-tuple-element.15.refs_0_), channel_id=1, source_target_pairs={{0,1},{1,0},{2,3},{3,2},{4,5},{5,4},{6,7},{7,6},{8,9},{9,8},{10,11... | collective-permute-start | bytes 221192 | tf_op jit(solution)/shard_map/ppermute | solution.py:18
  11.8 6.4 %collective-permute-start.5 = (bf16[8,3200]{1,0:T(8,128)(2,1)S(1)}, bf16[8,3200]{1,0:T(8,128)(2,1)S(1)}, u32[]{:S(2)}, u32[]{:S(2)}) collective-permute-start(bf16[8,3200]{1,0:T(8,128)(2,1)S(1)} %shard_map.88.refs_0_), channel_id=1, source_target_pairs={{0,6},{2,4},{4,2},{6,0},{1,7},{3,5},{5,3},{7,1},{8,14},{10,12},{12... | collective-permute-start | bytes 153608 | tf_op jit(solution)/shard_map/ppermute | solution.py:22
  13.9 8.0 %collective-permute-start.2 = (bf16[24,1536]{1,0:T(8,128)(2,1)S(1)}, bf16[24,1536]{1,0:T(8,128)(2,1)S(1)}, u32[]{:S(2)}, u32[]{:S(2)}) collective-permute-start(bf16[24,1536]{1,0:T(8,128)(2,1)S(1)} %get-tuple-element.14.refs_1_), channel_id=1, source_target_pairs={{0,1},{1,0},{2,3},{3,2},{4,5},{5,4},{6,7},{7,6},{8,9},{9,8},{10,11... | collective-permute-start | bytes 221192 | tf_op jit(solution)/shard_map/ppermute | solution.py:18
  14.4 6.8 %collective-permute-start.3 = (bf16[8,3072]{1,0:T(8,128)(2,1)S(1)}, bf16[8,3072]{1,0:T(8,128)(2,1)S(1)}, u32[]{:S(2)}, u32[]{:S(2)}) collective-permute-start(bf16[8,3072]{1,0:T(8,128)(2,1)S(1)} %copy-done.3), channel_id=1, source_target_pairs={{0,7},{1,6},{2,5},{3,4},{4,3},{5,2},{6,1},{7,0},{8,15},{9,14},{10,... | collective-permute-start | bytes 147464 | tf_op jit(solution)/shard_map/ppermute | solution.py:31
  23.1 13.0 %copy-start.5 = (f32[8,2]{0,1:T(2,128)S(1)}, f32[8,2]{0,1:T(2,128)}, u32[]{:S(2)}) copy-start(f32[8,2]{0,1:T(2,128)} %param.10) | copy-start | bytes 196
  23.2 8.0 %collective-permute-start.6 = (bf16[16,3072]{1,0:T(8,128)(2,1)S(1)}, bf16[16,3072]{1,0:T(8,128)(2,1)S(1)}, u32[]{:S(2)}, u32[]{:S(2)}) collective-permute-start(bf16[16,3072]{1,0:T(8,128)(2,1)S(1)} %get-tuple-element.21), channel_id=1, source_target_pairs={{0,1},{1,0},{2,3},{3,2},{4,5},{5,4},{6,7},{7,6},{8,9},{9,8},{10,11... | collective-permute-start | bytes 294920 | tf_op jit(solution)/shard_map/ppermute | solution.py:18
  24.7 4.1 %collective-permute-start.7 = (bf16[8,3072]{1,0:T(8,128)(2,1)S(1)}, bf16[8,3072]{1,0:T(8,128)(2,1)S(1)}, u32[]{:S(2)}, u32[]{:S(2)}) collective-permute-start(bf16[8,3072]{1,0:T(8,128)(2,1)S(1)} %get-tuple-element.23), channel_id=1, source_target_pairs={{0,1},{1,0},{2,3},{3,2},{4,5},{5,4},{6,7},{7,6},{8,9},{9,8},{10,11... | collective-permute-start | bytes 147464 | tf_op jit(solution)/shard_map/ppermute | solution.py:18
  25.2 4.1 %collective-permute-start.10 = (bf16[8,3072]{1,0:T(8,128)(2,1)S(1)}, bf16[8,3072]{1,0:T(8,128)(2,1)S(1)}, u32[]{:S(2)}, u32[]{:S(2)}) collective-permute-start(bf16[8,3072]{1,0:T(8,128)(2,1)S(1)} %get-tuple-element.25), channel_id=1, source_target_pairs={{0,1},{1,0},{2,3},{3,2},{4,5},{5,4},{6,7},{7,6},{8,9},{9,8},{10,11... | collective-permute-start | bytes 147464 | tf_op jit(solution)/shard_map/ppermute | solution.py:18
  28.8 9.1 %collective-permute-start.8 = (bf16[8,3072]{1,0:T(8,128)(2,1)S(1)}, bf16[8,3072]{1,0:T(8,128)(2,1)S(1)}, u32[]{:S(2)}, u32[]{:S(2)}) collective-permute-start(bf16[8,3072]{1,0:T(8,128)(2,1)S(1)} %shard_map.95), channel_id=1, source_target_pairs={{0,4},{2,6},{4,0},{6,2},{1,5},{3,7},{5,1},{7,3},{8,12},{10,14},{12... | collective-permute-start | bytes 147464 | tf_op jit(solution)/shard_map/ppermute | solution.py:22
  29.3 8.6 %collective-permute-start.11 = (bf16[8,3072]{1,0:T(8,128)(2,1)S(1)}, bf16[8,3072]{1,0:T(8,128)(2,1)S(1)}, u32[]{:S(2)}, u32[]{:S(2)}) collective-permute-start(bf16[8,3072]{1,0:T(8,128)(2,1)S(1)} %shard_map.97), channel_id=1, source_target_pairs={{0,6},{2,4},{4,2},{6,0},{1,7},{3,5},{5,3},{7,1},{8,14},{10,12},{12... | collective-permute-start | bytes 147464 | tf_op jit(solution)/shard_map/ppermute | solution.py:22
  31.2 6.8 %collective-permute-start.9 = (bf16[8,3072]{1,0:T(8,128)(2,1)S(1)}, bf16[8,3072]{1,0:T(8,128)(2,1)S(1)}, u32[]{:S(2)}, u32[]{:S(2)}) collective-permute-start(bf16[8,3072]{1,0:T(8,128)(2,1)S(1)} %get-tuple-element.24), channel_id=1, source_target_pairs={{0,2},{2,0},{4,6},{6,4},{1,3},{3,1},{5,7},{7,5},{8,10},{10,8},{12,... | collective-permute-start | bytes 147464 | tf_op jit(solution)/shard_map/ppermute | solution.py:22
  32.6 3.6 %collective-permute-start.12 = (s32[8,128]{1,0:T(8,128)S(1)}, s32[8,128]{1,0:T(8,128)S(1)}, u32[]{:S(2)}, u32[]{:S(2)}) collective-permute-start(s32[8,128]{1,0:T(8,128)S(1)} %shard_map.99), channel_id=1, source_target_pairs={{0,16},{8,24},{16,0},{24,8},{1,17},{9,25},{17,1},{25,9},{2,18},{10... | collective-permute-start | bytes 12296 | tf_op jit(solution)/shard_map/ppermute | solution.py:22
  36.2 1.2 %collective-permute-start.13 = (s32[8,128]{1,0:T(8,128)S(1)}, s32[8,128]{1,0:T(8,128)S(1)}, u32[]{:S(2)}, u32[]{:S(2)}) collective-permute-start(s32[8,128]{1,0:T(8,128)S(1)} %add.3.sum_ref), channel_id=1, source_target_pairs={{0,8},{8,0},{16,24},{24,16},{1,9},{9,1},{17,25},{25,17},{2,10},{10... | collective-permute-start | bytes 12296 | tf_op jit(solution)/shard_map/ppermute | solution.py:22

commit v8 on v7

--- a/solution.py
+++ b/solution.py
@@ -139,14 +139,17 @@
     out_ref[...] = dot(hidden_ref[...], down_ref[:, columns])
 
 
-def pack_kernel(place, arrived_count, mine_ref, *refs):
+def pack_kernel(place, arrived_count, mine_ref, counts_ref, swapped_ref, *refs):
     arrived, outs = refs[:arrived_count], refs[arrived_count:]
-    size = outs[0].shape[0]
+    size, part = outs[0].shape[0], mine_ref.shape[1]
     for i, (p, out) in enumerate(zip(place, outs)):
         total = mine_ref[pl.ds(p * size, size), :]
         for piece in arrived:
             total += piece[pl.ds(i * size, size), :].astype(jnp.float32)
-        out[...] = total.astype(jnp.bfloat16)
+        out[:, :part] = total.astype(jnp.bfloat16)
+        if out.shape[1] > part:
+            carried = counts_ref[...] + swapped_ref[...]
+            out[:, part:] = carried.astype(jnp.float32).astype(jnp.bfloat16)
 
 
 def coefficient_kernel(ids_ref, scores_ref, out_ref):
@@ -162,15 +165,6 @@
         row = jnp.sum(jnp.where(ids == (me ^ s), weights, 0.0), 0, keepdims=True)
         column = jnp.sum(jnp.where(diagonal, row, 0.0), 1, keepdims=True)
         out_ref[pl.ds(s * tok_rows, tok_rows), :] = jnp.broadcast_to(column, (tok_rows, LANES))
-
-
-def table_kernel(ep_count, sum_ref, swapped_ref, counts_ref):
-    counts = sum_ref[...] + swapped_ref[...]
-    tok_rows = counts.shape[0]
-    for group in range(0, counts_ref.shape[0], tok_rows):
-        size = min(tok_rows, counts_ref.shape[0] - group)
-        start = group // tok_rows * LANES
-        counts_ref[pl.ds(group, size), :] = counts[:size, start : start + ep_count]
 
 
 def weighted_kernel(blocks, has_start, coefficient_ref, *refs):
@@ -185,6 +179,19 @@
         out_ref[:, span] = total.astype(out_ref.dtype)
 
 
+def finish_kernel(blocks, coefficient_ref, sum_ref, swapped_ref, begun_ref, *refs):
+    pieces, (out_ref, counts_ref) = refs[:-2], refs[-2:]
+    weighted_kernel(blocks, 1, coefficient_ref, begun_ref, *pieces, out_ref)
+    tok_rows, part = out_ref.shape
+    counts = sum_ref[...] + swapped_ref[...]
+    counts += pieces[-1][:, part:].astype(jnp.float32).astype(jnp.int32)
+    for group in range(0, counts_ref.shape[0], tok_rows):
+        size = min(tok_rows, counts_ref.shape[0] - group)
+        start = group // tok_rows * LANES
+        columns = counts_ref.shape[1]
+        counts_ref[pl.ds(group, size), :] = counts[:size, start : start + columns]
+
+
 def vmem_call(kernel, outs, args, flops):
     return pl.pallas_call(
         kernel,
@@ -193,14 +200,6 @@
         out_specs=[pl.BlockSpec(memory_space=pltpu.VMEM)] * len(outs),
         compiler_params=pltpu.CompilerParams(vmem_limit_bytes=24 * MIB),
         cost_estimate=pl.CostEstimate(flops=flops, bytes_accessed=MIB, transcendentals=0),
-    )(*args)
-
-
-def output_call(kernel, shape, dtype, args):
-    return pl.pallas_call(
-        kernel,
-        out_shape=jax.ShapeDtypeStruct(shape, dtype),
-        compiler_params=pltpu.CompilerParams(vmem_limit_bytes=8 * MIB),
     )(*args)
 
 
@@ -229,8 +228,10 @@
         1000,
     )
 
+    half = ep_count // 2
     blocks = [message]
-    blocks += [swap(message, "ep", ep_count, s) for s in range(1, ep_count)]
+    for s in range(1, ep_count):
+        blocks.append(swap(message if s < half else tokens, "ep", ep_count, s))
     steps = range(1, tp_count)
     shape = (len(group) * tok_rows, part // 2)
     halves = vmem_call(stack_kernel, [(shape, bf16)] * 2, tuple(blocks[s] for s in group), 1000)
@@ -244,7 +245,7 @@
         [ref for d in steps for ref in (exchanged[h][d - 1], *[a[d - 1] for a in across])]
         for h in range(2)
     ]
-    (counts,) = vmem_call(sum_kernel, [((tok_rows, width), i32)], tuple(blocks), 1000)
+    (counts,) = vmem_call(sum_kernel, [((tok_rows, width), i32)], tuple(blocks[:half]), 1000)
     swapped = jnp.zeros_like(counts)
     for bit in range(rep_count.bit_length() - 1):
         counts = counts + swapped
@@ -279,16 +280,13 @@
     for number, group in enumerate(out_groups):
         outgoing = vmem_call(
             functools.partial(pack_kernel, places[number], len(steps)),
-            [((tok_rows, part), bf16)] * len(group),
-            (mine, *arrived[number]),
+            [((tok_rows, part + width * (s == ep_count - 1)), bf16) for s in group],
+            (mine, counts, swapped, *arrived[number]),
             1000,
         )
         for s, piece in zip(group, outgoing):
             back[s] = swap(piece, "ep", ep_count, s) if s else piece
     (coefficients,) = vmem_call(coefficient_kernel, [((rows, LANES), f32)], (ids, gains), 1000)
-    load_counts = output_call(
-        functools.partial(table_kernel, ep_count), (rep_count, ep_count), i32, (counts, swapped)
-    )
     first = [0, *out_groups[0]]
     (begun,) = vmem_call(
         functools.partial(weighted_kernel, first, 0),
@@ -297,13 +295,15 @@
         1000,
     )
     later = [s for s in range(ep_count) if s not in first]
-    moe_out = output_call(
-        functools.partial(weighted_kernel, later, 1),
-        (tok_rows, part),
-        bf16,
-        (coefficients, begun, *[back[s] for s in later]),
-    )
-    return moe_out, load_counts
+    return pl.pallas_call(
+        functools.partial(finish_kernel, later),
+        out_shape=[
+            jax.ShapeDtypeStruct((tok_rows, part), bf16),
+            jax.ShapeDtypeStruct((rep_count, ep_count), i32),
+        ],
+        compiler_params=pltpu.CompilerParams(vmem_limit_bytes=8 * MIB),
+        name="finish",
+    )(coefficients, counts, swapped, begun, *[back[s] for s in later])
 
 
 def row_groups(ep_count):

time: 38.8 us -> 40.2 us (1.036)
  starting transfers between devices: 20.9 us -> 22.2 us
  waiting for transfers between devices: 10.9 us -> 11.6 us
  Pallas kernels: 5.26 us -> 4.68 us
    ppermute x8, waiting for transfers between devices: 7.25 us -> 9.71 us  [swap(): return lax.ppermute(array, axis, [(i, i ^ span) for i in range(count)])]
    ppermute x5, waiting for transfers between devices: 1.88 us -> 0.02 us  [shift(): lax.ppermute(array, axis, [(i, (i + step) % count) for i in range(count)])]
    ppermute x8, starting transfers between devices: 12.5 us -> 13.9 us  [swap(): return lax.ppermute(array, axis, [(i, i ^ span) for i in range(count)])]
    pallas_call x2 -> x1, Pallas kernels: 1.23 us -> 0.65 us  [per_device(): pl.pallas_call(functools.partial(finish_kernel, later), out_shape=[jax.Sh...]
  transfers between devices with their start and end apart: 14 -> 14, of which waited for: 7 -> 6; matrix products, arithmetic and copies ran while one was open for 0% -> 0% of each run, Pallas kernels for 8% -> 7%
where the time goes in v8:
time: 40.2 us; the launch traced here: 40 us
  starting transfers between devices  22.2 us (55%)
  waiting for transfers between devices  11.6 us (29%)
  Pallas kernels  4.68 us (12%)
  between operations  0.78 us (2%)
  local copies, waits for them, and re-layouts  0.76 us (2%)
    ppermute x8, starting transfers between devices, swap(): return lax.ppermute(array, axis, [(i, i ^ span) for i in range(count)])  13.9 us
    ppermute x8, waiting for transfers between devices, swap(): return lax.ppermute(array, axis, [(i, i ^ span) for i in range(count)])  9.71 us
    ppermute x5, starting transfers between devices, shift(): lax.ppermute(array, axis, [(i, (i + step) % count) for i in range(count)])  5.67 us
    pallas_call x13, Pallas kernels, vmem_call(): pl.pallas_call(kernel, out_shape=[pltpu.VMEM(shape, dtype) for shape, dty...  4.03 us
    ppermute x1, starting transfers between devices, diagonal(): return lax.ppermute(array, ('ep', 'tp'), pairs)  2.68 us
    ppermute x1, waiting for transfers between devices, diagonal(): return lax.ppermute(array, ('ep', 'tp'), pairs)  1.85 us
  transfers between devices with their start and end apart: 14, of which 6 were waited for; matrix products, arithmetic and copies ran while one was open for 0% of the time, Pallas kernels for 7%

profile of v8, /device:TPU:0, one launch (start us, length us, event | category | flops | bytes accessed | tf_op | source)
XLA Modules:
  0.0 40.0 jit_solution(8203681442368283733)
XLA Ops:
  0.7 0.7 %copy-done.3 = bf16[8,3072]{1,0:T(8,128)(2,1)S(1)} copy-done((bf16[8,3072]{1,0:T(8,128)(2,1)S(1)}, bf16[8,3072]{1,0:T(8,128)(2,1)}, u32[]{:S(2)}) %copy-start.3) | copy-done | bytes 49176
  1.4 0.1 shard_map.88.refs_0_
  1.6 3.1 %collective-permute-start = (bf16[8,3200]{1,0:T(8,128)(2,1)S(1)}, bf16[8,3200]{1,0:T(8,128)(2,1)S(1)}, u32[]{:S(2)}, u32[]{:S(2)}) collective-permute-start(bf16[8,3200]{1,0:T(8,128)(2,1)S(1)} %shard_map.88.refs_0_), channel_id=1, source_target_pairs={{0,2},{2,0},{4,6},{6,4},{1,3},{3,1},{5,7},{7,5},{8,10},{10,8},{12,... | collective-permute-start | bytes 153608 | tf_op jit(solution)/shard_map/ppermute | solution.py:22
  4.7 2.6 %collective-permute-start.3 = (bf16[8,3072]{1,0:T(8,128)(2,1)S(1)}, bf16[8,3072]{1,0:T(8,128)(2,1)S(1)}, u32[]{:S(2)}, u32[]{:S(2)}) collective-permute-start(bf16[8,3072]{1,0:T(8,128)(2,1)S(1)} %copy-done.3), channel_id=1, source_target_pairs={{0,4},{2,6},{4,0},{6,2},{1,5},{3,7},{5,1},{7,3},{8,12},{10,14},{12... | collective-permute-start | bytes 147464 | tf_op jit(solution)/shard_map/ppermute | solution.py:22
  7.3 2.9 %collective-permute-done.3.refs_1_ = bf16[8,3072]{1,0:T(8,128)(2,1)S(1)} collective-permute-done((bf16[8,3072]{1,0:T(8,128)(2,1)S(1)}, bf16[8,3072]{1,0:T(8,128)(2,1)S(1)}, u32[]{:S(2)}, u32[]{:S(2)}) %collective-permute-start.3) | collective-permute-done | bytes 49184 | tf_op jit(solution)/shard_map/ppermute | solution.py:22
  10.2 1.6 %collective-permute-start.6 = (bf16[24,1536]{1,0:T(8,128)(2,1)S(1)}, bf16[24,1536]{1,0:T(8,128)(2,1)S(1)}, u32[]{:S(2)}, u32[]{:S(2)}) collective-permute-start(bf16[24,1536]{1,0:T(8,128)(2,1)S(1)} %get-tuple-element.15.refs_0_), channel_id=1, source_target_pairs={{0,1},{1,0},{2,3},{3,2},{4,5},{5,4},{6,7},{7,6},{8,9},{9,8},{10,11... | collective-permute-start | bytes 221192 | tf_op jit(solution)/shard_map/ppermute | solution.py:18
  11.8 2.1 %collective-permute-start.7 = (bf16[8,3072]{1,0:T(8,128)(2,1)S(1)}, bf16[8,3072]{1,0:T(8,128)(2,1)S(1)}, u32[]{:S(2)}, u32[]{:S(2)}) collective-permute-start(bf16[8,3072]{1,0:T(8,128)(2,1)S(1)} %copy-done.3), channel_id=1, source_target_pairs={{0,6},{2,4},{4,2},{6,0},{1,7},{3,5},{5,3},{7,1},{8,14},{10,12},{12... | collective-permute-start | bytes 147464 | tf_op jit(solution)/shard_map/ppermute | solution.py:22
  13.9 0.5 %collective-permute-start.4 = (bf16[24,1536]{1,0:T(8,128)(2,1)S(1)}, bf16[24,1536]{1,0:T(8,128)(2,1)S(1)}, u32[]{:S(2)}, u32[]{:S(2)}) collective-permute-start(bf16[24,1536]{1,0:T(8,128)(2,1)S(1)} %get-tuple-element.14.refs_1_), channel_id=1, source_target_pairs={{0,1},{1,0},{2,3},{3,2},{4,5},{5,4},{6,7},{7,6},{8,9},{9,8},{10,11... | collective-permute-start | bytes 221192 | tf_op jit(solution)/shard_map/ppermute | solution.py:18
  14.4 2.7 %collective-permute-start.5 = (bf16[8,3072]{1,0:T(8,128)(2,1)S(1)}, bf16[8,3072]{1,0:T(8,128)(2,1)S(1)}, u32[]{:S(2)}, u32[]{:S(2)}) collective-permute-start(bf16[8,3072]{1,0:T(8,128)(2,1)S(1)} %copy-done.3), channel_id=1, source_target_pairs={{0,7},{1,6},{2,5},{3,4},{4,3},{5,2},{6,1},{7,0},{8,15},{9,14},{10,... | collective-permute-start | bytes 147464 | tf_op jit(solution)/shard_map/ppermute | solution.py:31
  17.1 1.1 %collective-permute-done.7.refs_2_ = bf16[8,3072]{1,0:T(8,128)(2,1)S(1)} collective-permute-done((bf16[8,3072]{1,0:T(8,128)(2,1)S(1)}, bf16[8,3072]{1,0:T(8,128)(2,1)S(1)}, u32[]{:S(2)}, u32[]{:S(2)}) %collective-permute-start.7) | collective-permute-done | bytes 49184 | tf_op jit(solution)/shard_map/ppermute | solution.py:22
  18.1 1.2 %shard_map.91 = (f32[32,512]{1,0:T(8,128)S(1)}, f32[32,512]{1,0:T(8,128)S(1)}) custom-call(bf16[24,1536]{1,0:T(8,128)(2,1)S(1)} %get-tuple-element.15.refs_0_, bf16[24,1536]{1,0:T(8,128)(2,1)S(1)} %get-tuple-element.14.refs_1_, bf16[8,3072]{1,0:T(8,128)(2,1)S(1)} %collective-permute-done.7.refs_2_, bf16[6144,512]{1,0:T(8,128)(2,1)S(1)} %bitcast.6, ...), custom_call_target="tpu_custom_call" | custom-call | flops 201326592 | bytes 1048576 | tf_op jit(solution)/shard_map/pallas_call | solution.py:196
  19.3 1.9 %collective-permute-done.5.refs_1_ = bf16[8,3072]{1,0:T(8,128)(2,1)S(1)} collective-permute-done((bf16[8,3072]{1,0:T(8,128)(2,1)S(1)}, bf16[8,3072]{1,0:T(8,128)(2,1)S(1)}, u32[]{:S(2)}, u32[]{:S(2)}) %collective-permute-start.5) | collective-permute-done | bytes 49184 | tf_op jit(solution)/shard_map/ppermute | solution.py:31
  21.2 0.0 collective-permute-done.6.refs_0_
  21.2 0.6 %shard_map.92 = (f32[32,512]{1,0:T(8,128)S(1)}, f32[32,512]{1,0:T(8,128)S(1)}) custom-call(bf16[24,1536]{1,0:T(8,128)(2,1)S(1)} %collective-permute-done.6.refs_0_, bf16[8,3072]{1,0:T(8,128)(2,1)S(1)} %collective-permute-done.5.refs_1_, bf16[6144,512]{1,0:T(8,128)(2,1)S(1)} %bitcast.7, bf16[6144,512]{1,0:T(8,128)(2,1)S(1)} %bitcast.10, ...), custom_call_target="tpu_custom_call" | custom-call | flops 100663296 | bytes 1048576 | tf_op jit(solution)/shard_map/pallas_call | solution.py:196
  21.8 0.0 collective-permute-done.4.refs_0_
  21.8 1.3 %shard_map.93 = (bf16[32,512]{1,0:T(8,128)(2,1)S(1)}, bf16[8,3072]{1,0:T(8,128)(2,1)S(1)}, bf16[8,3072]{1,0:T(8,128)(2,1)S(1)}, bf16[16,3072]{1,0:T(8,128)(2,1)S(1)}) custom-call(bf16[24,1536]{1,0:T(8,128)(2,1)S(1)} %collective-permute-done.4.refs_0_, bf16[8,3072]{1,0:T(8,128)(2,1)S(1)} %collective-permute-done.5.refs_1_, ...), custom_call_target="tpu_custom_call" | custom-call | flops 301989888 | bytes 1048576 | tf_op jit(solution)/shard_map/pallas_call | solution.py:196
  23.1 0.0 copy-start.5
  23.1 1.6 %collective-permute-start.8 = (bf16[16,3072]{1,0:T(8,128)(2,1)S(1)}, bf16[16,3072]{1,0:T(8,128)(2,1)S(1)}, u32[]{:S(2)}, u32[]{:S(2)}) collective-permute-start(bf16[16,3072]{1,0:T(8,128)(2,1)S(1)} %get-tuple-element.21), channel_id=1, source_target_pairs={{0,1},{1,0},{2,3},{3,2},{4,5},{5,4},{6,7},{7,6},{8,9},{9,8},{10,11... | collective-permute-start | bytes 294920 | tf_op jit(solution)/shard_map/ppermute | solution.py:18
  24.7 0.5 %collective-permute-start.12 = (bf16[8,3072]{1,0:T(8,128)(2,1)S(1)}, bf16[8,3072]{1,0:T(8,128)(2,1)S(1)}, u32[]{:S(2)}, u32[]{:S(2)}) collective-permute-start(bf16[8,3072]{1,0:T(8,128)(2,1)S(1)} %get-tuple-element.25), channel_id=1, source_target_pairs={{0,1},{1,0},{2,3},{3,2},{4,5},{5,4},{6,7},{7,6},{8,9},{9,8},{10,11... | collective-permute-start | bytes 147464 | tf_op jit(solution)/shard_map/ppermute | solution.py:18
  25.2 1.5 %collective-permute-start.9 = (bf16[8,3072]{1,0:T(8,128)(2,1)S(1)}, bf16[8,3072]{1,0:T(8,128)(2,1)S(1)}, u32[]{:S(2)}, u32[]{:S(2)}) collective-permute-start(bf16[8,3072]{1,0:T(8,128)(2,1)S(1)} %get-tuple-element.23), channel_id=1, source_target_pairs={{0,1},{1,0},{2,3},{3,2},{4,5},{5,4},{6,7},{7,6},{8,9},{9,8},{10,11... | collective-permute-start | bytes 147464 | tf_op jit(solution)/shard_map/ppermute | solution.py:18
  26.7 1.5 %collective-permute-start.1 = (s32[8,128]{1,0:T(8,128)S(1)}, s32[8,128]{1,0:T(8,128)S(1)}, u32[]{:S(2)}, u32[]{:S(2)}) collective-permute-start(s32[8,128]{1,0:T(8,128)S(1)} %shard_map.89), channel_id=1, source_target_pairs={{0,16},{8,24},{16,0},{24,8},{1,17},{9,25},{17,1},{25,9},{2,18},{10... | collective-permute-start | bytes 12296 | tf_op jit(solution)/shard_map/ppermute | solution.py:22
  28.2 2.1 %collective-permute-done.1 = s32[8,128]{1,0:T(8,128)S(1)} collective-permute-done((s32[8,128]{1,0:T(8,128)S(1)}, s32[8,128]{1,0:T(8,128)S(1)}, u32[]{:S(2)}, u32[]{:S(2)}) %collective-permute-start.1) | collective-permute-done | bytes 4128 | tf_op jit(solution)/shard_map/ppermute | solution.py:22
  30.3 0.6 %shard_map.94.mine_ref = f32[32,3072]{1,0:T(8,128)S(1)} custom-call(bf16[32,512]{1,0:T(8,128)(2,1)S(1)} %get-tuple-element.20.hidden_ref, bf16[512,6144]{1,0:T(8,128)(2,1)S(1)} %bitcast.14), custom_call_target="tpu_custom_call" | custom-call | flops 100663296 | bytes 1048576 | tf_op jit(solution)/shard_map/pallas_call | solution.py:196
  31.0 0.5 %collective-permute-done.2.swapped_ref = s32[8,128]{1,0:T(8,128)S(1)} collective-permute-done((s32[8,128]{1,0:T(8,128)S(1)}, s32[8,128]{1,0:T(8,128)S(1)}, u32[]{:S(2)}, u32[]{:S(2)}) %collective-permute-start.2) | collective-permute-done | bytes 4128 | tf_op jit(solution)/shard_map/ppermute | solution.py:22
  31.5 0.0 collective-permute-done.12.refs_0_
  31.5 1.8 %collective-permute-start.13 = (bf16[8,3200]{1,0:T(8,128)(2,1)S(1)}, bf16[8,3200]{1,0:T(8,128)(2,1)S(1)}, u32[]{:S(2)}, u32[]{:S(2)}) collective-permute-start(bf16[8,3200]{1,0:T(8,128)(2,1)S(1)} %shard_map.98), channel_id=1, source_target_pairs={{0,6},{2,4},{4,2},{6,0},{1,7},{3,5},{5,3},{7,1},{8,14},{10,12},{12... | collective-permute-start | bytes 153608 | tf_op jit(solution)/shard_map/ppermute | solution.py:22
  33.3 0.0 collective-permute-done.9.refs_0_
  33.3 0.1 collective-permute-start.10
  33.5 2.7 %collective-permute-start.11 = (bf16[8,3072]{1,0:T(8,128)(2,1)S(1)}, bf16[8,3072]{1,0:T(8,128)(2,1)S(1)}, u32[]{:S(2)}, u32[]{:S(2)}) collective-permute-start(bf16[8,3072]{1,0:T(8,128)(2,1)S(1)} %get-tuple-element.24), channel_id=1, source_target_pairs={{0,2},{2,0},{4,6},{6,4},{1,3},{3,1},{5,7},{7,5},{8,10},{10,8},{12,... | collective-permute-start | bytes 147464 | tf_op jit(solution)/shard_map/ppermute | solution.py:22
  36.1 0.1 shard_map.86.coefficient_ref
  36.2 3.1 %collective-permute-done.10.refs_1_ = bf16[8,3072]{1,0:T(8,128)(2,1)S(1)} collective-permute-done((bf16[8,3072]{1,0:T(8,128)(2,1)S(1)}, bf16[8,3072]{1,0:T(8,128)(2,1)S(1)}, u32[]{:S(2)}, u32[]{:S(2)}) %collective-permute-start.10) | collective-permute-done | bytes 49184 | tf_op jit(solution)/shard_map/ppermute | solution.py:22
  39.4 0.7 %finish.1 = (bf16[8,3072]{1,0:T(8,128)(2,1)}, s32[4,4]{1,0:T(4,128)}) custom-call(f32[32,128]{1,0:T(8,128)S(1)} %shard_map.86.coefficient_ref, s32[8,128]{1,0:T(8,128)S(1)} %add.3.counts_ref.sum_ref, s32[8,128]{1,0:T(8,128)S(1)} %collective-permute-done.2.swapped_ref, f32[8,3072]{1,0:T(8,128)S(1)} %shard_map.97.begun_ref, ...), custom_call_target="tpu_custom_call" | custom-call | tf_op jit(solution)/shard_map/finish/pallas_call | solution.py:298
  (25 shorter events, 0.1 us)
Async XLA Ops:
  0.6 0.8 %copy-start.3 = (bf16[8,3072]{1,0:T(8,128)(2,1)S(1)}, bf16[8,3072]{1,0:T(8,128)(2,1)}, u32[]{:S(2)}) copy-start(bf16[8,3072]{1,0:T(8,128)(2,1)} %tokens_ref.1) | copy-start | bytes 147460
  0.6 0.8 %copy-start.6 = (s32[8,2]{0,1:T(2,128)S(1)}, s32[8,2]{0,1:T(2,128)}, u32[]{:S(2)}) copy-start(s32[8,2]{0,1:T(2,128)} %param.9) | copy-start | bytes 196
  0.7 0.8 %copy-start.4 = (s32[8,2]{0,1:T(2,128)S(1)}, s32[8,2]{0,1:T(2,128)}, u32[]{:S(2)}) copy-start(s32[8,2]{0,1:T(2,128)} %param.8) | copy-start | bytes 196
  0.7 17.5 %copy-start.2 = (bf16[1,512,6144]{2,1,0:T(8,128)(2,1)S(1)}, bf16[1,512,6144]{2,1,0:T(8,128)(2,1)}, u32[]{:S(2)}) copy-start(bf16[1,512,6144]{2,1,0:T(8,128)(2,1)} %param.13) | copy-start | bytes 18874372
  0.7 17.5 %copy-start.1 = (bf16[1,6144,512]{2,1,0:T(8,128)(2,1)S(1)}, bf16[1,6144,512]{2,1,0:T(8,128)(2,1)}, u32[]{:S(2)}) copy-start(bf16[1,6144,512]{2,1,0:T(8,128)(2,1)} %param.12) | copy-start | bytes 18874372
  0.7 17.5 %copy-start = (bf16[1,6144,512]{2,1,0:T(8,128)(2,1)S(1)}, bf16[1,6144,512]{2,1,0:T(8,128)(2,1)}, u32[]{:S(2)}) copy-start(bf16[1,6144,512]{2,1,0:T(8,128)(2,1)} %param.11) | copy-start | bytes 18874372
  1.6 8.6 %collective-permute-start = (bf16[8,3200]{1,0:T(8,128)(2,1)S(1)}, bf16[8,3200]{1,0:T(8,128)(2,1)S(1)}, u32[]{:S(2)}, u32[]{:S(2)}) collective-permute-start(bf16[8,3200]{1,0:T(8,128)(2,1)S(1)} %shard_map.88.refs_0_), channel_id=1, source_target_pairs={{0,2},{2,0},{4,6},{6,4},{1,3},{3,1},{5,7},{7,5},{8,10},{10,8},{12,... | collective-permute-start | bytes 153608 | tf_op jit(solution)/shard_map/ppermute | solution.py:22
  4.7 5.5 %collective-permute-start.3 = (bf16[8,3072]{1,0:T(8,128)(2,1)S(1)}, bf16[8,3072]{1,0:T(8,128)(2,1)S(1)}, u32[]{:S(2)}, u32[]{:S(2)}) collective-permute-start(bf16[8,3072]{1,0:T(8,128)(2,1)S(1)} %copy-done.3), channel_id=1, source_target_pairs={{0,4},{2,6},{4,0},{6,2},{1,5},{3,7},{5,1},{7,3},{8,12},{10,14},{12... | collective-permute-start | bytes 147464 | tf_op jit(solution)/shard_map/ppermute | solution.py:22
  10.2 11.0 %collective-permute-start.6 = (bf16[24,1536]{1,0:T(8,128)(2,1)S(1)}, bf16[24,1536]{1,0:T(8,128)(2,1)S(1)}, u32[]{:S(2)}, u32[]{:S(2)}) collective-permute-start(bf16[24,1536]{1,0:T(8,128)(2,1)S(1)} %get-tuple-element.15.refs_0_), channel_id=1, source_target_pairs={{0,1},{1,0},{2,3},{3,2},{4,5},{5,4},{6,7},{7,6},{8,9},{9,8},{10,11... | collective-permute-start | bytes 221192 | tf_op jit(solution)/shard_map/ppermute | solution.py:18
  11.8 6.4 %collective-permute-start.7 = (bf16[8,3072]{1,0:T(8,128)(2,1)S(1)}, bf16[8,3072]{1,0:T(8,128)(2,1)S(1)}, u32[]{:S(2)}, u32[]{:S(2)}) collective-permute-start(bf16[8,3072]{1,0:T(8,128)(2,1)S(1)} %copy-done.3), channel_id=1, source_target_pairs={{0,6},{2,4},{4,2},{6,0},{1,7},{3,5},{5,3},{7,1},{8,14},{10,12},{12... | collective-permute-start | bytes 147464 | tf_op jit(solution)/shard_map/ppermute | solution.py:22
  13.9 8.0 %collective-permute-start.4 = (bf16[24,1536]{1,0:T(8,128)(2,1)S(1)}, bf16[24,1536]{1,0:T(8,128)(2,1)S(1)}, u32[]{:S(2)}, u32[]{:S(2)}) collective-permute-start(bf16[24,1536]{1,0:T(8,128)(2,1)S(1)} %get-tuple-element.14.refs_1_), channel_id=1, source_target_pairs={{0,1},{1,0},{2,3},{3,2},{4,5},{5,4},{6,7},{7,6},{8,9},{9,8},{10,11... | collective-permute-start | bytes 221192 | tf_op jit(solution)/shard_map/ppermute | solution.py:18
  14.4 6.8 %collective-permute-start.5 = (bf16[8,3072]{1,0:T(8,128)(2,1)S(1)}, bf16[8,3072]{1,0:T(8,128)(2,1)S(1)}, u32[]{:S(2)}, u32[]{:S(2)}) collective-permute-start(bf16[8,3072]{1,0:T(8,128)(2,1)S(1)} %copy-done.3), channel_id=1, source_target_pairs={{0,7},{1,6},{2,5},{3,4},{4,3},{5,2},{6,1},{7,0},{8,15},{9,14},{10,... | collective-permute-start | bytes 147464 | tf_op jit(solution)/shard_map/ppermute | solution.py:31
  23.1 13.0 %copy-start.5 = (f32[8,2]{0,1:T(2,128)S(1)}, f32[8,2]{0,1:T(2,128)}, u32[]{:S(2)}) copy-start(f32[8,2]{0,1:T(2,128)} %param.10) | copy-start | bytes 196
  23.1 10.3 %collective-permute-start.8 = (bf16[16,3072]{1,0:T(8,128)(2,1)S(1)}, bf16[16,3072]{1,0:T(8,128)(2,1)S(1)}, u32[]{:S(2)}, u32[]{:S(2)}) collective-permute-start(bf16[16,3072]{1,0:T(8,128)(2,1)S(1)} %get-tuple-element.21), channel_id=1, source_target_pairs={{0,1},{1,0},{2,3},{3,2},{4,5},{5,4},{6,7},{7,6},{8,9},{9,8},{10,11... | collective-permute-start | bytes 294920 | tf_op jit(solution)/shard_map/ppermute | solution.py:18
  24.7 6.8 %collective-permute-start.12 = (bf16[8,3072]{1,0:T(8,128)(2,1)S(1)}, bf16[8,3072]{1,0:T(8,128)(2,1)S(1)}, u32[]{:S(2)}, u32[]{:S(2)}) collective-permute-start(bf16[8,3072]{1,0:T(8,128)(2,1)S(1)} %get-tuple-element.25), channel_id=1, source_target_pairs={{0,1},{1,0},{2,3},{3,2},{4,5},{5,4},{6,7},{7,6},{8,9},{9,8},{10,11... | collective-permute-start | bytes 147464 | tf_op jit(solution)/shard_map/ppermute | solution.py:18
  25.2 8.1 %collective-permute-start.9 = (bf16[8,3072]{1,0:T(8,128)(2,1)S(1)}, bf16[8,3072]{1,0:T(8,128)(2,1)S(1)}, u32[]{:S(2)}, u32[]{:S(2)}) collective-permute-start(bf16[8,3072]{1,0:T(8,128)(2,1)S(1)} %get-tuple-element.23), channel_id=1, source_target_pairs={{0,1},{1,0},{2,3},{3,2},{4,5},{5,4},{6,7},{7,6},{8,9},{9,8},{10,11... | collective-permute-start | bytes 147464 | tf_op jit(solution)/shard_map/ppermute | solution.py:18
  26.7 3.6 %collective-permute-start.1 = (s32[8,128]{1,0:T(8,128)S(1)}, s32[8,128]{1,0:T(8,128)S(1)}, u32[]{:S(2)}, u32[]{:S(2)}) collective-permute-start(s32[8,128]{1,0:T(8,128)S(1)} %shard_map.89), channel_id=1, source_target_pairs={{0,16},{8,24},{16,0},{24,8},{1,17},{9,25},{17,1},{25,9},{2,18},{10... | collective-permute-start | bytes 12296 | tf_op jit(solution)/shard_map/ppermute | solution.py:22
  30.3 1.2 %collective-permute-start.2 = (s32[8,128]{1,0:T(8,128)S(1)}, s32[8,128]{1,0:T(8,128)S(1)}, u32[]{:S(2)}, u32[]{:S(2)}) collective-permute-start(s32[8,128]{1,0:T(8,128)S(1)} %add.3.counts_ref.sum_ref), channel_id=1, source_target_pairs={{0,8},{8,0},{16,24},{24,16},{1,9},{9,1},{17,25},{25,17},{2,10},{10... | collective-permute-start | bytes 12296 | tf_op jit(solution)/shard_map/ppermute | solution.py:22
  31.5 7.9 %collective-permute-start.13 = (bf16[8,3200]{1,0:T(8,128)(2,1)S(1)}, bf16[8,3200]{1,0:T(8,128)(2,1)S(1)}, u32[]{:S(2)}, u32[]{:S(2)}) collective-permute-start(bf16[8,3200]{1,0:T(8,128)(2,1)S(1)} %shard_map.98), channel_id=1, source_target_pairs={{0,6},{2,4},{4,2},{6,0},{1,7},{3,5},{5,3},{7,1},{8,14},{10,12},{12... | collective-permute-start | bytes 153608 | tf_op jit(solution)/shard_map/ppermute | solution.py:22
  33.3 6.0 %collective-permute-start.10 = (bf16[8,3072]{1,0:T(8,128)(2,1)S(1)}, bf16[8,3072]{1,0:T(8,128)(2,1)S(1)}, u32[]{:S(2)}, u32[]{:S(2)}) collective-permute-start(bf16[8,3072]{1,0:T(8,128)(2,1)S(1)} %shard_map.96), channel_id=1, source_target_pairs={{0,4},{2,6},{4,0},{6,2},{1,5},{3,7},{5,1},{7,3},{8,12},{10,14},{12... | collective-permute-start | bytes 147464 | tf_op jit(solution)/shard_map/ppermute | solution.py:22
  33.5 5.9 %collective-permute-start.11 = (bf16[8,3072]{1,0:T(8,128)(2,1)S(1)}, bf16[8,3072]{1,0:T(8,128)(2,1)S(1)}, u32[]{:S(2)}, u32[]{:S(2)}) collective-permute-start(bf16[8,3072]{1,0:T(8,128)(2,1)S(1)} %get-tuple-element.24), channel_id=1, source_target_pairs={{0,2},{2,0},{4,6},{6,4},{1,3},{3,1},{5,7},{7,5},{8,10},{10,8},{12,... | collective-permute-start | bytes 147464 | tf_op jit(solution)/shard_map/ppermute | solution.py:22
